TPU v7x, 8 devices: a whole 2x2x1 slice. The times are simulated.
8 devices in a mesh: model: 1 (over z), replica: 2 (over y), fsdp: 4 (over x, core).
Axes of the slice: x: 2, y: 2, z: 1, core: 2. Of those that a mesh axis runs over, the one named last changes fastest.
Arguments:
- x_in: bfloat16 [3, 8192, 2048], P(None, ('model', 'replica', 'fsdp'))
- dy_out: bfloat16 [3, 8192, 2048], P(None, ('model', 'replica', 'fsdp'))
- lengths: int32 [3, 8], P(None, ('model', 'replica', 'fsdp'))
- w_up: bfloat16 [1, 2048, 8192], P(None, ('model', 'fsdp'))
- w_down: bfloat16 [1, 8192, 2048], P(None, ('model', 'fsdp'))
Outputs:
- output 1: float32 [1, 2048, 8192], P(None, ('model', 'fsdp'))
- output 2: float32 [1, 8192, 2048], P(None, ('model', 'fsdp'))
All inputs are finite; a program needn't handle non-finite values.
Results may differ from a plain program's by a relative error of at most 0.001.
Values are sent between devices in bfloat16 or wider.
A program may use at most 1 GiB of HBM per device.

v0:
```python
import jax
import jax.numpy as jnp
from jax import lax
from jax.experimental import pallas as pl
from jax.experimental.pallas import tpu as pltpu
from jax.sharding import PartitionSpec as P


D = 2048
TOK = 1024
MICRO = 3
BASE = 256
REST = TOK - BASE
TM = 128
NT = MICRO * REST // TM
RROWS = MICRO * REST + TM
FIRST = 3
PIECES = (4, 4, 4, 2, 1)
SIZES = (5, 7, 8, 9, 10, 11, 12, 15)
G = 4
M = G * TM
FB = 256
HB = FB // 2
NCH = D // FB
HALF = 1024
WSETS = ((0, 2), (2, 2), (4, 4))
ORDER = (3, 4, 0, 5, 6, 1, 7, 2)
LAG = 3
OWN_ONLY = 3
C1 = 0.7978845608028654
C3 = 0.044715
BF = jnp.bfloat16
F32 = jnp.float32


ANY = pl.BlockSpec(memory_space=pltpu.HBM)
SM = pl.BlockSpec(memory_space=pltpu.SMEM)
VM = pl.BlockSpec(memory_space=pltpu.VMEM)
MIB = 1024 * 1024
GRANT = 60 * 1024 * 1024

CORE = [(0, 1), (1, 0), (2, 3), (3, 2)]
XSWAP = [(0, 2), (2, 0), (1, 3), (3, 1)]
XDIAG = [(0, 3), (3, 0), (1, 2), (2, 1)]
YSWAP = [(0, 1), (1, 0)]
YDIAG = [(r * 4 + f, (1 - r) * 4 + (f ^ 1)) for r in range(2) for f in range(4)]


def core_swap(v):
    return lax.ppermute(v, "fsdp", CORE)


def x_swap(v):
    return lax.ppermute(v, "fsdp", XSWAP)


def x_diag(v):
    return lax.ppermute(v, "fsdp", XDIAG)


def y_swap(v):
    return lax.ppermute(v, "replica", YSWAP)


def y_diag(v):
    return lax.ppermute(v, ("replica", "fsdp"), YDIAG)


def cost(flops, nbytes):
    return pl.CostEstimate(flops=flops, bytes_accessed=nbytes, transcendentals=0)


def start(lens, x_in, dy):
    def kern(len_ref, x_ref, d_ref, all_ref, s1_ref, land, buf, send, recv, isem, osem):
        r, f = lax.axis_index("replica"), lax.axis_index("fsdp")
        me = r * 4 + f
        loads = []
        for a, ref in enumerate((x_ref, d_ref)):
            cp = pltpu.make_async_copy(ref.at[:, pl.ds(0, BASE), :], buf.at[a], isem.at[a])
            cp.start()
            loads.append(cp)
        barrier = pltpu.get_barrier_semaphore()
        peers = []
        for k in range(1, 8):
            p = lax.rem(me + k, 8)
            peers.append((0, p // 4, lax.rem(p, 4)))
        for p in peers:
            pl.semaphore_signal(barrier, inc=1, device_id=p, device_id_type=pl.DeviceIdType.MESH)
        pl.semaphore_wait(barrier, 7)
        cps = []
        for k, p in enumerate(peers):
            cp = pltpu.make_async_remote_copy(
                src_ref=len_ref,
                dst_ref=land.at[k],
                send_sem=send.at[k],
                recv_sem=recv.at[k],
                device_id=p,
                device_id_type=pl.DeviceIdType.MESH,
            )
            cp.start()
            cps.append(cp)
        outs = []
        for a in range(2):
            loads[a].wait()
            cp = pltpu.make_async_copy(buf.at[a], s1_ref.at[a], osem.at[a])
            cp.start()
            outs.append(cp)
        for cp in cps:
            cp.wait()
        all_ref[0] = len_ref[...]
        for k in range(7):
            all_ref[k + 1] = land[k]
        for cp in outs:
            cp.wait()

    return pl.pallas_call(
        kern,
        in_specs=[VM, ANY, ANY],
        out_specs=[VM, ANY],
        out_shape=[jax.ShapeDtypeStruct((8, 8, 128), jnp.int32), jax.ShapeDtypeStruct((2, MICRO, BASE, D), BF)],
        scratch_shapes=[
            pltpu.VMEM((7, 8, 128), jnp.int32),
            pltpu.VMEM((2, MICRO, BASE, D), BF),
            pltpu.SemaphoreType.DMA((7,)),
            pltpu.SemaphoreType.DMA((7,)),
            pltpu.SemaphoreType.DMA((2,)),
            pltpu.SemaphoreType.DMA((2,)),
        ],
        compiler_params=pltpu.CompilerParams(collective_id=0, has_side_effects=True, vmem_limit_bytes=GRANT),
        cost_estimate=cost(10_000_000_000, 13_000_000),
        name="start",
    )(lens, x_in, dy)


def pack_rest(x_in, dy, rest, offs):
    def kern(rest_ref, offs_ref, x_ref, d_ref, out_ref, buf, zero, isem, osem, zsem):
        loads = []
        for k in range(MICRO):
            for a, ref in enumerate((x_ref, d_ref)):
                cp = pltpu.make_async_copy(ref.at[k, pl.ds(BASE, REST), :], buf.at[k, a], isem.at[k, a])
                cp.start()
                loads.append(cp)
        zero[...] = jnp.zeros_like(zero)
        for k in range(MICRO):
            n = rest_ref[k]
            for a in range(2):
                loads[2 * k + a].wait()
                for r in range(0, REST, TM):
                    row = lax.broadcasted_iota(jnp.int32, (TM, D), 0) + r
                    blk = buf[k, a, r : r + TM, :]
                    buf[k, a, r : r + TM, :] = jnp.where(row < n, blk, jnp.zeros_like(blk))
            o = pl.multiple_of(offs_ref[k], 16)
            cps = [
                pltpu.make_async_copy(buf.at[k, a], out_ref.at[a, pl.ds(o, REST), :], osem.at[a]) for a in range(2)
            ]
            for cp in cps:
                cp.start()
            for cp in cps:
                cp.wait()
        for o in (pl.multiple_of(offs_ref[MICRO], 16), MICRO * REST):
            cps = [pltpu.make_async_copy(zero, out_ref.at[a, pl.ds(o, TM), :], zsem.at[a]) for a in range(2)]
            for cp in cps:
                cp.start()
            for cp in cps:
                cp.wait()

    return pl.pallas_call(
        kern,
        in_specs=[SM, SM, ANY, ANY],
        out_specs=ANY,
        out_shape=jax.ShapeDtypeStruct((2, RROWS, D), BF),
        scratch_shapes=[
            pltpu.VMEM((MICRO, 2, REST, D), BF),
            pltpu.VMEM((TM, D), BF),
            pltpu.SemaphoreType.DMA((MICRO, 2)),
            pltpu.SemaphoreType.DMA((2,)),
            pltpu.SemaphoreType.DMA((2,)),
        ],
        compiler_params=pltpu.CompilerParams(vmem_limit_bytes=GRANT),
        cost_estimate=cost(15_000_000_000, 50_000_000),
        name="pack_rest",
    )(rest, offs, x_in, dy)


def build_send(own, sib, info):
    np_ = 1 + len(PIECES)

    def kern(info_ref, own_ref, sib_ref, *refs):
        outs, (buf, isem, osem) = refs[:np_], refs[np_:]
        n, mine, shift = info_ref[0], info_ref[1], info_ref[2]
        starts = [0] + [info_ref[3 + k] for k in range(len(PIECES))]

        def load(i, slot):
            @pl.when(i < mine)
            def _():
                r = pl.multiple_of(i * TM, TM)
                pltpu.make_async_copy(own_ref.at[:, pl.ds(r, TM), :], buf.at[slot], isem.at[slot]).start()

            @pl.when(i >= mine)
            def _():
                r = pl.multiple_of((i + shift) * TM, TM)
                pltpu.make_async_copy(sib_ref.at[:, pl.ds(r, TM), :], buf.at[slot], isem.at[slot]).start()

        def store(i, slot):
            for k in range(np_):
                here = i >= starts[k]
                if k + 1 < np_:
                    here = jnp.logical_and(here, i < starts[k + 1])

                @pl.when(here)
                def _():
                    r = pl.multiple_of((i - starts[k]) * TM, TM)
                    pltpu.make_async_copy(buf.at[slot], outs[k].at[:, pl.ds(r, TM), :], osem.at[slot]).start()

        def stored(slot):
            pltpu.make_async_copy(buf.at[slot], outs[0].at[:, pl.ds(0, TM), :], osem.at[slot]).wait()

        for s in range(3):

            @pl.when(s < n)
            def _():
                load(s, s)

        def body(i, _):
            slot = lax.rem(i, 4)
            pltpu.make_async_copy(own_ref.at[:, pl.ds(0, TM), :], buf.at[slot], isem.at[slot]).wait()
            store(i, slot)

            @pl.when(i >= 1)
            def _():
                stored(lax.rem(i + 3, 4))

            @pl.when(i + 3 < n)
            def _():
                load(i + 3, lax.rem(i + 3, 4))

            return 0

        lax.fori_loop(0, n, body, 0)

        @pl.when(n > 0)
        def _():
            stored(lax.rem(n + 3, 4))

    return pl.pallas_call(
        kern,
        in_specs=[SM, ANY, ANY],
        out_specs=[ANY] * np_,
        out_shape=[jax.ShapeDtypeStruct((2, k * TM, D), BF) for k in (FIRST, *PIECES)],
        scratch_shapes=[pltpu.VMEM((4, 2, TM, D), BF), pltpu.SemaphoreType.DMA((4,)), pltpu.SemaphoreType.DMA((4,))],
        compiler_params=pltpu.CompilerParams(vmem_limit_bytes=GRANT),
        cost_estimate=cost(10_000_000_000, 36_000_000),
        name="build_send",
    )(info, own, sib)


def gelu_and_slope(u):
    u2 = u * u
    t = jnp.tanh(u * (C1 + (C1 * C3) * u2))
    half = 0.5 + 0.5 * t
    act = u * half
    slope = half + (0.5 * u) * (1.0 - t * t) * (C1 + (3 * C1 * C3) * u2)
    return act, slope


def pick(e, lo, hi, fn):
    if hi - lo == 1:
        fn(lo)
        return
    mid = (lo + hi) // 2

    @pl.when(e < mid * 32)
    def _():
        pick(e, lo, mid, fn)

    @pl.when(e >= mid * 32)
    def _():
        pick(e, mid, hi, fn)


def issue_group(tab_ref, g, slot, src, xb, db, sem):
    for s in range(G):
        e = tab_ref[g * G + s]
        r = pl.multiple_of(lax.rem(e, 32) * TM, TM)

        def fetch(k):
            rows = pl.ds(s * TM, TM)
            pltpu.make_async_copy(src[k].at[0, pl.ds(r, TM), :], xb.at[slot, rows, :], sem.at[slot, 0]).start()
            pltpu.make_async_copy(src[k].at[1, pl.ds(r, TM), :], db.at[slot, rows, :], sem.at[slot, 1]).start()

        pick(e, 0, len(src), fetch)


def wait_group(slot, xb, db, sem):
    pltpu.make_async_copy(xb.at[slot], xb.at[slot], sem.at[slot, 0]).wait()
    pltpu.make_async_copy(db.at[slot], db.at[slot], sem.at[slot, 1]).wait()


def add_group(x, dy, wu, wd, gd, gu):
    u = lax.dot_general(wu[...], x, (((0,), (1,)), ((), ())), preferred_element_type=F32).astype(BF).astype(F32)
    da = lax.dot_general(wd[...], dy, (((1,), (1,)), ((), ())), preferred_element_type=F32)
    act, slope = gelu_and_slope(u)
    dh = (da * slope).astype(BF)
    gd[...] += jnp.dot(act.astype(BF), dy, preferred_element_type=F32)
    gu[...] += jnp.dot(dh, x, preferred_element_type=F32)


def weight_copies(c, lo, f, w, wub, wdb, sem):
    own, sib, fx, fd, wd_own, wd_oth = w
    cps = []
    c0, co = c * HB, (c - lo) * HB
    if not isinstance(c, int):
        c0, co = pl.multiple_of(c0, HB), pl.multiple_of(co, HB)
    for a in range(2):
        for k, (ref, col) in enumerate(((own, c0), (sib, c0), (fx, co), (fd, co))):
            rows = pl.ds(pl.multiple_of((f ^ k) * 512, 512), 512)
            cps.append(
                pltpu.make_async_copy(ref.at[a, :, pl.ds(col, HB)], wub.at[rows, pl.ds(a * HB, HB)], sem.at[k, a])
            )
    cps.append(pltpu.make_async_copy(wd_own.at[pl.ds(c0, HB), :], wdb.at[pl.ds(0, HB), :], sem.at[4, 0]))
    cps.append(pltpu.make_async_copy(wd_oth.at[pl.ds(co, HB), :], wdb.at[pl.ds(HB, HB), :], sem.at[4, 1]))
    return cps


def gather_scratch(n_acc):
    return [
        pltpu.VMEM((2, M, D), BF),
        pltpu.VMEM((2, M, D), BF),
        pltpu.VMEM((n_acc, D, FB), BF),
        pltpu.VMEM((n_acc, FB, D), BF),
        pltpu.VMEM((n_acc, FB, D), F32),
        pltpu.VMEM((n_acc, FB, D), F32),
        pltpu.SemaphoreType.DMA((2, 2)),
        pltpu.SemaphoreType.DMA((n_acc, 5, 2)),
    ]


def early_grads(tab, info, srcs, w, w_lo, lo_chunk, n_chunks, deps=()):
    ns = len(srcs)

    def kern(tab_ref, info_ref, *refs):
        src, wrefs, refs = refs[:ns], refs[ns : ns + 6], refs[ns + 6 + len(deps) :]
        out_d, out_u, xb, db, wub, wdb, gd, gu, sem, wsem, asem = refs
        groups, f = info_ref[0], info_ref[1]

        def weights(q, slot):
            return weight_copies(lo_chunk + q, w_lo, f, wrefs, wub.at[slot], wdb.at[slot], wsem.at[slot])

        def results(q, slot):
            return (
                pltpu.make_async_copy(gd.at[slot], out_d.at[q], asem.at[slot, 0]),
                pltpu.make_async_copy(gu.at[slot], out_u.at[q], asem.at[slot, 1]),
            )

        issue_group(tab_ref, 0, 0, src, xb, db, sem)
        for cp in weights(0, 0):
            cp.start()

        def chunk(q, t):
            ws = lax.rem(q, 2)

            @pl.when(q + 1 < n_chunks)
            def _():
                for cp in weights(q + 1, 1 - ws):
                    cp.start()

            @pl.when(q >= 2)
            def _():
                for cp in results(q - 2, ws):
                    cp.wait()

            gd[ws] = jnp.zeros((FB, D), F32)
            gu[ws] = jnp.zeros((FB, D), F32)
            for cp in weights(q, ws):
                cp.wait()

            def group(g, t):
                slot = lax.rem(t, 2)
                last = g + 1 == groups

                @pl.when(jnp.logical_or(jnp.logical_not(last), q + 1 < n_chunks))
                def _():
                    issue_group(tab_ref, jnp.where(last, 0, g + 1), 1 - slot, src, xb, db, sem)

                wait_group(slot, xb, db, sem)
                add_group(xb[slot], db[slot], wub.at[ws], wdb.at[ws], gd.at[ws], gu.at[ws])
                return t + 1

            t = lax.fori_loop(0, groups, group, t)
            for cp in results(q, ws):
                cp.start()
            return t

        lax.fori_loop(0, n_chunks, chunk, 0)
        for q in range(max(n_chunks - 2, 0), n_chunks):
            for cp in results(q, q % 2):
                cp.wait()

    return pl.pallas_call(
        kern,
        in_specs=[SM, SM] + [ANY] * (ns + 6) + [SM] * len(deps),
        out_specs=[ANY] * 2,
        out_shape=[jax.ShapeDtypeStruct((n_chunks, FB, D), F32)] * 2,
        scratch_shapes=gather_scratch(2) + [pltpu.SemaphoreType.DMA((2, 2))],
        compiler_params=pltpu.CompilerParams(vmem_limit_bytes=GRANT),
        cost_estimate=cost(8 * 5632 * D * FB * n_chunks, 60_000_000 * n_chunks),
    )(tab, info, *srcs, *w, *deps)


def chunk_grads(j, w_lo, tab, info, skip, srcs, w, prior, at, deps):
    ns = len(srcs)

    def kern(tab_ref, info_ref, *refs):
        src, refs = refs[:ns], refs[ns:]
        wrefs, (pd, pu), refs = refs[:6], refs[6:8], refs[8 + len(deps) :]
        keep_d, send_d, keep_u, send_u, xb, db, wub, wdb, gd, gu, sem, wsem, osem = refs
        groups, xi, f = info_ref[0], info_ref[1], info_ref[2]
        wub, wdb, gd, gu = wub.at[0], wdb.at[0], gd.at[0], gu.at[0]

        @pl.when(groups > skip)
        def _():
            issue_group(tab_ref, skip, 0, src, xb, db, sem)

        cps = weight_copies(j, w_lo, f, wrefs, wub, wdb, wsem.at[0])
        cps.append(pltpu.make_async_copy(pd.at[at], gd, osem.at[0]))
        cps.append(pltpu.make_async_copy(pu.at[at], gu, osem.at[1]))
        for cp in cps:
            cp.start()
        for cp in cps:
            cp.wait()

        def body(g, _):
            slot = lax.rem(g - skip, 2)

            @pl.when(g + 1 < groups)
            def _():
                issue_group(tab_ref, g + 1, 1 - slot, src, xb, db, sem)

            wait_group(slot, xb, db, sem)
            add_group(xb[slot], db[slot], wub, wdb, gd, gu)
            return 0

        lax.fori_loop(skip, groups, body, 0)
        kc = pl.multiple_of(xi * HALF, HALF)
        sc = pl.multiple_of((1 - xi) * HALF, HALF)
        ocp = [(gd.at[pl.ds(HB, HB), :], send_d), (gd.at[pl.ds(0, HB), :], keep_d)]
        for a in range(2):
            rows, cols = pl.ds(a * HB, HB), pl.ds(a * HALF, HALF)
            ocp.append((gu.at[rows, pl.ds(sc, HALF)], send_u.at[:, cols]))
            ocp.append((gu.at[rows, pl.ds(kc, HALF)], keep_u.at[:, cols]))
        ocp = [pltpu.make_async_copy(a, b, osem.at[i]) for i, (a, b) in enumerate(ocp)]
        for cp in ocp:
            cp.start()
        for cp in ocp:
            cp.wait()

    return pl.pallas_call(
        kern,
        in_specs=[SM, SM] + [ANY] * (ns + 8 + len(deps)),
        out_specs=[ANY] * 4,
        out_shape=[jax.ShapeDtypeStruct((HB, D), F32)] * 4,
        scratch_shapes=gather_scratch(1) + [pltpu.SemaphoreType.DMA((6,))],
        compiler_params=pltpu.CompilerParams(vmem_limit_bytes=GRANT),
        cost_estimate=cost(8 * 3072 * D * FB, 40_000_000),
    )(tab, info, *srcs, *w, *prior, *deps)


def finish_down(j, pos, keep, recv, out):
    first = out is None

    def kern(pos_ref, kd, rc, *refs):
        out_d, fd, vd, sem = refs if first else refs[1:]
        y = pos_ref[0]
        vd[...] = kd[...] + rc[...]
        row = pl.multiple_of(y * HALF + j * HB, HB)
        cps = [
            pltpu.make_async_copy(vd, fd, sem.at[0]),
            pltpu.make_async_copy(vd, out_d.at[pl.ds(row, HB), :], sem.at[1]),
        ]
        for cp in cps:
            cp.start()
        for cp in cps:
            cp.wait()

    extra = [] if first else [out]
    return pl.pallas_call(
        kern,
        in_specs=[SM, VM, VM] + [ANY] * len(extra),
        out_specs=[ANY] * 2,
        out_shape=[jax.ShapeDtypeStruct((D, D), F32), jax.ShapeDtypeStruct((HB, D), F32)],
        scratch_shapes=[pltpu.VMEM((HB, D), F32), pltpu.SemaphoreType.DMA((2,))],
        input_output_aliases={} if first else {3: 0},
        compiler_params=pltpu.CompilerParams(vmem_limit_bytes=16 * MIB),
        cost_estimate=cost(2_000_000_000, 4_000_000),
    )(pos, keep, recv, *extra)


def finish_up(j, pos, keep, recv, out):
    first = out is None

    def kern(pos_ref, ku, rc, *refs):
        out_u, fuc, fus, vu, sem = refs if first else refs[1:]
        y, xi, c = pos_ref[0], pos_ref[1], pos_ref[2]
        mine = pl.ds(pl.multiple_of(c * 512, 512), 512)
        other = pl.ds(pl.multiple_of((1 - c) * 512, 512), 512)
        vu[0] = (ku[:, 0:HALF] + rc[:, HALF:D]).T
        vu[1] = (ku[:, HALF:D] + rc[:, 0:HALF]).T
        cps = [
            pltpu.make_async_copy(vu.at[:, other, :], fus, sem.at[0]),
            pltpu.make_async_copy(vu.at[:, mine, :], fuc, sem.at[1]),
        ]
        for a in range(2):
            xa = xi if a == 0 else 1 - xi
            col = pl.multiple_of(((2 * xa + c) * 2 + y) * HALF + j * HB, HB)
            cps.append(pltpu.make_async_copy(vu.at[a, mine, :], out_u.at[:, pl.ds(col, HB)], sem.at[2 + a]))
        for cp in cps:
            cp.start()
        for cp in cps:
            cp.wait()

    extra = [] if first else [out]
    return pl.pallas_call(
        kern,
        in_specs=[SM, VM, VM] + [ANY] * len(extra),
        out_specs=[ANY] * 3,
        out_shape=[
            jax.ShapeDtypeStruct((512, 4 * D), F32),
            jax.ShapeDtypeStruct((2, 512, HB), F32),
            jax.ShapeDtypeStruct((2, 512, HB), F32),
        ],
        scratch_shapes=[pltpu.VMEM((2, HALF, HB), F32), pltpu.SemaphoreType.DMA((4,))],
        input_output_aliases={} if first else {3: 0},
        compiler_params=pltpu.CompilerParams(vmem_limit_bytes=16 * MIB),
        cost_estimate=cost(2_000_000_000, 4_000_000),
    )(pos, keep, recv, *extra)


def store(j, pos, rd, ruc, ruy, rus, outs):
    def kern(pos_ref, d_ref, uc_ref, uy_ref, us_ref, _d, _u, out_d, out_u, vd, vu, isem, osem):
        y, xi, c = pos_ref[0], pos_ref[1], pos_ref[2]
        row = pl.multiple_of((1 - y) * HALF + j * HB, HB)
        work = [(d_ref, vd, [(vd, out_d.at[pl.ds(row, HB), :])])]
        for k, (ref, cc, yy) in enumerate(((uc_ref, c, 1 - y), (uy_ref, 1 - c, 1 - y), (us_ref, 1 - c, y))):
            puts = []
            for a in range(2):
                xa = xi if a == 0 else 1 - xi
                col = pl.multiple_of(((2 * xa + cc) * 2 + yy) * HALF + j * HB, HB)
                puts.append((vu.at[k, a], out_u.at[:, pl.ds(col, HB)]))
            work.append((ref, vu.at[k], puts))
        loads = [pltpu.make_async_copy(src, mid, isem.at[n]) for n, (src, mid, _) in enumerate(work)]
        for cp in loads:
            cp.start()
        done = []
        for cp, (_, _, puts) in zip(loads, work):
            cp.wait()
            for src, dst in puts:
                put = pltpu.make_async_copy(src, dst, osem.at[len(done)])
                put.start()
                done.append(put)
        for put in done:
            put.wait()

    return pl.pallas_call(
        kern,
        in_specs=[SM] + [ANY] * 6,
        out_specs=[ANY] * 2,
        out_shape=[jax.ShapeDtypeStruct((D, D), F32), jax.ShapeDtypeStruct((512, 4 * D), F32)],
        scratch_shapes=[
            pltpu.VMEM((HB, D), F32),
            pltpu.VMEM((3, 2, 512, HB), F32),
            pltpu.SemaphoreType.DMA((4,)),
            pltpu.SemaphoreType.DMA((7,)),
        ],
        input_output_aliases={5: 0, 6: 1},
        compiler_params=pltpu.CompilerParams(vmem_limit_bytes=16 * MIB),
        cost_estimate=cost(3_000_000_000, 5_000_000),
    )(pos, rd, ruc, ruy, rus, *outs)


def nothing(k):
    return pl.pallas_call(lambda o: None, out_specs=ANY, out_shape=jax.ShapeDtypeStruct((2, k * TM, D), BF))()


def present(n):
    return (n >= 4, n >= 8, n >= 12, n % 4 >= 2, n % 2 == 1)


def exchange_branch(n, early):
    def run(pieces, *rest):
        got = []
        for k, here in enumerate(present(n)):
            got.append(y_swap(pieces[k]) if here else nothing(PIECES[k]))
        acc = early(*rest)
        sib = []
        for k, here in enumerate(present(n)):
            sib.append(core_swap(got[k]) if here else nothing(PIECES[k]))
        return (*got, *sib, *acc)

    return run


def solution(mesh):
    tok_spec = P(None, ("model", "replica", "fsdp"), None)
    len_spec = P(None, ("model", "replica", "fsdp"))
    w_spec = P(None, ("model", "fsdp"), None)

    def group_grads(x_in, dy, lengths, w_up, w_down):
        y, f = lax.axis_index("replica"), lax.axis_index("fsdp")
        xi, c = f // 2, f % 2
        w_up, w_down = w_up[0], w_down[0]

        row = jnp.zeros((8, 128), jnp.int32).at[:MICRO, 0].set(lengths[:, 0].astype(jnp.int32))
        around, s1 = start(row, x_in, dy)
        s1 = s1.reshape(2, MICRO * BASE, D)
        s1_y = y_swap(s1)
        me = y * 4 + f
        lens = around[(me - jnp.arange(8)) % 8][:, :MICRO, 0]

        def cols(xd, cd, lo=0, n=HALF):
            own = lax.dynamic_slice(w_up, (0, ((2 * xd + cd) * 2 + y) * HALF + lo), (512, n))
            oth = lax.dynamic_slice(w_up, (0, ((2 * (1 - xd) + cd) * 2 + y) * HALF + lo), (512, n))
            return jnp.stack([own, oth])

        wd_own = lax.dynamic_slice(w_down, (y * HALF, 0), (HALF, D))
        from_s = core_swap(cols(xi, 1 - c))
        mine = cols(xi, c)
        wsets = []
        for lo, n in WSETS:
            a = x_swap(cols(1 - xi, c, lo * HB, n * HB))
            b = x_diag(cols(1 - xi, 1 - c, lo * HB, n * HB))
            d = x_swap(lax.dynamic_slice(w_down, (y * HALF + lo * HB, 0), (n * HB, D)))
            wsets.append((mine, from_s, a, b, wd_own, d))

        rest = lens - BASE
        r16 = (rest + 15) // 16 * 16
        tiles = (jnp.sum(r16, axis=1) + TM - 1) // TM
        my_rest = lax.dynamic_index_in_dim(rest, me, keepdims=False)
        my16 = lax.dynamic_index_in_dim(r16, me, keepdims=False)
        offs = jnp.concatenate([jnp.zeros((1,), jnp.int32), jnp.cumsum(my16)])
        both = tiles[0::2] + tiles[1::2]
        share = jnp.stack([(both + 1) // 2, both // 2], axis=1).reshape(8)
        which = jnp.sum(jnp.max(share) - FIRST > jnp.array(SIZES[:-1]))
        more = jnp.array(SIZES)[which]

        def at(v, i):
            return lax.dynamic_index_in_dim(v, i, keepdims=False)

        t_own, t_sib = at(tiles, me), at(tiles, me ^ 1)
        h_own = at(share, me)
        h_y, h_ys = at(share, me ^ 4), at(share, me ^ 5)
        at_f = [FIRST + 4 * jnp.minimum(more // 4, k) for k in range(4)]
        at_one = at_f[3] + more % 4 // 2 * 2
        starts = [at_f[0], at_f[1], at_f[2], at_f[3], at_one]

        packed = pack_rest(x_in, dy, my_rest, offs)
        packed_s = core_swap(packed)
        s1_s = core_swap(s1)
        pa, *pieces = build_send(packed, packed_s, jnp.stack([h_own, t_own, t_sib - h_own, *starts]).astype(jnp.int32))
        qa = y_swap(pa)

        i = jnp.arange(64)
        n_own = 12 + t_own + t_sib
        g_own = (n_own + G - 1) // G
        k = i - g_own * G
        tab = jnp.where(i < n_own, 3 * 32 + i - 12 - t_own, 2 * 32 + NT)
        tab = jnp.where(i < 12 + t_own, 2 * 32 + i - 12, tab)
        tab = jnp.where(i < 12, (i // 6) * 32 + i % 6, tab)
        tab = jnp.where((k >= 0) & (k < 12), (4 + k // 6) * 32 + k % 6, tab).astype(jnp.int32)
        info_own = jnp.stack([g_own, f]).astype(jnp.int32)
        info_all = jnp.stack([g_own + 3, f]).astype(jnp.int32)

        i = jnp.arange(56) - 12
        own_list = i < h_y
        t = jnp.where(own_list, i, i - h_y)
        late = 2 * 32 + t
        for n, lo in enumerate(starts):
            late = jnp.where(t >= lo, (3 + n) * 32 + t - lo, late)
        late = jnp.where(own_list, late, late + 6 * 32)
        late = jnp.where(i < h_y + h_ys, late, 14 * 32 + NT)
        late = jnp.where(i < 0, (i + 12) // 6 * 32 + (i + 12) % 6, late).astype(jnp.int32)
        info_late = jnp.stack([3 + (h_y + h_ys + G - 1) // G, xi, f]).astype(jnp.int32)
        pos = jnp.stack([y, xi, c]).astype(jnp.int32)

        own_srcs = (s1, s1_s, packed, packed_s)
        acc0 = early_grads(tab, info_own, own_srcs, wsets[0], 0, 0, 2)
        acc1 = early_grads(tab, info_own, own_srcs, wsets[1], 2, 2, 1, (late, info_late, pos))
        s1_ys = core_swap(s1_y)
        srcs = (*own_srcs, s1_y, s1_ys)
        acc2 = early_grads(tab, info_all, srcs, wsets[1], 2, 3, 1)

        def early(tab, info, srcs, w):
            return early_grads(tab, info, srcs, w, 4, 4, 4)

        got = lax.switch(
            which,
            [exchange_branch(n, early) for n in SIZES],
            pieces, tab, info_all, srcs, list(wsets[2]),
        )
        pieces, sib_pieces, acc3 = got[:5], got[5:10], got[10:]
        qas = core_swap(qa)
        srcs = (s1_y, s1_ys, qa, *pieces, qas, *sib_pieces, packed)
        prior = [(acc0, 0), (acc0, 1), (acc1, 0), (acc2, 0), *((acc3, k) for k in range(4))]

        out_d = out_u = None
        fin = []
        for p, j in enumerate(ORDER):
            deps = (fin[p - 2][0],) if p >= 2 else ()
            w_at = next(h for h, (lo, n) in enumerate(WSETS) if lo <= j < lo + n)
            keep_d, send_d, keep_u, send_u = chunk_grads(
                j, WSETS[w_at][0], late, info_late, 0 if j < OWN_ONLY else 3, srcs, wsets[w_at], *prior[j], deps
            )
            recv_d = x_swap(send_d)
            recv_u = x_swap(send_u)
            out_d, fd = finish_down(j, pos, keep_d, recv_d, out_d)
            rd = y_swap(fd)
            out_u, fuc, fus = finish_up(j, pos, keep_u, recv_u, out_u)
            ruc = y_swap(fuc)
            ruy = y_diag(fus)
            rus = core_swap(fus)
            fin.append((fd, (rd, ruc, ruy, rus)))
            if p >= LAG:
                out_d, out_u = store(ORDER[p - LAG], pos, *fin[p - LAG][1], (out_d, out_u))
        for p in range(NCH - LAG, NCH):
            out_d, out_u = store(ORDER[p], pos, *fin[p][1], (out_d, out_u))
        return out_u[None], out_d[None]


    return jax.shard_map(
        group_grads,
        mesh=mesh,
        in_specs=(tok_spec, tok_spec, len_spec, w_spec, w_spec),
        out_specs=(w_spec, w_spec),
        check_vma=False,
    )
```

profile of v0, /device:TPU:0, one launch (start us, length us, event | category | flops | bytes accessed | tf_op | source)
XLA Modules:
  0.0 1378.1 jit_solution(3304713265461160113)
XLA Ops:
  2.0 8.3 start.1
  13.4 16.6 %pack_rest.1.own_ref.refs_2_.refs_14_ = bf16[2,2432,2048]{2,1,0:T(8,128)(2,1)} custom-call(s32[3]{0:T(128)} %fusion.3.rest_ref, s32[4]{0:T(128)} %pad_add_fusion.3.offs_ref, bf16[3,1024,2048]{2,1,0:T(8,128)(2,1)} %x_ref.3, bf16[3,1024,2048]{2,1,0:T(8,128)(2,1)} %d_ref.3), custom_call_target="tpu_custom_call" | custom-call | flops 15000000512 | bytes 50000000 | tf_op jit(solution)/shard_map/pack_rest/pallas_call | solution.py:167
  31.4 136.8 %collective-permute-done.50.refs_0_.refs_4_ = bf16[2,768,2048]{2,1,0:T(8,128)(2,1)} collective-permute-done((bf16[2,768,2048]{2,1,0:T(8,128)(2,1)}, bf16[2,768,2048]{2,1,0:T(8,128)(2,1)}, u32[]{:S(2)}, u32[]{:S(2)}) %collective-permute-start.50) | collective-permute-done | bytes 6291488 | tf_op jit(solution)/shard_map/ppermute | solution.py:62
  171.1 3.9 constant_dynamic-slice_fusion.13
  180.2 15.4 %collective-permute-done.56.refs_17_ = bf16[2,512,512]{2,1,0:T(8,128)(2,1)S(1)} collective-permute-done((bf16[2,512,512]{2,1,0:T(8,128)(2,1)S(1)}, bf16[2,512,512]{2,1,0:T(8,128)(2,1)S(1)}, u32[]{:S(2)}, u32[]{:S(2)}) %collective-permute-start.56) | collective-permute-done | bytes 1048608 | tf_op jit(solution)/shard_map/ppermute | solution.py:54
  213.2 5.6 dynamic-slice_bitcast_fusion.refs_8_.refs_19_.refs_10_
  218.9 9.0 build_send.1
  228.0 36.3 %collective-permute-done.57.refs_18_ = bf16[2,512,512]{2,1,0:T(8,128)(2,1)} collective-permute-done((bf16[2,512,512]{2,1,0:T(8,128)(2,1)}, bf16[2,512,512]{2,1,0:T(8,128)(2,1)}, u32[]{:S(2)}, u32[]{:S(2)}) %collective-permute-start.57) | collective-permute-done | bytes 1048608 | tf_op jit(solution)/shard_map/ppermute | solution.py:58
  264.3 363.1 %conditional.1 = (bf16[2,512,2048]{2,1,0:T(8,128)(2,1)}, bf16[2,512,2048]{2,1,0:T(8,128)(2,1)}, bf16[2,512,2048]{2,1,0:T(8,128)(2,1)}, bf16[2,256,2048]{2,1,0:T(...) conditional(s32[]{:T(128)} %clamp.3, ...), branch_computations={%region_5.6_spmd, %region_6.7_spmd, %region_7.8_spmd, %region_8.9_... | conditional | flops 94489280512 | bytes 365829600 | solution.py:694
  275.5 224.9 %collective-permute-done.22 = bf16[2,256,2048]{2,1,0:T(8,128)(2,1)} collective-permute-done((bf16[2,256,2048]{2,1,0:T(8,128)(2,1)}, bf16[2,256,2048]{2,1,0:T(8,128)(2,1)}, u32[]{:S(2)}, u32[]{:S(2)}) %collective-permute-start.22) | collective-permute-done | bytes 2097184 | tf_op jit(solution)/shard_map/cond/branch_4_fun/ppermute | solution.py:62
  501.0 119.2 %branch_4_fun.9 = (f32[4,256,2048]{2,1,0:T(8,128)}, f32[4,256,2048]{2,1,0:T(8,128)}) custom-call(s32[64]{0:T(128)S(1)} %get-tuple-element.363.tab_ref, s32[2]{0:T(128)S(1)} %get-tuple-element.364.info_ref, bf16[2,768,2048]{2,1,0:T(8,128)(2,1)} %get-tuple-element.365.refs_0_, bf16[2,768,2048]{2,1,0:T(8,128)(2,1)} %get-tuple-element.366.refs_1_, ...), custom_call_target="tpu_custom_call" | custom-call | flops 94489280512 | bytes 240000000 | tf_op jit(solution)/shard_map/cond/branch_4_fun/pallas_call | solution.py:399
  627.4 21.3 %collective-permute-start.53 = (bf16[2,384,2048]{2,1,0:T(8,128)(2,1)}, bf16[2,384,2048]{2,1,0:T(8,128)(2,1)}, u32[]{:S(2)}, u32[]{:S(2)}) collective-permute-start(bf16[2,384,2048]{2,1,0:T(8,128)(2,1)} %get-tuple-element.557), channel_id=1, source_target_pairs={{0,4},{4,0},{1,5},{5,1},{2,6},{6,2},{3,7},{7,3}} | collective-permute-start | bytes 9437192 | tf_op jit(solution)/shard_map/ppermute | solution.py:62
  663.1 37.4 %collective-permute-done.63.refs_6_.refs_17_ = bf16[2,512,256]{2,1,0:T(8,128)(2,1)S(1)} collective-permute-done((bf16[2,512,256]{2,1,0:T(8,128)(2,1)}, bf16[2,512,256]{2,1,0:T(8,128)(2,1)S(1)}, u32[]{:S(2)}, u32[]{:S(2)}) %collective-permute-start.63) | collective-permute-done | bytes 524320 | tf_op jit(solution)/shard_map/ppermute | solution.py:54
  700.5 9.7 collective-permute-done.64.refs_7_.refs_18_
  711.3 6.5 collective-permute-done.53.refs_2_
  717.8 46.2 %shard_map.87 = (f32[2,256,2048]{2,1,0:T(8,128)}, f32[2,256,2048]{2,1,0:T(8,128)}) custom-call(s32[64]{0:T(128)S(1)} %and_select_fusion.4.tab_ref, s32[2]{0:T(128)} %pad_add_fusion.5.info_ref, bf16[2,768,2048]{2,1,0:T(8,128)(2,1)} %bitcast.68, bf16[2,768,2048]{2,1,0:T(8,128)(2,1)} %collective-permute-done.54.refs_1_, ...), custom_call_target="tpu_custom_call" | custom-call | flops 47244640256 | bytes 120000000 | tf_op jit(solution)/shard_map/pallas_call | solution.py:399
  764.8 32.7 %shard_map.89 = (f32[1,256,2048]{2,1,0:T(8,128)}, f32[1,256,2048]{2,1,0:T(8,128)}) custom-call(s32[64]{0:T(128)S(1)} %and_select_fusion.4.tab_ref, s32[2]{0:T(128)S(1)} %pad_add_fusion.4.info_ref, bf16[2,768,2048]{2,1,0:T(8,128)(2,1)} %bitcast.69, bf16[2,768,2048]{2,1,0:T(8,128)(2,1)} %collective-permute-done.54.refs_1_, ...), custom_call_target="tpu_custom_call" | custom-call | flops 23622320128 | bytes 60000000 | tf_op jit(solution)/shard_map/pallas_call | solution.py:399
  799.1 24.5 %shard_map.90 = (f32[128,2048]{1,0:T(8,128)}, f32[128,2048]{1,0:T(8,128)}, f32[128,2048]{1,0:T(8,128)}, f32[128,2048]{1,0:T(8,128)}) custom-call(s32[56]{0:T(128)} %compare_select_fusion.14.refs_10_.tab_ref, s32[3]{0:T(128)} %pad_add_fusion.2.refs_11_.info_ref, bf16[2,768,2048]{2,1,0:T(8,128)(2,1)} %collective-permute-done.50.refs_0_.refs_4_, ...), custom_call_target="tpu_custom_call" | custom-call | flops 12884901888 | bytes 40000000 | tf_op jit(solution)/shard_map/pallas_call | solution.py:457
  823.7 25.4 %shard_map.88 = (f32[128,2048]{1,0:T(8,128)}, f32[128,2048]{1,0:T(8,128)}, f32[128,2048]{1,0:T(8,128)}, f32[128,2048]{1,0:T(8,128)}) custom-call(s32[56]{0:T(128)} %compare_select_fusion.14.refs_10_.tab_ref, s32[3]{0:T(128)} %pad_add_fusion.2.refs_11_.info_ref, bf16[2,768,2048]{2,1,0:T(8,128)(2,1)} %collective-permute-done.50.refs_0_.refs_4_, ...), custom_call_target="tpu_custom_call" | custom-call | flops 12884901888 | bytes 40000000 | tf_op jit(solution)/shard_map/pallas_call | solution.py:457
  853.9 32.4 %shard_map.94 = (f32[128,2048]{1,0:T(8,128)}, f32[128,2048]{1,0:T(8,128)}, f32[128,2048]{1,0:T(8,128)}, f32[128,2048]{1,0:T(8,128)}) custom-call(s32[56]{0:T(128)} %compare_select_fusion.14.refs_10_.tab_ref, s32[3]{0:T(128)} %pad_add_fusion.2.refs_11_.info_ref, bf16[2,768,2048]{2,1,0:T(8,128)(2,1)} %collective-permute-done.50.refs_0_.refs_4_, ...), custom_call_target="tpu_custom_call" | custom-call | flops 12884901888 | bytes 40000000 | tf_op jit(solution)/shard_map/pallas_call | solution.py:457
  889.7 24.7 %shard_map.93 = (f32[128,2048]{1,0:T(8,128)}, f32[128,2048]{1,0:T(8,128)}, f32[128,2048]{1,0:T(8,128)}, f32[128,2048]{1,0:T(8,128)}) custom-call(s32[56]{0:T(128)} %compare_select_fusion.14.refs_10_.tab_ref, s32[3]{0:T(128)} %pad_add_fusion.2.refs_11_.info_ref, bf16[2,768,2048]{2,1,0:T(8,128)(2,1)} %collective-permute-done.50.refs_0_.refs_4_, ...), custom_call_target="tpu_custom_call" | custom-call | flops 12884901888 | bytes 40000000 | tf_op jit(solution)/shard_map/pallas_call | solution.py:457
  914.5 5.9 collective-permute-done.73.rc
  925.0 7.3 collective-permute-start.75
  933.7 9.1 collective-permute-done.69.rc
  945.5 19.7 %collective-permute-done.68.rc = f32[128,2048]{1,0:T(8,128)S(1)} collective-permute-done((f32[128,2048]{1,0:T(8,128)}, f32[128,2048]{1,0:T(8,128)S(1)}, u32[]{:S(2)}, u32[]{:S(2)}) %collective-permute-start.68) | collective-permute-done | bytes 1048608 | tf_op jit(solution)/shard_map/ppermute | solution.py:54
  968.0 32.6 %shard_map.97 = (f32[128,2048]{1,0:T(8,128)}, f32[128,2048]{1,0:T(8,128)}, f32[128,2048]{1,0:T(8,128)}, f32[128,2048]{1,0:T(8,128)}) custom-call(s32[56]{0:T(128)} %compare_select_fusion.14.refs_10_.tab_ref, s32[3]{0:T(128)} %pad_add_fusion.2.refs_11_.info_ref, bf16[2,768,2048]{2,1,0:T(8,128)(2,1)} %collective-permute-done.50.refs_0_.refs_4_, ...), custom_call_target="tpu_custom_call" | custom-call | flops 12884901888 | bytes 40000000 | tf_op jit(solution)/shard_map/pallas_call | solution.py:457
  1000.6 3.4 collective-permute-start.78
  1005.0 4.7 collective-permute-done.83.rc
  1010.7 8.5 collective-permute-start.79
  1019.2 24.7 %shard_map.100 = (f32[128,2048]{1,0:T(8,128)}, f32[128,2048]{1,0:T(8,128)}, f32[128,2048]{1,0:T(8,128)}, f32[128,2048]{1,0:T(8,128)}) custom-call(s32[56]{0:T(128)} %compare_select_fusion.14.refs_10_.tab_ref, s32[3]{0:T(128)} %pad_add_fusion.2.refs_11_.info_ref, bf16[2,768,2048]{2,1,0:T(8,128)(2,1)} %collective-permute-done.50.refs_0_.refs_4_, ...), custom_call_target="tpu_custom_call" | custom-call | flops 12884901888 | bytes 40000000 | tf_op jit(solution)/shard_map/pallas_call | solution.py:457
  1055.5 25.4 %shard_map.86 = (f32[1,256,2048]{2,1,0:T(8,128)}, f32[1,256,2048]{2,1,0:T(8,128)}) custom-call(s32[64]{0:T(128)S(1)} %copy-done.59, s32[2]{0:T(128)} %pad_add_fusion.5.info_ref, bf16[2,768,2048]{2,1,0:T(8,128)(2,1)} %bitcast.70, bf16[2,768,2048]{2,1,0:T(8,128)(2,1)} %collective-permute-done.54.refs_1_, ...), custom_call_target="tpu_custom_call" | custom-call | flops 23622320128 | bytes 60000000 | tf_op jit(solution)/shard_map/pallas_call | solution.py:399
  1081.0 3.3 shard_map.103
  1087.9 3.2 collective-permute-start.88
  1093.0 6.5 collective-permute-done.84.rc
  1101.4 20.5 %collective-permute-done.95.rc = f32[128,2048]{1,0:T(8,128)} collective-permute-done((f32[128,2048]{1,0:T(8,128)}, f32[128,2048]{1,0:T(8,128)}, u32[]{:S(2)}, u32[]{:S(2)}) %collective-permute-start.95) | collective-permute-done | bytes 1048608 | tf_op jit(solution)/shard_map/ppermute | solution.py:54
  1138.2 4.6 collective-permute-done.70.rc
  1143.8 25.0 %shard_map.109 = (f32[128,2048]{1,0:T(8,128)}, f32[128,2048]{1,0:T(8,128)}, f32[128,2048]{1,0:T(8,128)}, f32[128,2048]{1,0:T(8,128)}) custom-call(s32[56]{0:T(128)} %compare_select_fusion.14.refs_10_.tab_ref, s32[3]{0:T(128)} %pad_add_fusion.2.refs_11_.info_ref, bf16[2,768,2048]{2,1,0:T(8,128)(2,1)} %collective-permute-done.50.refs_0_.refs_4_, ...), custom_call_target="tpu_custom_call" | custom-call | flops 12884901888 | bytes 40000000 | tf_op jit(solution)/shard_map/pallas_call | solution.py:457
  1175.9 5.5 collective-permute-done.91.d_ref
  1181.4 11.2 collective-permute-done.107.uc_ref
  1193.5 10.4 collective-permute-done.108.uy_ref
  1204.5 32.3 %shard_map.108 = (f32[128,2048]{1,0:T(8,128)}, f32[128,2048]{1,0:T(8,128)}, f32[128,2048]{1,0:T(8,128)}, f32[128,2048]{1,0:T(8,128)}) custom-call(s32[56]{0:T(128)} %compare_select_fusion.14.refs_10_.tab_ref, s32[3]{0:T(128)} %pad_add_fusion.2.refs_11_.info_ref, bf16[2,768,2048]{2,1,0:T(8,128)(2,1)} %collective-permute-done.50.refs_0_.refs_4_, ...), custom_call_target="tpu_custom_call" | custom-call | flops 12884901888 | bytes 40000000 | tf_op jit(solution)/shard_map/pallas_call | solution.py:457
  1243.0 3.3 shard_map.111
  1253.8 9.2 collective-permute-done.85.rc
  1263.0 21.3 %collective-permute-done.98.rc = f32[128,2048]{1,0:T(8,128)S(1)} collective-permute-done((f32[128,2048]{1,0:T(8,128)}, f32[128,2048]{1,0:T(8,128)S(1)}, u32[]{:S(2)}, u32[]{:S(2)}) %collective-permute-start.98) | collective-permute-done | bytes 1048608 | tf_op jit(solution)/shard_map/ppermute | solution.py:54
  1289.9 3.3 shard_map.117
  1293.2 39.1 %collective-permute-done.103.uc_ref = f32[2,512,128]{2,1,0:T(8,128)S(1)} collective-permute-done((f32[2,512,128]{2,1,0:T(8,128)S(1)}, f32[2,512,128]{2,1,0:T(8,128)S(1)}, u32[]{:S(2)}, u32[]{:S(2)}) %collective-permute-start.103) | collective-permute-done | bytes 524320 | tf_op jit(solution)/shard_map/ppermute | solution.py:62
  1334.4 3.3 shard_map.118
  1340.0 35.5 %collective-permute-done.99.uc_ref = f32[2,512,128]{2,1,0:T(8,128)S(1)} collective-permute-done((f32[2,512,128]{2,1,0:T(8,128)S(1)}, f32[2,512,128]{2,1,0:T(8,128)S(1)}, u32[]{:S(2)}, u32[]{:S(2)}) %collective-permute-start.99) | collective-permute-done | bytes 524320 | tf_op jit(solution)/shard_map/ppermute | solution.py:62
  (304 shorter events, 136.1 us)
Async XLA Ops:
  30.0 188.9 %collective-permute-start.52 = (bf16[2,2432,2048]{2,1,0:T(8,128)(2,1)}, bf16[2,2432,2048]{2,1,0:T(8,128)(2,1)}, u32[]{:S(2)}, u32[]{:S(2)}) collective-permute-start(bf16[2,2432,2048]{2,1,0:T(8,128)(2,1)} %pack_rest.1.own_ref.refs_2_.refs_14_), channel_id=1, source_target_pairs={{0,1},{1,0},{2,3},{3,2},{4,5},{5,4},{6,7},{7,6}} | collective-permute-start | bytes 59768840 | tf_op jit(solution)/shard_map/ppermute | solution.py:50
  30.1 138.2 %collective-permute-start.50 = (bf16[2,768,2048]{2,1,0:T(8,128)(2,1)}, bf16[2,768,2048]{2,1,0:T(8,128)(2,1)}, u32[]{:S(2)}, u32[]{:S(2)}) collective-permute-start(bf16[2,768,2048]{2,1,0:T(8,128)(2,1)} %bitcast.58), channel_id=1, source_target_pairs={{0,4},{4,0},{1,5},{5,1},{2,6},{6,2},{3,7},{7,3}} | collective-permute-start | bytes 18874376 | tf_op jit(solution)/shard_map/ppermute | solution.py:62
  31.2 233.1 %collective-permute-start.54 = (bf16[2,768,2048]{2,1,0:T(8,128)(2,1)}, bf16[2,768,2048]{2,1,0:T(8,128)(2,1)}, u32[]{:S(2)}, u32[]{:S(2)}) collective-permute-start(bf16[2,768,2048]{2,1,0:T(8,128)(2,1)} %bitcast.59), channel_id=1, source_target_pairs={{0,1},{1,0},{2,3},{3,2},{4,5},{5,4},{6,7},{7,6}} | collective-permute-start | bytes 18874376 | tf_op jit(solution)/shard_map/ppermute | solution.py:50
  168.2 96.0 %collective-permute-start.51 = (bf16[2,768,2048]{2,1,0:T(8,128)(2,1)}, bf16[2,768,2048]{2,1,0:T(8,128)(2,1)}, u32[]{:S(2)}, u32[]{:S(2)}) collective-permute-start(bf16[2,768,2048]{2,1,0:T(8,128)(2,1)} %collective-permute-done.50.refs_0_.refs_4_), channel_id=1, source_target_pairs={{0,1},{1,0},{2,3},{3,2},{4,5},{5,4},{6,7},{7,6}} | collective-permute-start | bytes 18874376 | tf_op jit(solution)/shard_map/ppermute | solution.py:50
  176.6 87.7 %collective-permute-start.55 = (bf16[2,512,1024]{2,1,0:T(8,128)(2,1)}, bf16[2,512,1024]{2,1,0:T(8,128)(2,1)}, u32[]{:S(2)}, u32[]{:S(2)}) collective-permute-start(bf16[2,512,1024]{2,1,0:T(8,128)(2,1)} %pad_maximum_fusion.1), channel_id=1, source_target_pairs={{0,1},{1,0},{2,3},{3,2},{4,5},{5,4},{6,7},{7,6}} | collective-permute-start | bytes 6291464 | tf_op jit(solution)/shard_map/ppermute | solution.py:50
  195.6 68.7 %collective-permute-start.58 = (bf16[512,2048]{1,0:T(8,128)(2,1)}, bf16[512,2048]{1,0:T(8,128)(2,1)}, u32[]{:S(2)}, u32[]{:S(2)}) collective-permute-start(bf16[512,2048]{1,0:T(8,128)(2,1)} %dynamic-slice_bitcast_fusion.1), channel_id=1, source_target_pairs={{0,2},{2,0},{1,3},{3,1},{4,6},{6,4},{5,7},{7,5}} | collective-permute-start | bytes 6291464 | tf_op jit(solution)/shard_map/ppermute | solution.py:54
  218.9 45.4 %collective-permute-start.57 = (bf16[2,512,512]{2,1,0:T(8,128)(2,1)}, bf16[2,512,512]{2,1,0:T(8,128)(2,1)}, u32[]{:S(2)}, u32[]{:S(2)}) collective-permute-start(bf16[2,512,512]{2,1,0:T(8,128)(2,1)} %pad_maximum_fusion.3), channel_id=1, source_target_pairs={{0,3},{3,0},{1,2},{2,1},{4,7},{7,4},{5,6},{6,5}} | collective-permute-start | bytes 3145736 | tf_op jit(solution)/shard_map/ppermute | solution.py:58
  271.9 228.6 %collective-permute-start.20 = (bf16[2,512,2048]{2,1,0:T(8,128)(2,1)}, bf16[2,512,2048]{2,1,0:T(8,128)(2,1)}, u32[]{:S(2)}, u32[]{:S(2)}) collective-permute-start(bf16[2,512,2048]{2,1,0:T(8,128)(2,1)} %get-tuple-element.360), channel_id=1, source_target_pairs={{0,4},{4,0},{1,5},{5,1},{2,6},{6,2},{3,7},{7,3}} | collective-permute-start | bytes 12582920 | tf_op jit(solution)/shard_map/cond/branch_4_fun/ppermute | solution.py:62
  273.4 227.4 %collective-permute-start.21 = (bf16[2,512,2048]{2,1,0:T(8,128)(2,1)}, bf16[2,512,2048]{2,1,0:T(8,128)(2,1)}, u32[]{:S(2)}, u32[]{:S(2)}) collective-permute-start(bf16[2,512,2048]{2,1,0:T(8,128)(2,1)} %get-tuple-element.361), channel_id=1, source_target_pairs={{0,4},{4,0},{1,5},{5,1},{2,6},{6,2},{3,7},{7,3}} | collective-permute-start | bytes 12582920 | tf_op jit(solution)/shard_map/cond/branch_4_fun/ppermute | solution.py:62
  273.9 226.4 %collective-permute-start.22 = (bf16[2,256,2048]{2,1,0:T(8,128)(2,1)}, bf16[2,256,2048]{2,1,0:T(8,128)(2,1)}, u32[]{:S(2)}, u32[]{:S(2)}) collective-permute-start(bf16[2,256,2048]{2,1,0:T(8,128)(2,1)} %get-tuple-element.362), channel_id=1, source_target_pairs={{0,4},{4,0},{1,5},{5,1},{2,6},{6,2},{3,7},{7,3}} | collective-permute-start | bytes 6291464 | tf_op jit(solution)/shard_map/cond/branch_4_fun/ppermute | solution.py:62
  500.3 119.8 %collective-permute-start.25 = (bf16[2,256,2048]{2,1,0:T(8,128)(2,1)}, bf16[2,256,2048]{2,1,0:T(8,128)(2,1)}, u32[]{:S(2)}, u32[]{:S(2)}) collective-permute-start(bf16[2,256,2048]{2,1,0:T(8,128)(2,1)} %collective-permute-done.22), channel_id=1, source_target_pairs={{0,1},{1,0},{2,3},{3,2},{4,5},{5,4},{6,7},{7,6}} | collective-permute-start | bytes 6291464 | tf_op jit(solution)/shard_map/cond/branch_4_fun/ppermute | solution.py:50
  500.4 119.7 %collective-permute-start.23 = (bf16[2,512,2048]{2,1,0:T(8,128)(2,1)}, bf16[2,512,2048]{2,1,0:T(8,128)(2,1)}, u32[]{:S(2)}, u32[]{:S(2)}) collective-permute-start(bf16[2,512,2048]{2,1,0:T(8,128)(2,1)} %collective-permute-done.20), channel_id=1, source_target_pairs={{0,1},{1,0},{2,3},{3,2},{4,5},{5,4},{6,7},{7,6}} | collective-permute-start | bytes 12582920 | tf_op jit(solution)/shard_map/cond/branch_4_fun/ppermute | solution.py:50
  500.8 119.3 %collective-permute-start.24 = (bf16[2,512,2048]{2,1,0:T(8,128)(2,1)}, bf16[2,512,2048]{2,1,0:T(8,128)(2,1)}, u32[]{:S(2)}, u32[]{:S(2)}) collective-permute-start(bf16[2,512,2048]{2,1,0:T(8,128)(2,1)} %collective-permute-done.21), channel_id=1, source_target_pairs={{0,1},{1,0},{2,3},{3,2},{4,5},{5,4},{6,7},{7,6}} | collective-permute-start | bytes 12582920 | tf_op jit(solution)/shard_map/cond/branch_4_fun/ppermute | solution.py:50
  627.4 90.4 %collective-permute-start.53 = (bf16[2,384,2048]{2,1,0:T(8,128)(2,1)}, bf16[2,384,2048]{2,1,0:T(8,128)(2,1)}, u32[]{:S(2)}, u32[]{:S(2)}) collective-permute-start(bf16[2,384,2048]{2,1,0:T(8,128)(2,1)} %get-tuple-element.557), channel_id=1, source_target_pairs={{0,4},{4,0},{1,5},{5,1},{2,6},{6,2},{3,7},{7,3}} | collective-permute-start | bytes 9437192 | tf_op jit(solution)/shard_map/ppermute | solution.py:62
  651.8 66.0 %collective-permute-start.65 = (bf16[256,2048]{1,0:T(8,128)(2,1)}, bf16[256,2048]{1,0:T(8,128)(2,1)}, u32[]{:S(2)}, u32[]{:S(2)}) collective-permute-start(bf16[256,2048]{1,0:T(8,128)(2,1)} %get-tuple-element.675), channel_id=1, source_target_pairs={{0,2},{2,0},{1,3},{3,1},{4,6},{6,4},{5,7},{7,5}} | collective-permute-start | bytes 3145736 | tf_op jit(solution)/shard_map/ppermute | solution.py:54
  654.3 109.7 %collective-permute-start.60 = (bf16[2,512,256]{2,1,0:T(8,128)(2,1)}, bf16[2,512,256]{2,1,0:T(8,128)(2,1)S(1)}, u32[]{:S(2)}, u32[]{:S(2)}) collective-permute-start(bf16[2,512,256]{2,1,0:T(8,128)(2,1)} %pad_maximum_fusion.4), channel_id=1, source_target_pairs={{0,2},{2,0},{1,3},{3,1},{4,6},{6,4},{5,7},{7,5}} | collective-permute-start | bytes 1572872 | tf_op jit(solution)/shard_map/ppermute | solution.py:54
  657.2 53.0 %collective-permute-start.64 = (bf16[2,512,256]{2,1,0:T(8,128)(2,1)S(1)}, bf16[2,512,256]{2,1,0:T(8,128)(2,1)S(1)}, u32[]{:S(2)}, u32[]{:S(2)}) collective-permute-start(bf16[2,512,256]{2,1,0:T(8,128)(2,1)S(1)} %pad_maximum_fusion.7), channel_id=1, source_target_pairs={{0,3},{3,0},{1,2},{2,1},{4,7},{7,4},{5,6},{6,5}} | collective-permute-start | bytes 1572872 | tf_op jit(solution)/shard_map/ppermute | solution.py:58
  700.5 63.5 %collective-permute-start.61 = (bf16[2,512,256]{2,1,0:T(8,128)(2,1)}, bf16[2,512,256]{2,1,0:T(8,128)(2,1)}, u32[]{:S(2)}, u32[]{:S(2)}) collective-permute-start(bf16[2,512,256]{2,1,0:T(8,128)(2,1)} %pad_maximum_fusion.5), channel_id=1, source_target_pairs={{0,3},{3,0},{1,2},{2,1},{4,7},{7,4},{5,6},{6,5}} | collective-permute-start | bytes 1572872 | tf_op jit(solution)/shard_map/ppermute | solution.py:58
  710.2 53.8 %collective-permute-start.62 = (bf16[256,2048]{1,0:T(8,128)(2,1)}, bf16[256,2048]{1,0:T(8,128)(2,1)}, u32[]{:S(2)}, u32[]{:S(2)}) collective-permute-start(bf16[256,2048]{1,0:T(8,128)(2,1)} %get-tuple-element.676), channel_id=1, source_target_pairs={{0,2},{2,0},{1,3},{3,1},{4,6},{6,4},{5,7},{7,5}} | collective-permute-start | bytes 3145736 | tf_op jit(solution)/shard_map/ppermute | solution.py:54
  717.8 79.7 %collective-permute-start.59 = (bf16[2,384,2048]{2,1,0:T(8,128)(2,1)}, bf16[2,384,2048]{2,1,0:T(8,128)(2,1)S(1)}, u32[]{:S(2)}, u32[]{:S(2)}) collective-permute-start(bf16[2,384,2048]{2,1,0:T(8,128)(2,1)} %collective-permute-done.53.refs_2_), channel_id=1, source_target_pairs={{0,1},{1,0},{2,3},{3,2},{4,5},{5,4},{6,7},{7,6}} | collective-permute-start | bytes 9437192 | tf_op jit(solution)/shard_map/ppermute | solution.py:50
  849.1 73.8 %collective-permute-start.72 = (f32[128,2048]{1,0:T(8,128)}, f32[128,2048]{1,0:T(8,128)S(1)}, u32[]{:S(2)}, u32[]{:S(2)}) collective-permute-start(f32[128,2048]{1,0:T(8,128)} %get-tuple-element.598), channel_id=1, source_target_pairs={{0,2},{2,0},{1,3},{3,1},{4,6},{6,4},{5,7},{7,5}} | collective-permute-start | bytes 3145736 | tf_op jit(solution)/shard_map/ppermute | solution.py:54
  851.1 69.3 %collective-permute-start.73 = (f32[128,2048]{1,0:T(8,128)}, f32[128,2048]{1,0:T(8,128)}, u32[]{:S(2)}, u32[]{:S(2)}) collective-permute-start(f32[128,2048]{1,0:T(8,128)} %get-tuple-element.600), channel_id=1, source_target_pairs={{0,2},{2,0},{1,3},{3,1},{4,6},{6,4},{5,7},{7,5}} | collective-permute-start | bytes 3145736 | tf_op jit(solution)/shard_map/ppermute | solution.py:54
  886.3 56.5 %collective-permute-start.69 = (f32[128,2048]{1,0:T(8,128)}, f32[128,2048]{1,0:T(8,128)S(1)}, u32[]{:S(2)}, u32[]{:S(2)}) collective-permute-start(f32[128,2048]{1,0:T(8,128)} %get-tuple-element.591), channel_id=1, source_target_pairs={{0,2},{2,0},{1,3},{3,1},{4,6},{6,4},{5,7},{7,5}} | collective-permute-start | bytes 3145736 | tf_op jit(solution)/shard_map/ppermute | solution.py:54
  914.4 50.8 %collective-permute-start.68 = (f32[128,2048]{1,0:T(8,128)}, f32[128,2048]{1,0:T(8,128)S(1)}, u32[]{:S(2)}, u32[]{:S(2)}) collective-permute-start(f32[128,2048]{1,0:T(8,128)} %get-tuple-element.588), channel_id=1, source_target_pairs={{0,2},{2,0},{1,3},{3,1},{4,6},{6,4},{5,7},{7,5}} | collective-permute-start | bytes 3145736 | tf_op jit(solution)/shard_map/ppermute | solution.py:54
  925.0 79.0 %collective-permute-start.75 = (f32[2,512,128]{2,1,0:T(8,128)}, f32[2,512,128]{2,1,0:T(8,128)S(1)}, u32[]{:S(2)}, u32[]{:S(2)}) collective-permute-start(f32[2,512,128]{2,1,0:T(8,128)} %get-tuple-element.603), channel_id=1, source_target_pairs={{0,5},{1,4},{2,7},{3,6},{4,1},{5,0},{6,3},{7,2}} | collective-permute-start | bytes 1572872 | tf_op jit(solution)/shard_map/ppermute | solution.py:66
  932.3 118.3 %collective-permute-start.76 = (f32[2,512,128]{2,1,0:T(8,128)}, f32[2,512,128]{2,1,0:T(8,128)}, u32[]{:S(2)}, u32[]{:S(2)}) collective-permute-start(f32[2,512,128]{2,1,0:T(8,128)} %get-tuple-element.603), channel_id=1, source_target_pairs={{0,1},{1,0},{2,3},{3,2},{4,5},{5,4},{6,7},{7,6}} | collective-permute-start | bytes 1572872 | tf_op jit(solution)/shard_map/ppermute | solution.py:50
  933.6 66.9 %collective-permute-start.74 = (f32[2,512,128]{2,1,0:T(8,128)}, f32[2,512,128]{2,1,0:T(8,128)}, u32[]{:S(2)}, u32[]{:S(2)}) collective-permute-start(f32[2,512,128]{2,1,0:T(8,128)} %get-tuple-element.602), channel_id=1, source_target_pairs={{0,4},{4,0},{1,5},{5,1},{2,6},{6,2},{3,7},{7,3}} | collective-permute-start | bytes 1572872 | tf_op jit(solution)/shard_map/ppermute | solution.py:62
  942.8 62.1 %collective-permute-start.82 = (f32[128,2048]{1,0:T(8,128)}, f32[128,2048]{1,0:T(8,128)S(1)}, u32[]{:S(2)}, u32[]{:S(2)}) collective-permute-start(f32[128,2048]{1,0:T(8,128)} %get-tuple-element.611), channel_id=1, source_target_pairs={{0,2},{2,0},{1,3},{3,1},{4,6},{6,4},{5,7},{7,5}} | collective-permute-start | bytes 3145736 | tf_op jit(solution)/shard_map/ppermute | solution.py:54
  1000.6 54.8 %collective-permute-start.78 = (f32[128,2048]{1,0:T(8,128)S(1)}, f32[128,2048]{1,0:T(8,128)}, u32[]{:S(2)}, u32[]{:S(2)}) collective-permute-start(f32[128,2048]{1,0:T(8,128)S(1)} %copy-done.9), channel_id=1, source_target_pairs={{0,4},{4,0},{1,5},{5,1},{2,6},{6,2},{3,7},{7,3}} | collective-permute-start | bytes 3145736 | tf_op jit(solution)/shard_map/ppermute | solution.py:62
  1004.8 45.8 %collective-permute-start.80 = (f32[2,512,128]{2,1,0:T(8,128)}, f32[2,512,128]{2,1,0:T(8,128)S(1)}, u32[]{:S(2)}, u32[]{:S(2)}) collective-permute-start(f32[2,512,128]{2,1,0:T(8,128)} %copy-done.48), channel_id=1, source_target_pairs={{0,5},{1,4},{2,7},{3,6},{4,1},{5,0},{6,3},{7,2}} | collective-permute-start | bytes 1572872 | tf_op jit(solution)/shard_map/ppermute | solution.py:66
  1004.8 48.6 %collective-permute-start.81 = (f32[2,512,128]{2,1,0:T(8,128)}, f32[2,512,128]{2,1,0:T(8,128)}, u32[]{:S(2)}, u32[]{:S(2)}) collective-permute-start(f32[2,512,128]{2,1,0:T(8,128)} %copy-done.48), channel_id=1, source_target_pairs={{0,1},{1,0},{2,3},{3,2},{4,5},{5,4},{6,7},{7,6}} | collective-permute-start | bytes 1572872 | tf_op jit(solution)/shard_map/ppermute | solution.py:50
  1051.4 48.0 %collective-permute-start.84 = (f32[128,2048]{1,0:T(8,128)}, f32[128,2048]{1,0:T(8,128)}, u32[]{:S(2)}, u32[]{:S(2)}) collective-permute-start(f32[128,2048]{1,0:T(8,128)} %get-tuple-element.620), channel_id=1, source_target_pairs={{0,2},{2,0},{1,3},{3,1},{4,6},{6,4},{5,7},{7,5}} | collective-permute-start | bytes 3145736 | tf_op jit(solution)/shard_map/ppermute | solution.py:54
  1055.5 66.5 %collective-permute-start.95 = (f32[128,2048]{1,0:T(8,128)}, f32[128,2048]{1,0:T(8,128)}, u32[]{:S(2)}, u32[]{:S(2)}) collective-permute-start(f32[128,2048]{1,0:T(8,128)} %get-tuple-element.636), channel_id=1, source_target_pairs={{0,2},{2,0},{1,3},{3,1},{4,6},{6,4},{5,7},{7,5}} | collective-permute-start | bytes 3145736 | tf_op jit(solution)/shard_map/ppermute | solution.py:54
  1080.9 61.9 %collective-permute-start.70 = (f32[128,2048]{1,0:T(8,128)}, f32[128,2048]{1,0:T(8,128)S(1)}, u32[]{:S(2)}, u32[]{:S(2)}) collective-permute-start(f32[128,2048]{1,0:T(8,128)} %get-tuple-element.596), channel_id=1, source_target_pairs={{0,2},{2,0},{1,3},{3,1},{4,6},{6,4},{5,7},{7,5}} | collective-permute-start | bytes 3145736 | tf_op jit(solution)/shard_map/ppermute | solution.py:54
  1134.5 46.9 %collective-permute-start.91 = (f32[128,2048]{1,0:T(8,128)S(1)}, f32[128,2048]{1,0:T(8,128)}, u32[]{:S(2)}, u32[]{:S(2)}) collective-permute-start(f32[128,2048]{1,0:T(8,128)S(1)} %copy-done.3), channel_id=1, source_target_pairs={{0,4},{4,0},{1,5},{5,1},{2,6},{6,2},{3,7},{7,3}} | collective-permute-start | bytes 3145736 | tf_op jit(solution)/shard_map/ppermute | solution.py:62
  1137.7 54.9 %collective-permute-start.107 = (f32[2,512,128]{2,1,0:T(8,128)}, f32[2,512,128]{2,1,0:T(8,128)}, u32[]{:S(2)}, u32[]{:S(2)}) collective-permute-start(f32[2,512,128]{2,1,0:T(8,128)} %get-tuple-element.655), channel_id=1, source_target_pairs={{0,4},{4,0},{1,5},{5,1},{2,6},{6,2},{3,7},{7,3}} | collective-permute-start | bytes 1572872 | tf_op jit(solution)/shard_map/ppermute | solution.py:62
  1143.8 60.1 %collective-permute-start.108 = (f32[2,512,128]{2,1,0:T(8,128)}, f32[2,512,128]{2,1,0:T(8,128)}, u32[]{:S(2)}, u32[]{:S(2)}) collective-permute-start(f32[2,512,128]{2,1,0:T(8,128)} %get-tuple-element.656), channel_id=1, source_target_pairs={{0,5},{1,4},{2,7},{3,6},{4,1},{5,0},{6,3},{7,2}} | collective-permute-start | bytes 1572872 | tf_op jit(solution)/shard_map/ppermute | solution.py:66
  1174.0 62.8 %collective-permute-start.109 = (f32[2,512,128]{2,1,0:T(8,128)}, f32[2,512,128]{2,1,0:T(8,128)}, u32[]{:S(2)}, u32[]{:S(2)}) collective-permute-start(f32[2,512,128]{2,1,0:T(8,128)} %get-tuple-element.656), channel_id=1, source_target_pairs={{0,1},{1,0},{2,3},{3,2},{4,5},{5,4},{6,7},{7,6}} | collective-permute-start | bytes 1572872 | tf_op jit(solution)/shard_map/ppermute | solution.py:50
  1175.9 63.0 %collective-permute-start.90 = (f32[128,2048]{1,0:T(8,128)}, f32[128,2048]{1,0:T(8,128)}, u32[]{:S(2)}, u32[]{:S(2)}) collective-permute-start(f32[128,2048]{1,0:T(8,128)} %get-tuple-element.631), channel_id=1, source_target_pairs={{0,2},{2,0},{1,3},{3,1},{4,6},{6,4},{5,7},{7,5}} | collective-permute-start | bytes 3145736 | tf_op jit(solution)/shard_map/ppermute | solution.py:54
  1181.4 59.5 %collective-permute-start.96 = (f32[128,2048]{1,0:T(8,128)}, f32[128,2048]{1,0:T(8,128)}, u32[]{:S(2)}, u32[]{:S(2)}) collective-permute-start(f32[128,2048]{1,0:T(8,128)} %get-tuple-element.642), channel_id=1, source_target_pairs={{0,2},{2,0},{1,3},{3,1},{4,6},{6,4},{5,7},{7,5}} | collective-permute-start | bytes 3145736 | tf_op jit(solution)/shard_map/ppermute | solution.py:54
  1236.8 47.5 %collective-permute-start.98 = (f32[128,2048]{1,0:T(8,128)}, f32[128,2048]{1,0:T(8,128)S(1)}, u32[]{:S(2)}, u32[]{:S(2)}) collective-permute-start(f32[128,2048]{1,0:T(8,128)} %get-tuple-element.648), channel_id=1, source_target_pairs={{0,2},{2,0},{1,3},{3,1},{4,6},{6,4},{5,7},{7,5}} | collective-permute-start | bytes 3145736 | tf_op jit(solution)/shard_map/ppermute | solution.py:54
  1238.8 45.5 %collective-permute-start.106 = (f32[128,2048]{1,0:T(8,128)S(1)}, f32[128,2048]{1,0:T(8,128)S(1)}, u32[]{:S(2)}, u32[]{:S(2)}) collective-permute-start(f32[128,2048]{1,0:T(8,128)S(1)} %copy-done.11), channel_id=1, source_target_pairs={{0,4},{4,0},{1,5},{5,1},{2,6},{6,2},{3,7},{7,3}} | collective-permute-start | bytes 3145736 | tf_op jit(solution)/shard_map/ppermute | solution.py:62
  1238.9 48.5 %collective-permute-start.110 = (f32[128,2048]{1,0:T(8,128)S(1)}, f32[128,2048]{1,0:T(8,128)S(1)}, u32[]{:S(2)}, u32[]{:S(2)}) collective-permute-start(f32[128,2048]{1,0:T(8,128)S(1)} %copy-done.1), channel_id=1, source_target_pairs={{0,4},{4,0},{1,5},{5,1},{2,6},{6,2},{3,7},{7,3}} | collective-permute-start | bytes 3145736 | tf_op jit(solution)/shard_map/ppermute | solution.py:62
  1251.4 86.3 %collective-permute-start.102 = (f32[128,2048]{1,0:T(8,128)S(1)}, f32[128,2048]{1,0:T(8,128)S(1)}, u32[]{:S(2)}, u32[]{:S(2)}) collective-permute-start(f32[128,2048]{1,0:T(8,128)S(1)} %get-tuple-element.652), channel_id=1, source_target_pairs={{0,4},{4,0},{1,5},{5,1},{2,6},{6,2},{3,7},{7,3}} | collective-permute-start | bytes 3145736 | tf_op jit(solution)/shard_map/ppermute | solution.py:62
  1263.0 69.2 %collective-permute-start.104 = (f32[2,512,128]{2,1,0:T(8,128)S(1)}, f32[2,512,128]{2,1,0:T(8,128)S(1)}, u32[]{:S(2)}, u32[]{:S(2)}) collective-permute-start(f32[2,512,128]{2,1,0:T(8,128)S(1)} %get-tuple-element.654), channel_id=1, source_target_pairs={{0,5},{1,4},{2,7},{3,6},{4,1},{5,0},{6,3},{7,2}} | collective-permute-start | bytes 1572872 | tf_op jit(solution)/shard_map/ppermute | solution.py:66
  1284.4 48.0 %collective-permute-start.105 = (f32[2,512,128]{2,1,0:T(8,128)S(1)}, f32[2,512,128]{2,1,0:T(8,128)S(1)}, u32[]{:S(2)}, u32[]{:S(2)}) collective-permute-start(f32[2,512,128]{2,1,0:T(8,128)S(1)} %get-tuple-element.654), channel_id=1, source_target_pairs={{0,1},{1,0},{2,3},{3,2},{4,5},{5,4},{6,7},{7,6}} | collective-permute-start | bytes 1572872 | tf_op jit(solution)/shard_map/ppermute | solution.py:50
  1284.4 47.9 %collective-permute-start.103 = (f32[2,512,128]{2,1,0:T(8,128)S(1)}, f32[2,512,128]{2,1,0:T(8,128)S(1)}, u32[]{:S(2)}, u32[]{:S(2)}) collective-permute-start(f32[2,512,128]{2,1,0:T(8,128)S(1)} %get-tuple-element.653), channel_id=1, source_target_pairs={{0,4},{4,0},{1,5},{5,1},{2,6},{6,2},{3,7},{7,3}} | collective-permute-start | bytes 1572872 | tf_op jit(solution)/shard_map/ppermute | solution.py:62
  1287.3 88.2 %collective-permute-start.97 = (f32[128,2048]{1,0:T(8,128)S(1)}, f32[128,2048]{1,0:T(8,128)S(1)}, u32[]{:S(2)}, u32[]{:S(2)}) collective-permute-start(f32[128,2048]{1,0:T(8,128)S(1)} %get-tuple-element.646), channel_id=1, source_target_pairs={{0,4},{4,0},{1,5},{5,1},{2,6},{6,2},{3,7},{7,3}} | collective-permute-start | bytes 3145736 | tf_op jit(solution)/shard_map/ppermute | solution.py:62
  (84 other events, 2407.3 us)
where the time goes:
time: 1390 us; the launch traced here: 1380 us
  waiting for transfers between devices  672 us (48%)
  Pallas kernels  537 us (39%)
  starting transfers between devices  81.8 us (6%)
  local copies, waits for them, and re-layouts  48.7 us (4%)
  loops' own time  14.9 us (1%)
    ppermute x21, waiting for transfers between devices, y_swap(): return lax.ppermute(v, 'replica', YSWAP)  461 us
    pallas_call x4, Pallas kernels, early_grads(): pl.pallas_call(kern, in_specs=[SM, SM] + [ANY] * (ns + 6) + [SM] * len(de...  223 us
    pallas_call x8, Pallas kernels, chunk_grads(): pl.pallas_call(kern, in_specs=[SM, SM] + [ANY] * (ns + 8 + len(deps)), ou...  222 us
    ppermute x22, waiting for transfers between devices, x_swap(): return lax.ppermute(v, 'fsdp', XSWAP)  154 us
    ppermute x21, starting transfers between devices, y_swap(): return lax.ppermute(v, 'replica', YSWAP)  50.2 us
    ppermute x3, waiting for transfers between devices, x_diag(): return lax.ppermute(v, 'fsdp', XDIAG)  46 us
  transfers between devices with their start and end apart: 70, of which 22 were waited for; matrix products, arithmetic and copies ran while one was open for 3% of the time, Pallas kernels for 35%

commit v1 on v0

--- a/solution.py
+++ b/solution.py
@@ -15,8 +15,9 @@
 NT = MICRO * REST // TM
 RROWS = MICRO * REST + TM
 FIRST = 3
-PIECES = (4, 4, 4, 2, 1)
+PIECES = (4, 4, 3, 2, 1, 1)
 SIZES = (5, 7, 8, 9, 10, 11, 12, 15)
+PARTS = ((0, 4), (0, 3, 4), (0, 2, 4), (0, 1, 4), (0, 1, 4, 5), (0, 1, 3, 4), (0, 1, 2, 4), (0, 1, 2, 3, 4, 5))
 G = 4
 M = G * TM
 FB = 256
@@ -26,7 +27,6 @@
 WSETS = ((0, 2), (2, 2), (4, 4))
 ORDER = (3, 4, 0, 5, 6, 1, 7, 2)
 LAG = 3
-OWN_ONLY = 3
 C1 = 0.7978845608028654
 C3 = 0.044715
 BF = jnp.bfloat16
@@ -142,13 +142,13 @@
                 loads.append(cp)
         zero[...] = jnp.zeros_like(zero)
         for k in range(MICRO):
-            n = rest_ref[k]
             for a in range(2):
                 loads[2 * k + a].wait()
-                for r in range(0, REST, TM):
-                    row = lax.broadcasted_iota(jnp.int32, (TM, D), 0) + r
-                    blk = buf[k, a, r : r + TM, :]
-                    buf[k, a, r : r + TM, :] = jnp.where(row < n, blk, jnp.zeros_like(blk))
+            n = rest_ref[k]
+            ragged = pl.multiple_of(jnp.minimum(n // 16 * 16, REST - 16), 16)
+            row = lax.broadcasted_iota(jnp.int32, (16, D), 0) + ragged
+            blk = buf[k, 1, pl.ds(ragged, 16), :]
+            buf[k, 1, pl.ds(ragged, 16), :] = jnp.where(row < n, blk, jnp.zeros_like(blk))
             o = pl.multiple_of(offs_ref[k], 16)
             cps = [
                 pltpu.make_async_copy(buf.at[k, a], out_ref.at[a, pl.ds(o, REST), :], osem.at[a]) for a in range(2)
@@ -305,19 +305,24 @@
     gu[...] += jnp.dot(dh, x, preferred_element_type=F32)
 
 
-def weight_copies(c, lo, f, w, wub, wdb, sem):
-    own, sib, fx, fd, wd_own, wd_oth = w
+def weight_copies(c, lo, at, w, wub, wdb, sem):
+    w_up, sib, fx, fd, w_down, wd_oth = w
+    y, f = at
+    xi, core = f // 2, f % 2
     cps = []
     c0, co = c * HB, (c - lo) * HB
     if not isinstance(c, int):
         c0, co = pl.multiple_of(c0, HB), pl.multiple_of(co, HB)
     for a in range(2):
-        for k, (ref, col) in enumerate(((own, c0), (sib, c0), (fx, co), (fd, co))):
+        xa = xi if a == 0 else 1 - xi
+        col = pl.multiple_of(((2 * xa + core) * 2 + y) * HALF + c0, HB)
+        parts = [w_up.at[:, pl.ds(col, HB)], sib.at[a, :, pl.ds(c0, HB)]]
+        parts += [ref.at[a, :, pl.ds(co, HB)] for ref in (fx, fd)]
+        for k, part in enumerate(parts):
             rows = pl.ds(pl.multiple_of((f ^ k) * 512, 512), 512)
-            cps.append(
-                pltpu.make_async_copy(ref.at[a, :, pl.ds(col, HB)], wub.at[rows, pl.ds(a * HB, HB)], sem.at[k, a])
-            )
-    cps.append(pltpu.make_async_copy(wd_own.at[pl.ds(c0, HB), :], wdb.at[pl.ds(0, HB), :], sem.at[4, 0]))
+            cps.append(pltpu.make_async_copy(part, wub.at[rows, pl.ds(a * HB, HB)], sem.at[k, a]))
+    own = pl.ds(pl.multiple_of(y * HALF + c0, HB), HB)
+    cps.append(pltpu.make_async_copy(w_down.at[own, :], wdb.at[pl.ds(0, HB), :], sem.at[4, 0]))
     cps.append(pltpu.make_async_copy(wd_oth.at[pl.ds(co, HB), :], wdb.at[pl.ds(HB, HB), :], sem.at[4, 1]))
     return cps
 
@@ -335,16 +340,43 @@
     ]
 
 
-def early_grads(tab, info, srcs, w, w_lo, lo_chunk, n_chunks, deps=()):
-    ns = len(srcs)
+def early_grads(tab, info, srcs, wsets, lo_chunk, n_new, prior=(), deps=()):
+    ns, nw, npr = len(srcs), len(wsets), len(prior)
+    sizes = [p[0].shape[0] for p in prior]
+    n_chunks = n_new + sum(sizes)
 
     def kern(tab_ref, info_ref, *refs):
-        src, wrefs, refs = refs[:ns], refs[ns : ns + 6], refs[ns + 6 + len(deps) :]
+        src, refs = refs[:ns], refs[ns:]
+        wrefs, refs = [refs[6 * k : 6 * k + 6] for k in range(nw)], refs[6 * nw :]
+        pri, refs = refs[: 2 * npr], refs[2 * npr + len(deps) :]
         out_d, out_u, xb, db, wub, wdb, gd, gu, sem, wsem, asem = refs
-        groups, f = info_ref[0], info_ref[1]
-
-        def weights(q, slot):
-            return weight_copies(lo_chunk + q, w_lo, f, wrefs, wub.at[slot], wdb.at[slot], wsem.at[slot])
+        hi, at = info_ref[1], (info_ref[2], info_ref[3])
+
+        def lo(q):
+            return jnp.where(q < n_new, 0, info_ref[0])
+
+        def weights(q, slot, act):
+            c = jnp.where(q < n_new, lo_chunk + q, q - n_new) if npr else lo_chunk + q
+
+            def act_all(k):
+                for cp in weight_copies(c, wsets[k][0], at, wrefs[k], wub.at[slot], wdb.at[slot], wsem.at[slot]):
+                    act(cp)
+
+            if nw == 1:
+                act_all(0)
+                return
+            for k in range(nw):
+                first, count, _ = wsets[k]
+
+                @pl.when(jnp.logical_and(c >= first, c < first + count))
+                def _():
+                    act_all(k)
+
+        def start_copy(cp):
+            cp.start()
+
+        def wait_copy(cp):
+            cp.wait()
 
         def results(q, slot):
             return (
@@ -352,41 +384,56 @@
                 pltpu.make_async_copy(gu.at[slot], out_u.at[q], asem.at[slot, 1]),
             )
 
-        issue_group(tab_ref, 0, 0, src, xb, db, sem)
-        for cp in weights(0, 0):
-            cp.start()
+        issue_group(tab_ref, lo(0), 0, src, xb, db, sem)
+        weights(0, 0, start_copy)
 
         def chunk(q, t):
             ws = lax.rem(q, 2)
 
             @pl.when(q + 1 < n_chunks)
             def _():
-                for cp in weights(q + 1, 1 - ws):
-                    cp.start()
+                weights(q + 1, 1 - ws, start_copy)
 
             @pl.when(q >= 2)
             def _():
                 for cp in results(q - 2, ws):
                     cp.wait()
 
-            gd[ws] = jnp.zeros((FB, D), F32)
-            gu[ws] = jnp.zeros((FB, D), F32)
-            for cp in weights(q, ws):
-                cp.wait()
+            @pl.when(q < n_new)
+            def _():
+                gd[ws] = jnp.zeros((FB, D), F32)
+                gu[ws] = jnp.zeros((FB, D), F32)
+
+            base = n_new
+            for k in range(npr):
+                first, base = base, base + sizes[k]
+
+                @pl.when(jnp.logical_and(q >= first, q < base))
+                def _():
+                    cps = (
+                        pltpu.make_async_copy(pri[2 * k].at[q - first], gd.at[ws], asem.at[ws, 0]),
+                        pltpu.make_async_copy(pri[2 * k + 1].at[q - first], gu.at[ws], asem.at[ws, 1]),
+                    )
+                    for cp in cps:
+                        cp.start()
+                    for cp in cps:
+                        cp.wait()
+
+            weights(q, ws, wait_copy)
 
             def group(g, t):
                 slot = lax.rem(t, 2)
-                last = g + 1 == groups
+                last = g + 1 == hi
 
                 @pl.when(jnp.logical_or(jnp.logical_not(last), q + 1 < n_chunks))
                 def _():
-                    issue_group(tab_ref, jnp.where(last, 0, g + 1), 1 - slot, src, xb, db, sem)
+                    issue_group(tab_ref, jnp.where(last, lo(q + 1), g + 1), 1 - slot, src, xb, db, sem)
 
                 wait_group(slot, xb, db, sem)
                 add_group(xb[slot], db[slot], wub.at[ws], wdb.at[ws], gd.at[ws], gu.at[ws])
                 return t + 1
 
-            t = lax.fori_loop(0, groups, group, t)
+            t = lax.fori_loop(lo(q), hi, group, t)
             for cp in results(q, ws):
                 cp.start()
             return t
@@ -396,32 +443,36 @@
             for cp in results(q, q % 2):
                 cp.wait()
 
+    flat = [a for _, _, w in wsets for a in w]
+    pri = [a for p in prior for a in p]
     return pl.pallas_call(
         kern,
-        in_specs=[SM, SM] + [ANY] * (ns + 6) + [SM] * len(deps),
+        in_specs=[SM, SM] + [ANY] * (ns + len(flat) + len(pri)) + [SM] * len(deps),
         out_specs=[ANY] * 2,
         out_shape=[jax.ShapeDtypeStruct((n_chunks, FB, D), F32)] * 2,
         scratch_shapes=gather_scratch(2) + [pltpu.SemaphoreType.DMA((2, 2))],
         compiler_params=pltpu.CompilerParams(vmem_limit_bytes=GRANT),
-        cost_estimate=cost(8 * 5632 * D * FB * n_chunks, 60_000_000 * n_chunks),
-    )(tab, info, *srcs, *w, *deps)
-
-
-def chunk_grads(j, w_lo, tab, info, skip, srcs, w, prior, at, deps):
+        cost_estimate=cost(8 * 5632 * D * FB * n_new, 60_000_000 * n_new),
+    )(tab, info, *srcs, *flat, *pri, *deps)
+
+
+def chunk_grads(j, tab, info, srcs, wset, prior, at, deps):
     ns = len(srcs)
+    w_lo, _, w = wset
 
     def kern(tab_ref, info_ref, *refs):
         src, refs = refs[:ns], refs[ns:]
         wrefs, (pd, pu), refs = refs[:6], refs[6:8], refs[8 + len(deps) :]
         keep_d, send_d, keep_u, send_u, xb, db, wub, wdb, gd, gu, sem, wsem, osem = refs
-        groups, xi, f = info_ref[0], info_ref[1], info_ref[2]
+        groups, y, f = info_ref[0], info_ref[1], info_ref[2]
+        xi = f // 2
         wub, wdb, gd, gu = wub.at[0], wdb.at[0], gd.at[0], gu.at[0]
 
-        @pl.when(groups > skip)
+        @pl.when(groups > 0)
         def _():
-            issue_group(tab_ref, skip, 0, src, xb, db, sem)
-
-        cps = weight_copies(j, w_lo, f, wrefs, wub, wdb, wsem.at[0])
+            issue_group(tab_ref, 0, 0, src, xb, db, sem)
+
+        cps = weight_copies(j, w_lo, (y, f), wrefs, wub, wdb, wsem.at[0])
         cps.append(pltpu.make_async_copy(pd.at[at], gd, osem.at[0]))
         cps.append(pltpu.make_async_copy(pu.at[at], gu, osem.at[1]))
         for cp in cps:
@@ -430,7 +481,7 @@
             cp.wait()
 
         def body(g, _):
-            slot = lax.rem(g - skip, 2)
+            slot = lax.rem(g, 2)
 
             @pl.when(g + 1 < groups)
             def _():
@@ -440,7 +491,7 @@
             add_group(xb[slot], db[slot], wub, wdb, gd, gu)
             return 0
 
-        lax.fori_loop(skip, groups, body, 0)
+        lax.fori_loop(0, groups, body, 0)
         kc = pl.multiple_of(xi * HALF, HALF)
         sc = pl.multiple_of((1 - xi) * HALF, HALF)
         ocp = [(gd.at[pl.ds(HB, HB), :], send_d), (gd.at[pl.ds(0, HB), :], keep_d)]
@@ -490,7 +541,7 @@
         out_shape=[jax.ShapeDtypeStruct((D, D), F32), jax.ShapeDtypeStruct((HB, D), F32)],
         scratch_shapes=[pltpu.VMEM((HB, D), F32), pltpu.SemaphoreType.DMA((2,))],
         input_output_aliases={} if first else {3: 0},
-        compiler_params=pltpu.CompilerParams(vmem_limit_bytes=16 * MIB),
+        compiler_params=pltpu.CompilerParams(vmem_limit_bytes=GRANT),
         cost_estimate=cost(2_000_000_000, 4_000_000),
     )(pos, keep, recv, *extra)
 
@@ -530,7 +581,7 @@
         ],
         scratch_shapes=[pltpu.VMEM((2, HALF, HB), F32), pltpu.SemaphoreType.DMA((4,))],
         input_output_aliases={} if first else {3: 0},
-        compiler_params=pltpu.CompilerParams(vmem_limit_bytes=16 * MIB),
+        compiler_params=pltpu.CompilerParams(vmem_limit_bytes=GRANT),
         cost_estimate=cost(2_000_000_000, 4_000_000),
     )(pos, keep, recv, *extra)
 
@@ -581,22 +632,32 @@
     return pl.pallas_call(lambda o: None, out_specs=ANY, out_shape=jax.ShapeDtypeStruct((2, k * TM, D), BF))()
 
 
-def present(n):
-    return (n >= 4, n >= 8, n >= 12, n % 4 >= 2, n % 2 == 1)
-
-
-def exchange_branch(n, early):
+def exchange_branch(parts, early):
+    here = [k in parts for k in range(len(PIECES))]
+
     def run(pieces, *rest):
         got = []
-        for k, here in enumerate(present(n)):
-            got.append(y_swap(pieces[k]) if here else nothing(PIECES[k]))
+        for k in range(len(PIECES)):
+            got.append(y_swap(pieces[k]) if here[k] else nothing(PIECES[k]))
         acc = early(*rest)
         sib = []
-        for k, here in enumerate(present(n)):
-            sib.append(core_swap(got[k]) if here else nothing(PIECES[k]))
+        for k in range(len(PIECES)):
+            sib.append(core_swap(got[k]) if here[k] else nothing(PIECES[k]))
         return (*got, *sib, *acc)
 
     return run
+
+
+def piece_starts():
+    table = []
+    for size, parts in zip(SIZES, PARTS):
+        at, row = FIRST, []
+        for k in range(len(PIECES)):
+            row.append(at)
+            at += PIECES[k] if k in parts else 0
+        assert at == FIRST + size
+        table.append(row)
+    return table
 
 
 def solution(mesh):
@@ -621,15 +682,13 @@
             oth = lax.dynamic_slice(w_up, (0, ((2 * (1 - xd) + cd) * 2 + y) * HALF + lo), (512, n))
             return jnp.stack([own, oth])
 
-        wd_own = lax.dynamic_slice(w_down, (y * HALF, 0), (HALF, D))
         from_s = core_swap(cols(xi, 1 - c))
-        mine = cols(xi, c)
         wsets = []
         for lo, n in WSETS:
             a = x_swap(cols(1 - xi, c, lo * HB, n * HB))
             b = x_diag(cols(1 - xi, 1 - c, lo * HB, n * HB))
             d = x_swap(lax.dynamic_slice(w_down, (y * HALF + lo * HB, 0), (n * HB, D)))
-            wsets.append((mine, from_s, a, b, wd_own, d))
+            wsets.append((lo, n, [w_up, from_s, a, b, w_down, d]))
 
         rest = lens - BASE
         r16 = (rest + 15) // 16 * 16
@@ -640,7 +699,7 @@
         both = tiles[0::2] + tiles[1::2]
         share = jnp.stack([(both + 1) // 2, both // 2], axis=1).reshape(8)
         which = jnp.sum(jnp.max(share) - FIRST > jnp.array(SIZES[:-1]))
-        more = jnp.array(SIZES)[which]
+        starts = jnp.array(piece_starts())[which]
 
         def at(v, i):
             return lax.dynamic_index_in_dim(v, i, keepdims=False)
@@ -648,14 +707,12 @@
         t_own, t_sib = at(tiles, me), at(tiles, me ^ 1)
         h_own = at(share, me)
         h_y, h_ys = at(share, me ^ 4), at(share, me ^ 5)
-        at_f = [FIRST + 4 * jnp.minimum(more // 4, k) for k in range(4)]
-        at_one = at_f[3] + more % 4 // 2 * 2
-        starts = [at_f[0], at_f[1], at_f[2], at_f[3], at_one]
-
         packed = pack_rest(x_in, dy, my_rest, offs)
         packed_s = core_swap(packed)
         s1_s = core_swap(s1)
-        pa, *pieces = build_send(packed, packed_s, jnp.stack([h_own, t_own, t_sib - h_own, *starts]).astype(jnp.int32))
+        pa, *pieces = build_send(
+            packed, packed_s, jnp.concatenate([jnp.stack([h_own, t_own, t_sib - h_own]), starts]).astype(jnp.int32)
+        )
         qa = y_swap(pa)
 
         i = jnp.arange(64)
@@ -666,40 +723,41 @@
         tab = jnp.where(i < 12 + t_own, 2 * 32 + i - 12, tab)
         tab = jnp.where(i < 12, (i // 6) * 32 + i % 6, tab)
         tab = jnp.where((k >= 0) & (k < 12), (4 + k // 6) * 32 + k % 6, tab).astype(jnp.int32)
-        info_own = jnp.stack([g_own, f]).astype(jnp.int32)
-        info_all = jnp.stack([g_own + 3, f]).astype(jnp.int32)
-
-        i = jnp.arange(56) - 12
+        info_own = jnp.stack([0, g_own, y, f]).astype(jnp.int32)
+        info_all = jnp.stack([g_own, g_own + 3, y, f]).astype(jnp.int32)
+
+        i = jnp.arange(40)
         own_list = i < h_y
         t = jnp.where(own_list, i, i - h_y)
-        late = 2 * 32 + t
-        for n, lo in enumerate(starts):
-            late = jnp.where(t >= lo, (3 + n) * 32 + t - lo, late)
-        late = jnp.where(own_list, late, late + 6 * 32)
-        late = jnp.where(i < h_y + h_ys, late, 14 * 32 + NT)
-        late = jnp.where(i < 0, (i + 12) // 6 * 32 + (i + 12) % 6, late).astype(jnp.int32)
-        info_late = jnp.stack([3 + (h_y + h_ys + G - 1) // G, xi, f]).astype(jnp.int32)
+        late = t
+        for n in range(len(PIECES)):
+            late = jnp.where(t >= starts[n], (1 + n) * 32 + t - starts[n], late)
+        late = jnp.where(own_list, late, late + (1 + len(PIECES)) * 32)
+        late = jnp.where(i < h_y + h_ys, late, 2 * (1 + len(PIECES)) * 32 + NT).astype(jnp.int32)
+        info_late = jnp.stack([(h_y + h_ys + G - 1) // G, y, f]).astype(jnp.int32)
         pos = jnp.stack([y, xi, c]).astype(jnp.int32)
 
         own_srcs = (s1, s1_s, packed, packed_s)
-        acc0 = early_grads(tab, info_own, own_srcs, wsets[0], 0, 0, 2)
-        acc1 = early_grads(tab, info_own, own_srcs, wsets[1], 2, 2, 1, (late, info_late, pos))
+        acc0 = early_grads(tab, info_own, own_srcs, wsets[:1], 0, 2)
+        acc1 = early_grads(tab, info_own, own_srcs, wsets[1:2], 2, 1, (), (late, info_late, pos))
         s1_ys = core_swap(s1_y)
         srcs = (*own_srcs, s1_y, s1_ys)
-        acc2 = early_grads(tab, info_all, srcs, wsets[1], 2, 3, 1)
-
-        def early(tab, info, srcs, w):
-            return early_grads(tab, info, srcs, w, 4, 4, 4)
+        acc2 = early_grads(tab, info_all, srcs, wsets[1:2], 3, 1)
+
+        def early(tab, info, srcs, w, prior):
+            sets = [(lo, n, v) for (lo, n), v in zip(WSETS, w)]
+            return early_grads(tab, info, srcs, sets, 4, 4, prior)
 
         got = lax.switch(
             which,
-            [exchange_branch(n, early) for n in SIZES],
-            pieces, tab, info_all, srcs, list(wsets[2]),
+            [exchange_branch(parts, early) for parts in PARTS],
+            pieces, tab, info_all, srcs, [w for _, _, w in wsets], [list(acc0), list(acc1)],
         )
-        pieces, sib_pieces, acc3 = got[:5], got[5:10], got[10:]
+        k = len(PIECES)
+        pieces, sib_pieces, acc3 = got[:k], got[k : 2 * k], got[2 * k :]
         qas = core_swap(qa)
-        srcs = (s1_y, s1_ys, qa, *pieces, qas, *sib_pieces, packed)
-        prior = [(acc0, 0), (acc0, 1), (acc1, 0), (acc2, 0), *((acc3, k) for k in range(4))]
+        srcs = (qa, *pieces, qas, *sib_pieces, packed)
+        prior = [(acc3, 4), (acc3, 5), (acc3, 6), (acc2, 0), *((acc3, k) for k in range(4))]
 
         out_d = out_u = None
         fin = []
@@ -707,7 +765,7 @@
             deps = (fin[p - 2][0],) if p >= 2 else ()
             w_at = next(h for h, (lo, n) in enumerate(WSETS) if lo <= j < lo + n)
             keep_d, send_d, keep_u, send_u = chunk_grads(
-                j, WSETS[w_at][0], late, info_late, 0 if j < OWN_ONLY else 3, srcs, wsets[w_at], *prior[j], deps
+                j, late, info_late, srcs, wsets[w_at], *prior[j], deps
             )
             recv_d = x_swap(send_d)
             recv_u = x_swap(send_u)

time: 1390 us -> 1390 us (level)
  local copies, waits for them, and re-layouts: 48.7 us -> 24.4 us
  Pallas kernels: 537 us -> 561 us
    ppermute x22, waiting for transfers between devices: 154 us -> 202 us  [x_swap(): return lax.ppermute(v, 'fsdp', XSWAP)]
    ppermute x3, waiting for transfers between devices: 46 us -> 5.7 us  [x_diag(): return lax.ppermute(v, 'fsdp', XDIAG)]
    pallas_call x4, Pallas kernels: 223 us -> 259 us  [early_grads(): pl.pallas_call(kern, in_specs=[SM, SM] + [ANY] * (ns + len(flat) + len(pr...]
    pallas_call x8, Pallas kernels: 222 us -> 197 us  [chunk_grads(): pl.pallas_call(kern, in_specs=[SM, SM] + [ANY] * (ns + 8 + len(deps)), ou...]
    unnamed x125 -> x69, local copies, waits for them, and re-layouts: 23.4 us -> 7.39 us
    ppermute x21 -> x22, starting transfers between devices: 50.2 us -> 48 us  [y_swap(): return lax.ppermute(v, 'replica', YSWAP)]
    ppermute x21 -> x22, waiting for transfers between devices: 461 us -> 459 us  [y_swap(): return lax.ppermute(v, 'replica', YSWAP)]
  transfers between devices with their start and end apart: 70 -> 72, of which waited for: 22 -> 23; matrix products, arithmetic and copies ran while one was open for 3% -> 2% of each run, Pallas kernels for 35% -> 37%
where the time goes in v1:
time: 1390 us; the launch traced here: 1380 us
  waiting for transfers between devices  677 us (49%)
  Pallas kernels  561 us (40%)
  starting transfers between devices  70.6 us (5%)
  local copies, waits for them, and re-layouts  24.4 us (2%)
  other arithmetic  19.8 us (1%)
  loops' own time  16.8 us (1%)
    ppermute x22, waiting for transfers between devices, y_swap(): return lax.ppermute(v, 'replica', YSWAP)  459 us
    pallas_call x4, Pallas kernels, early_grads(): pl.pallas_call(kern, in_specs=[SM, SM] + [ANY] * (ns + len(flat) + len(pr...  259 us
    ppermute x22, waiting for transfers between devices, x_swap(): return lax.ppermute(v, 'fsdp', XSWAP)  202 us
    pallas_call x8, Pallas kernels, chunk_grads(): pl.pallas_call(kern, in_specs=[SM, SM] + [ANY] * (ns + 8 + len(deps)), ou...  197 us
    ppermute x22, starting transfers between devices, y_swap(): return lax.ppermute(v, 'replica', YSWAP)  48 us
  transfers between devices with their start and end apart: 72, of which 23 were waited for; matrix products, arithmetic and copies ran while one was open for 2% of the time, Pallas kernels for 37%

profile of v1, /device:TPU:0, one launch (start us, length us, event | category | flops | bytes accessed | tf_op | source)
XLA Modules:
  0.0 1378.6 jit_solution(16811936948604690741)
XLA Ops:
  2.0 8.3 start.1
  13.4 16.4 %pack_rest.1.own_ref.refs_2_.refs_14_ = bf16[2,2432,2048]{2,1,0:T(8,128)(2,1)} custom-call(s32[3]{0:T(128)} %fusion.3.rest_ref, s32[4]{0:T(128)} %pad_add_fusion.2.offs_ref, bf16[3,1024,2048]{2,1,0:T(8,128)(2,1)} %x_ref.3, bf16[3,1024,2048]{2,1,0:T(8,128)(2,1)} %d_ref.3), custom_call_target="tpu_custom_call" | custom-call | flops 15000000512 | bytes 50000000 | tf_op jit(solution)/shard_map/pack_rest/pallas_call | solution.py:167
  61.2 5.7 collective-permute-done.65.refs_7_.refs_18_
  68.4 5.1 compare_select_fusion.12.refs_10_.tab_ref
  79.1 3.2 dynamic-slice_bitcast_fusion
  82.3 9.9 collective-permute-done.66.refs_9_.refs_20_
  94.6 73.5 %collective-permute-done.61.refs_4_ = bf16[2,768,2048]{2,1,0:T(8,128)(2,1)} collective-permute-done((bf16[2,768,2048]{2,1,0:T(8,128)(2,1)}, bf16[2,768,2048]{2,1,0:T(8,128)(2,1)}, u32[]{:S(2)}, u32[]{:S(2)}) %collective-permute-start.61) | collective-permute-done | bytes 6291488 | tf_op jit(solution)/shard_map/ppermute | solution.py:62
  169.2 45.9 %shard_map.86 = (f32[2,256,2048]{2,1,0:T(8,128)}, f32[2,256,2048]{2,1,0:T(8,128)}) custom-call(s32[64]{0:T(128)S(1)} %and_select_fusion.4.tab_ref, s32[4]{0:T(128)} %fusion.10.info_ref, bf16[2,768,2048]{2,1,0:T(8,128)(2,1)} %bitcast.100, bf16[2,768,2048]{2,1,0:T(8,128)(2,1)} %collective-permute-done.60.refs_1_, ...), custom_call_target="tpu_custom_call" | custom-call | flops 47244640256 | bytes 120000000 | tf_op jit(solution)/shard_map/pallas_call | solution.py:448
  217.3 25.1 %shard_map.87 = (f32[1,256,2048]{2,1,0:T(8,128)}, f32[1,256,2048]{2,1,0:T(8,128)}) custom-call(s32[64]{0:T(128)S(1)} %and_select_fusion.4.tab_ref, s32[4]{0:T(128)} %fusion.10.info_ref, bf16[2,768,2048]{2,1,0:T(8,128)(2,1)} %bitcast.101, bf16[2,768,2048]{2,1,0:T(8,128)(2,1)} %collective-permute-done.60.refs_1_, ...), custom_call_target="tpu_custom_call" | custom-call | flops 23622320128 | bytes 60000000 | tf_op jit(solution)/shard_map/pallas_call | solution.py:448
  242.4 9.1 build_send.1
  251.5 34.4 %collective-permute-done.72.refs_20_ = bf16[512,2048]{1,0:T(8,128)(2,1)} collective-permute-done((bf16[512,2048]{1,0:T(8,128)(2,1)}, bf16[512,2048]{1,0:T(8,128)(2,1)}, u32[]{:S(2)}, u32[]{:S(2)}) %collective-permute-start.72) | collective-permute-done | bytes 2097184 | tf_op jit(solution)/shard_map/ppermute | solution.py:54
  285.9 408.7 %conditional.1 = (bf16[2,512,2048]{2,1,0:T(8,128)(2,1)}, bf16[2,512,2048]{2,1,0:T(8,128)(2,1)}, bf16[2,384,2048]{2,1,0:T(8,128)(2,1)}, bf16[2,256,2048]{2,1,0:T(...) conditional(s32[]{:T(128)} %clamp.3, ...), branch_computations={%region_5.6_spmd, %region_6.7_spmd, %region_7.8_spmd, %region_8.9_... | conditional | flops 94489280512 | bytes 365829696 | solution.py:751
  293.9 11.4 collective-permute-start.22
  307.3 202.0 %collective-permute-done.24 = bf16[2,128,2048]{2,1,0:T(8,128)(2,1)} collective-permute-done((bf16[2,128,2048]{2,1,0:T(8,128)(2,1)}, bf16[2,128,2048]{2,1,0:T(8,128)(2,1)}, u32[]{:S(2)}, u32[]{:S(2)}) %collective-permute-start.24) | collective-permute-done | bytes 1048608 | tf_op jit(solution)/shard_map/cond/branch_4_fun/ppermute | solution.py:62
  509.3 21.2 %collective-permute-done.25 = bf16[2,128,2048]{2,1,0:T(8,128)(2,1)} collective-permute-done((bf16[2,128,2048]{2,1,0:T(8,128)(2,1)}, bf16[2,128,2048]{2,1,0:T(8,128)(2,1)}, u32[]{:S(2)}, u32[]{:S(2)}) %collective-permute-start.25) | collective-permute-done | bytes 1048608 | tf_op jit(solution)/shard_map/cond/branch_4_fun/ppermute | solution.py:62
  531.1 154.7 %branch_4_fun.9 = (f32[7,256,2048]{2,1,0:T(8,128)}, f32[7,256,2048]{2,1,0:T(8,128)}) custom-call(s32[64]{0:T(128)S(1)} %get-tuple-element.573.tab_ref, s32[4]{0:T(128)S(1)} %get-tuple-element.574.info_ref, bf16[2,768,2048]{2,1,0:T(8,128)(2,1)} %get-tuple-element.575.refs_0_, bf16[2,768,2048]{2,1,0:T(8,128)(2,1)} %get-tuple-element.576.refs_1_, ...), custom_call_target="tpu_custom_call" | custom-call | flops 94489280512 | bytes 240000000 | tf_op jit(solution)/shard_map/cond/branch_4_fun/pallas_call | solution.py:448
  694.6 21.7 %collective-permute-start.59 = (bf16[2,384,2048]{2,1,0:T(8,128)(2,1)}, bf16[2,384,2048]{2,1,0:T(8,128)(2,1)S(1)}, u32[]{:S(2)}, u32[]{:S(2)}) collective-permute-start(bf16[2,384,2048]{2,1,0:T(8,128)(2,1)} %get-tuple-element.811), channel_id=1, source_target_pairs={{0,4},{4,0},{1,5},{5,1},{2,6},{6,2},{3,7},{7,3}} | collective-permute-start | bytes 9437192 | tf_op jit(solution)/shard_map/ppermute | solution.py:62
  716.3 69.0 %collective-permute-done.59.refs_0_ = bf16[2,384,2048]{2,1,0:T(8,128)(2,1)S(1)} collective-permute-done((bf16[2,384,2048]{2,1,0:T(8,128)(2,1)}, bf16[2,384,2048]{2,1,0:T(8,128)(2,1)S(1)}, u32[]{:S(2)}, u32[]{:S(2)}) %collective-permute-start.59) | collective-permute-done | bytes 3145760 | tf_op jit(solution)/shard_map/ppermute | solution.py:62
  785.3 33.2 %shard_map.89 = (f32[1,256,2048]{2,1,0:T(8,128)}, f32[1,256,2048]{2,1,0:T(8,128)}) custom-call(s32[64]{0:T(128)S(1)} %and_select_fusion.4.tab_ref, s32[4]{0:T(128)S(1)} %add_add_fusion.info_ref, bf16[2,768,2048]{2,1,0:T(8,128)(2,1)} %bitcast.110, bf16[2,768,2048]{2,1,0:T(8,128)(2,1)} %collective-permute-done.60.refs_1_, ...), custom_call_target="tpu_custom_call" | custom-call | flops 23622320128 | bytes 60000000 | tf_op jit(solution)/shard_map/pallas_call | solution.py:448
  818.5 24.8 %shard_map.90 = (f32[128,2048]{1,0:T(8,128)}, f32[128,2048]{1,0:T(8,128)}, f32[128,2048]{1,0:T(8,128)}, f32[128,2048]{1,0:T(8,128)}) custom-call(s32[40]{0:T(128)} %compare_select_fusion.12.refs_10_.tab_ref, s32[3]{0:T(128)} %pad_add_fusion.4.refs_11_.info_ref, bf16[2,384,2048]{2,1,0:T(8,128)(2,1)} %copy-done.17, ...), custom_call_target="tpu_custom_call" | custom-call | flops 12884901888 | bytes 40000000 | tf_op jit(solution)/shard_map/pallas_call | solution.py:508
  843.4 24.5 %shard_map.88 = (f32[128,2048]{1,0:T(8,128)}, f32[128,2048]{1,0:T(8,128)}, f32[128,2048]{1,0:T(8,128)}, f32[128,2048]{1,0:T(8,128)}) custom-call(s32[40]{0:T(128)} %compare_select_fusion.12.refs_10_.tab_ref, s32[3]{0:T(128)} %pad_add_fusion.4.refs_11_.info_ref, bf16[2,384,2048]{2,1,0:T(8,128)(2,1)} %copy-done.17, ...), custom_call_target="tpu_custom_call" | custom-call | flops 12884901888 | bytes 40000000 | tf_op jit(solution)/shard_map/pallas_call | solution.py:508
  873.0 24.5 %shard_map.94 = (f32[128,2048]{1,0:T(8,128)}, f32[128,2048]{1,0:T(8,128)}, f32[128,2048]{1,0:T(8,128)}, f32[128,2048]{1,0:T(8,128)}) custom-call(s32[40]{0:T(128)} %compare_select_fusion.12.refs_10_.tab_ref, s32[3]{0:T(128)} %pad_add_fusion.4.refs_11_.info_ref, bf16[2,384,2048]{2,1,0:T(8,128)(2,1)} %copy-done.17, ...), custom_call_target="tpu_custom_call" | custom-call | flops 12884901888 | bytes 40000000 | tf_op jit(solution)/shard_map/pallas_call | solution.py:508
  900.6 24.5 %shard_map.93 = (f32[128,2048]{1,0:T(8,128)}, f32[128,2048]{1,0:T(8,128)}, f32[128,2048]{1,0:T(8,128)}, f32[128,2048]{1,0:T(8,128)}) custom-call(s32[40]{0:T(128)} %compare_select_fusion.12.refs_10_.tab_ref, s32[3]{0:T(128)} %pad_add_fusion.4.refs_11_.info_ref, bf16[2,384,2048]{2,1,0:T(8,128)(2,1)} %copy-done.17, ...), custom_call_target="tpu_custom_call" | custom-call | flops 12884901888 | bytes 40000000 | tf_op jit(solution)/shard_map/pallas_call | solution.py:508
  925.2 14.1 %collective-permute-done.81.rc = f32[128,2048]{1,0:T(8,128)} collective-permute-done((f32[128,2048]{1,0:T(8,128)}, f32[128,2048]{1,0:T(8,128)}, u32[]{:S(2)}, u32[]{:S(2)}) %collective-permute-start.81) | collective-permute-done | bytes 1048608 | tf_op jit(solution)/shard_map/ppermute | solution.py:54
  942.3 3.1 shard_map.99
  947.6 14.2 %collective-permute-done.77.rc = f32[128,2048]{1,0:T(8,128)} collective-permute-done((f32[128,2048]{1,0:T(8,128)}, f32[128,2048]{1,0:T(8,128)}, u32[]{:S(2)}, u32[]{:S(2)}) %collective-permute-start.77) | collective-permute-done | bytes 1048608 | tf_op jit(solution)/shard_map/ppermute | solution.py:54
  964.8 18.4 %collective-permute-done.76.rc = f32[128,2048]{1,0:T(8,128)S(1)} collective-permute-done((f32[128,2048]{1,0:T(8,128)}, f32[128,2048]{1,0:T(8,128)S(1)}, u32[]{:S(2)}, u32[]{:S(2)}) %collective-permute-start.76) | collective-permute-done | bytes 1048608 | tf_op jit(solution)/shard_map/ppermute | solution.py:54
  983.2 24.6 %shard_map.100 = (f32[128,2048]{1,0:T(8,128)}, f32[128,2048]{1,0:T(8,128)}, f32[128,2048]{1,0:T(8,128)}, f32[128,2048]{1,0:T(8,128)}) custom-call(s32[40]{0:T(128)} %compare_select_fusion.12.refs_10_.tab_ref, s32[3]{0:T(128)} %pad_add_fusion.4.refs_11_.info_ref, bf16[2,384,2048]{2,1,0:T(8,128)(2,1)} %copy-done.17, ...), custom_call_target="tpu_custom_call" | custom-call | flops 12884901888 | bytes 40000000 | tf_op jit(solution)/shard_map/pallas_call | solution.py:508
  1015.7 24.6 %shard_map.97 = (f32[128,2048]{1,0:T(8,128)}, f32[128,2048]{1,0:T(8,128)}, f32[128,2048]{1,0:T(8,128)}, f32[128,2048]{1,0:T(8,128)}) custom-call(s32[40]{0:T(128)} %compare_select_fusion.12.refs_10_.tab_ref, s32[3]{0:T(128)} %pad_add_fusion.4.refs_11_.info_ref, bf16[2,384,2048]{2,1,0:T(8,128)(2,1)} %copy-done.17, ...), custom_call_target="tpu_custom_call" | custom-call | flops 12884901888 | bytes 40000000 | tf_op jit(solution)/shard_map/pallas_call | solution.py:508
  1040.3 22.1 %collective-permute-done.91.rc = f32[128,2048]{1,0:T(8,128)} collective-permute-done((f32[128,2048]{1,0:T(8,128)}, f32[128,2048]{1,0:T(8,128)}, u32[]{:S(2)}, u32[]{:S(2)}) %collective-permute-start.91) | collective-permute-done | bytes 1048608 | tf_op jit(solution)/shard_map/ppermute | solution.py:54
  1065.5 3.1 shard_map.102
  1068.7 16.3 %collective-permute-done.85.rc = f32[128,2048]{1,0:T(8,128)} collective-permute-done((f32[128,2048]{1,0:T(8,128)}, f32[128,2048]{1,0:T(8,128)}, u32[]{:S(2)}, u32[]{:S(2)}) %collective-permute-start.85) | collective-permute-done | bytes 1048608 | tf_op jit(solution)/shard_map/ppermute | solution.py:54
  1086.0 3.2 shard_map.103
  1092.3 15.1 %collective-permute-done.92.rc = f32[128,2048]{1,0:T(8,128)} collective-permute-done((f32[128,2048]{1,0:T(8,128)}, f32[128,2048]{1,0:T(8,128)}, u32[]{:S(2)}, u32[]{:S(2)}) %collective-permute-start.92) | collective-permute-done | bytes 1048608 | tf_op jit(solution)/shard_map/ppermute | solution.py:54
  1107.4 22.4 %collective-permute-done.103.rc = f32[128,2048]{1,0:T(8,128)} collective-permute-done((f32[128,2048]{1,0:T(8,128)}, f32[128,2048]{1,0:T(8,128)}, u32[]{:S(2)}, u32[]{:S(2)}) %collective-permute-start.103) | collective-permute-done | bytes 1048608 | tf_op jit(solution)/shard_map/ppermute | solution.py:54
  1144.6 5.4 collective-permute-done.78.rc
  1150.0 24.6 %shard_map.109 = (f32[128,2048]{1,0:T(8,128)}, f32[128,2048]{1,0:T(8,128)}, f32[128,2048]{1,0:T(8,128)}, f32[128,2048]{1,0:T(8,128)}) custom-call(s32[40]{0:T(128)} %compare_select_fusion.12.refs_10_.tab_ref, s32[3]{0:T(128)} %pad_add_fusion.4.refs_11_.info_ref, bf16[2,384,2048]{2,1,0:T(8,128)(2,1)} %copy-done.17, ...), custom_call_target="tpu_custom_call" | custom-call | flops 12884901888 | bytes 40000000 | tf_op jit(solution)/shard_map/pallas_call | solution.py:508
  1178.0 10.9 collective-permute-done.99.d_ref
  1188.9 11.2 collective-permute-done.115.uc_ref
  1200.1 10.1 collective-permute-done.116.uy_ref
  1210.8 24.7 %shard_map.108 = (f32[128,2048]{1,0:T(8,128)}, f32[128,2048]{1,0:T(8,128)}, f32[128,2048]{1,0:T(8,128)}, f32[128,2048]{1,0:T(8,128)}) custom-call(s32[40]{0:T(128)} %compare_select_fusion.12.refs_10_.tab_ref, s32[3]{0:T(128)} %pad_add_fusion.4.refs_11_.info_ref, bf16[2,384,2048]{2,1,0:T(8,128)(2,1)} %copy-done.17, ...), custom_call_target="tpu_custom_call" | custom-call | flops 12884901888 | bytes 40000000 | tf_op jit(solution)/shard_map/pallas_call | solution.py:508
  1240.4 3.3 shard_map.111
  1254.5 6.5 collective-permute-done.93.rc
  1260.9 22.5 %collective-permute-done.106.rc = f32[128,2048]{1,0:T(8,128)} collective-permute-done((f32[128,2048]{1,0:T(8,128)}, f32[128,2048]{1,0:T(8,128)}, u32[]{:S(2)}, u32[]{:S(2)}) %collective-permute-start.106) | collective-permute-done | bytes 1048608 | tf_op jit(solution)/shard_map/ppermute | solution.py:54
  1292.6 3.4 shard_map.117
  1296.0 34.9 %collective-permute-done.111.uc_ref = f32[2,512,128]{2,1,0:T(8,128)} collective-permute-done((f32[2,512,128]{2,1,0:T(8,128)}, f32[2,512,128]{2,1,0:T(8,128)}, u32[]{:S(2)}, u32[]{:S(2)}) %collective-permute-start.111) | collective-permute-done | bytes 524320 | tf_op jit(solution)/shard_map/ppermute | solution.py:62
  1336.4 3.2 shard_map.119
  1339.5 36.2 %collective-permute-done.107.uc_ref = f32[2,512,128]{2,1,0:T(8,128)S(1)} collective-permute-done((f32[2,512,128]{2,1,0:T(8,128)S(1)}, f32[2,512,128]{2,1,0:T(8,128)S(1)}, u32[]{:S(2)}, u32[]{:S(2)}) %collective-permute-start.107) | collective-permute-done | bytes 524320 | tf_op jit(solution)/shard_map/ppermute | solution.py:62
  (251 shorter events, 126.1 us)
Async XLA Ops:
  29.8 139.4 %collective-permute-start.58 = (bf16[2,2432,2048]{2,1,0:T(8,128)(2,1)}, bf16[2,2432,2048]{2,1,0:T(8,128)(2,1)}, u32[]{:S(2)}, u32[]{:S(2)}) collective-permute-start(bf16[2,2432,2048]{2,1,0:T(8,128)(2,1)} %pack_rest.1.own_ref.refs_2_.refs_14_), channel_id=1, source_target_pairs={{0,1},{1,0},{2,3},{3,2},{4,5},{5,4},{6,7},{7,6}} | collective-permute-start | bytes 59768840 | tf_op jit(solution)/shard_map/ppermute | solution.py:50
  29.9 63.7 %collective-permute-start.60 = (bf16[2,768,2048]{2,1,0:T(8,128)(2,1)}, bf16[2,768,2048]{2,1,0:T(8,128)(2,1)}, u32[]{:S(2)}, u32[]{:S(2)}) collective-permute-start(bf16[2,768,2048]{2,1,0:T(8,128)(2,1)} %bitcast.98), channel_id=1, source_target_pairs={{0,1},{1,0},{2,3},{3,2},{4,5},{5,4},{6,7},{7,6}} | collective-permute-start | bytes 18874376 | tf_op jit(solution)/shard_map/ppermute | solution.py:50
  30.3 137.8 %collective-permute-start.61 = (bf16[2,768,2048]{2,1,0:T(8,128)(2,1)}, bf16[2,768,2048]{2,1,0:T(8,128)(2,1)}, u32[]{:S(2)}, u32[]{:S(2)}) collective-permute-start(bf16[2,768,2048]{2,1,0:T(8,128)(2,1)} %bitcast.99), channel_id=1, source_target_pairs={{0,4},{4,0},{1,5},{5,1},{2,6},{6,2},{3,7},{7,3}} | collective-permute-start | bytes 18874376 | tf_op jit(solution)/shard_map/ppermute | solution.py:62
  34.7 59.0 %collective-permute-start.63 = (bf16[2,512,1024]{2,1,0:T(8,128)(2,1)}, bf16[2,512,1024]{2,1,0:T(8,128)(2,1)S(1)}, u32[]{:S(2)}, u32[]{:S(2)}) collective-permute-start(bf16[2,512,1024]{2,1,0:T(8,128)(2,1)} %pad_maximum_fusion), channel_id=1, source_target_pairs={{0,1},{1,0},{2,3},{3,2},{4,5},{5,4},{6,7},{7,6}} | collective-permute-start | bytes 6291464 | tf_op jit(solution)/shard_map/ppermute | solution.py:50
  92.3 122.9 %collective-permute-start.67 = (bf16[2,512,256]{2,1,0:T(8,128)(2,1)}, bf16[2,512,256]{2,1,0:T(8,128)(2,1)}, u32[]{:S(2)}, u32[]{:S(2)}) collective-permute-start(bf16[2,512,256]{2,1,0:T(8,128)(2,1)} %pad_maximum_fusion.5), channel_id=1, source_target_pairs={{0,2},{2,0},{1,3},{3,1},{4,6},{6,4},{5,7},{7,5}} | collective-permute-start | bytes 1572872 | tf_op jit(solution)/shard_map/ppermute | solution.py:54
  93.6 121.6 %collective-permute-start.68 = (bf16[2,512,256]{2,1,0:T(8,128)(2,1)}, bf16[2,512,256]{2,1,0:T(8,128)(2,1)}, u32[]{:S(2)}, u32[]{:S(2)}) collective-permute-start(bf16[2,512,256]{2,1,0:T(8,128)(2,1)} %pad_maximum_fusion.6), channel_id=1, source_target_pairs={{0,3},{3,0},{1,2},{2,1},{4,7},{7,4},{5,6},{6,5}} | collective-permute-start | bytes 1572872 | tf_op jit(solution)/shard_map/ppermute | solution.py:58
  93.6 123.7 %collective-permute-start.69 = (bf16[256,2048]{1,0:T(8,128)(2,1)}, bf16[256,2048]{1,0:T(8,128)(2,1)S(1)}, u32[]{:S(2)}, u32[]{:S(2)}) collective-permute-start(bf16[256,2048]{1,0:T(8,128)(2,1)} %get-tuple-element.937), channel_id=1, source_target_pairs={{0,2},{2,0},{1,3},{3,1},{4,6},{6,4},{5,7},{7,5}} | collective-permute-start | bytes 3145736 | tf_op jit(solution)/shard_map/ppermute | solution.py:54
  168.1 83.3 %collective-permute-start.70 = (bf16[2,512,512]{2,1,0:T(8,128)(2,1)}, bf16[2,512,512]{2,1,0:T(8,128)(2,1)}, u32[]{:S(2)}, u32[]{:S(2)}) collective-permute-start(bf16[2,512,512]{2,1,0:T(8,128)(2,1)} %pad_maximum_fusion.1), channel_id=1, source_target_pairs={{0,2},{2,0},{1,3},{3,1},{4,6},{6,4},{5,7},{7,5}} | collective-permute-start | bytes 3145736 | tf_op jit(solution)/shard_map/ppermute | solution.py:54
  169.2 116.7 %collective-permute-start.62 = (bf16[2,768,2048]{2,1,0:T(8,128)(2,1)}, bf16[2,768,2048]{2,1,0:T(8,128)(2,1)}, u32[]{:S(2)}, u32[]{:S(2)}) collective-permute-start(bf16[2,768,2048]{2,1,0:T(8,128)(2,1)} %collective-permute-done.61.refs_4_), channel_id=1, source_target_pairs={{0,1},{1,0},{2,3},{3,2},{4,5},{5,4},{6,7},{7,6}} | collective-permute-start | bytes 18874376 | tf_op jit(solution)/shard_map/ppermute | solution.py:50
  215.2 70.7 %collective-permute-start.72 = (bf16[512,2048]{1,0:T(8,128)(2,1)}, bf16[512,2048]{1,0:T(8,128)(2,1)}, u32[]{:S(2)}, u32[]{:S(2)}) collective-permute-start(bf16[512,2048]{1,0:T(8,128)(2,1)} %dynamic-slice_bitcast_fusion), channel_id=1, source_target_pairs={{0,2},{2,0},{1,3},{3,1},{4,6},{6,4},{5,7},{7,5}} | collective-permute-start | bytes 6291464 | tf_op jit(solution)/shard_map/ppermute | solution.py:54
  293.9 236.7 %collective-permute-start.22 = (bf16[2,512,2048]{2,1,0:T(8,128)(2,1)}, bf16[2,512,2048]{2,1,0:T(8,128)(2,1)}, u32[]{:S(2)}, u32[]{:S(2)}) collective-permute-start(bf16[2,512,2048]{2,1,0:T(8,128)(2,1)} %get-tuple-element.569), channel_id=1, source_target_pairs={{0,4},{4,0},{1,5},{5,1},{2,6},{6,2},{3,7},{7,3}} | collective-permute-start | bytes 12582920 | tf_op jit(solution)/shard_map/cond/branch_4_fun/ppermute | solution.py:62
  305.2 225.8 %collective-permute-start.23 = (bf16[2,512,2048]{2,1,0:T(8,128)(2,1)}, bf16[2,512,2048]{2,1,0:T(8,128)(2,1)}, u32[]{:S(2)}, u32[]{:S(2)}) collective-permute-start(bf16[2,512,2048]{2,1,0:T(8,128)(2,1)} %get-tuple-element.570), channel_id=1, source_target_pairs={{0,4},{4,0},{1,5},{5,1},{2,6},{6,2},{3,7},{7,3}} | collective-permute-start | bytes 12582920 | tf_op jit(solution)/shard_map/cond/branch_4_fun/ppermute | solution.py:62
  305.3 204.1 %collective-permute-start.24 = (bf16[2,128,2048]{2,1,0:T(8,128)(2,1)}, bf16[2,128,2048]{2,1,0:T(8,128)(2,1)}, u32[]{:S(2)}, u32[]{:S(2)}) collective-permute-start(bf16[2,128,2048]{2,1,0:T(8,128)(2,1)} %get-tuple-element.571), channel_id=1, source_target_pairs={{0,4},{4,0},{1,5},{5,1},{2,6},{6,2},{3,7},{7,3}} | collective-permute-start | bytes 3145736 | tf_op jit(solution)/shard_map/cond/branch_4_fun/ppermute | solution.py:62
  307.3 223.3 %collective-permute-start.25 = (bf16[2,128,2048]{2,1,0:T(8,128)(2,1)}, bf16[2,128,2048]{2,1,0:T(8,128)(2,1)}, u32[]{:S(2)}, u32[]{:S(2)}) collective-permute-start(bf16[2,128,2048]{2,1,0:T(8,128)(2,1)} %get-tuple-element.572), channel_id=1, source_target_pairs={{0,4},{4,0},{1,5},{5,1},{2,6},{6,2},{3,7},{7,3}} | collective-permute-start | bytes 3145736 | tf_op jit(solution)/shard_map/cond/branch_4_fun/ppermute | solution.py:62
  509.3 176.5 %collective-permute-start.28 = (bf16[2,128,2048]{2,1,0:T(8,128)(2,1)}, bf16[2,128,2048]{2,1,0:T(8,128)(2,1)}, u32[]{:S(2)}, u32[]{:S(2)}) collective-permute-start(bf16[2,128,2048]{2,1,0:T(8,128)(2,1)} %collective-permute-done.24), channel_id=1, source_target_pairs={{0,1},{1,0},{2,3},{3,2},{4,5},{5,4},{6,7},{7,6}} | collective-permute-start | bytes 3145736 | tf_op jit(solution)/shard_map/cond/branch_4_fun/ppermute | solution.py:50
  530.6 155.3 %collective-permute-start.29 = (bf16[2,128,2048]{2,1,0:T(8,128)(2,1)}, bf16[2,128,2048]{2,1,0:T(8,128)(2,1)}, u32[]{:S(2)}, u32[]{:S(2)}) collective-permute-start(bf16[2,128,2048]{2,1,0:T(8,128)(2,1)} %collective-permute-done.25), channel_id=1, source_target_pairs={{0,1},{1,0},{2,3},{3,2},{4,5},{5,4},{6,7},{7,6}} | collective-permute-start | bytes 3145736 | tf_op jit(solution)/shard_map/cond/branch_4_fun/ppermute | solution.py:50
  530.6 155.3 %collective-permute-start.26 = (bf16[2,512,2048]{2,1,0:T(8,128)(2,1)}, bf16[2,512,2048]{2,1,0:T(8,128)(2,1)}, u32[]{:S(2)}, u32[]{:S(2)}) collective-permute-start(bf16[2,512,2048]{2,1,0:T(8,128)(2,1)} %collective-permute-done.22), channel_id=1, source_target_pairs={{0,1},{1,0},{2,3},{3,2},{4,5},{5,4},{6,7},{7,6}} | collective-permute-start | bytes 12582920 | tf_op jit(solution)/shard_map/cond/branch_4_fun/ppermute | solution.py:50
  531.1 154.8 %collective-permute-start.27 = (bf16[2,512,2048]{2,1,0:T(8,128)(2,1)}, bf16[2,512,2048]{2,1,0:T(8,128)(2,1)}, u32[]{:S(2)}, u32[]{:S(2)}) collective-permute-start(bf16[2,512,2048]{2,1,0:T(8,128)(2,1)} %collective-permute-done.23), channel_id=1, source_target_pairs={{0,1},{1,0},{2,3},{3,2},{4,5},{5,4},{6,7},{7,6}} | collective-permute-start | bytes 12582920 | tf_op jit(solution)/shard_map/cond/branch_4_fun/ppermute | solution.py:50
  694.6 90.7 %collective-permute-start.59 = (bf16[2,384,2048]{2,1,0:T(8,128)(2,1)}, bf16[2,384,2048]{2,1,0:T(8,128)(2,1)S(1)}, u32[]{:S(2)}, u32[]{:S(2)}) collective-permute-start(bf16[2,384,2048]{2,1,0:T(8,128)(2,1)} %get-tuple-element.811), channel_id=1, source_target_pairs={{0,4},{4,0},{1,5},{5,1},{2,6},{6,2},{3,7},{7,3}} | collective-permute-start | bytes 9437192 | tf_op jit(solution)/shard_map/ppermute | solution.py:62
  868.0 74.3 %collective-permute-start.80 = (f32[128,2048]{1,0:T(8,128)}, f32[128,2048]{1,0:T(8,128)}, u32[]{:S(2)}, u32[]{:S(2)}) collective-permute-start(f32[128,2048]{1,0:T(8,128)} %get-tuple-element.856), channel_id=1, source_target_pairs={{0,2},{2,0},{1,3},{3,1},{4,6},{6,4},{5,7},{7,5}} | collective-permute-start | bytes 3145736 | tf_op jit(solution)/shard_map/ppermute | solution.py:54
  870.0 69.3 %collective-permute-start.81 = (f32[128,2048]{1,0:T(8,128)}, f32[128,2048]{1,0:T(8,128)}, u32[]{:S(2)}, u32[]{:S(2)}) collective-permute-start(f32[128,2048]{1,0:T(8,128)} %get-tuple-element.858), channel_id=1, source_target_pairs={{0,2},{2,0},{1,3},{3,1},{4,6},{6,4},{5,7},{7,5}} | collective-permute-start | bytes 3145736 | tf_op jit(solution)/shard_map/ppermute | solution.py:54
  897.6 64.2 %collective-permute-start.77 = (f32[128,2048]{1,0:T(8,128)}, f32[128,2048]{1,0:T(8,128)}, u32[]{:S(2)}, u32[]{:S(2)}) collective-permute-start(f32[128,2048]{1,0:T(8,128)} %get-tuple-element.849), channel_id=1, source_target_pairs={{0,2},{2,0},{1,3},{3,1},{4,6},{6,4},{5,7},{7,5}} | collective-permute-start | bytes 3145736 | tf_op jit(solution)/shard_map/ppermute | solution.py:54
  925.1 58.0 %collective-permute-start.76 = (f32[128,2048]{1,0:T(8,128)}, f32[128,2048]{1,0:T(8,128)S(1)}, u32[]{:S(2)}, u32[]{:S(2)}) collective-permute-start(f32[128,2048]{1,0:T(8,128)} %get-tuple-element.846), channel_id=1, source_target_pairs={{0,2},{2,0},{1,3},{3,1},{4,6},{6,4},{5,7},{7,5}} | collective-permute-start | bytes 3145736 | tf_op jit(solution)/shard_map/ppermute | solution.py:54
  945.4 65.4 %collective-permute-start.83 = (f32[2,512,128]{2,1,0:T(8,128)}, f32[2,512,128]{2,1,0:T(8,128)S(1)}, u32[]{:S(2)}, u32[]{:S(2)}) collective-permute-start(f32[2,512,128]{2,1,0:T(8,128)} %get-tuple-element.861), channel_id=1, source_target_pairs={{0,5},{1,4},{2,7},{3,6},{4,1},{5,0},{6,3},{7,2}} | collective-permute-start | bytes 1572872 | tf_op jit(solution)/shard_map/ppermute | solution.py:66
  945.5 65.4 %collective-permute-start.84 = (f32[2,512,128]{2,1,0:T(8,128)}, f32[2,512,128]{2,1,0:T(8,128)S(1)}, u32[]{:S(2)}, u32[]{:S(2)}) collective-permute-start(f32[2,512,128]{2,1,0:T(8,128)} %get-tuple-element.861), channel_id=1, source_target_pairs={{0,1},{1,0},{2,3},{3,2},{4,5},{5,4},{6,7},{7,6}} | collective-permute-start | bytes 1572872 | tf_op jit(solution)/shard_map/ppermute | solution.py:50
  961.7 51.9 %collective-permute-start.88 = (f32[2,512,128]{2,1,0:T(8,128)}, f32[2,512,128]{2,1,0:T(8,128)S(1)}, u32[]{:S(2)}, u32[]{:S(2)}) collective-permute-start(f32[2,512,128]{2,1,0:T(8,128)} %get-tuple-element.866), channel_id=1, source_target_pairs={{0,5},{1,4},{2,7},{3,6},{4,1},{5,0},{6,3},{7,2}} | collective-permute-start | bytes 1572872 | tf_op jit(solution)/shard_map/ppermute | solution.py:66
  964.7 51.0 %collective-permute-start.89 = (f32[2,512,128]{2,1,0:T(8,128)}, f32[2,512,128]{2,1,0:T(8,128)}, u32[]{:S(2)}, u32[]{:S(2)}) collective-permute-start(f32[2,512,128]{2,1,0:T(8,128)} %get-tuple-element.866), channel_id=1, source_target_pairs={{0,1},{1,0},{2,3},{3,2},{4,5},{5,4},{6,7},{7,6}} | collective-permute-start | bytes 1572872 | tf_op jit(solution)/shard_map/ppermute | solution.py:50
  1010.8 81.4 %collective-permute-start.79 = (f32[128,2048]{1,0:T(8,128)}, f32[128,2048]{1,0:T(8,128)S(1)}, u32[]{:S(2)}, u32[]{:S(2)}) collective-permute-start(f32[128,2048]{1,0:T(8,128)} %get-tuple-element.844.refs_23_), channel_id=1, source_target_pairs={{0,4},{4,0},{1,5},{5,1},{2,6},{6,2},{3,7},{7,3}} | collective-permute-start | bytes 3145736 | tf_op jit(solution)/shard_map/ppermute | solution.py:62
  1011.6 57.0 %collective-permute-start.86 = (f32[128,2048]{1,0:T(8,128)}, f32[128,2048]{1,0:T(8,128)S(1)}, u32[]{:S(2)}, u32[]{:S(2)}) collective-permute-start(f32[128,2048]{1,0:T(8,128)} %get-tuple-element.847.refs_23_), channel_id=1, source_target_pairs={{0,4},{4,0},{1,5},{5,1},{2,6},{6,2},{3,7},{7,3}} | collective-permute-start | bytes 3145736 | tf_op jit(solution)/shard_map/ppermute | solution.py:62
  1013.7 48.8 %collective-permute-start.91 = (f32[128,2048]{1,0:T(8,128)}, f32[128,2048]{1,0:T(8,128)}, u32[]{:S(2)}, u32[]{:S(2)}) collective-permute-start(f32[128,2048]{1,0:T(8,128)} %get-tuple-element.871), channel_id=1, source_target_pairs={{0,2},{2,0},{1,3},{3,1},{4,6},{6,4},{5,7},{7,5}} | collective-permute-start | bytes 3145736 | tf_op jit(solution)/shard_map/ppermute | solution.py:54
  1015.7 69.3 %collective-permute-start.85 = (f32[128,2048]{1,0:T(8,128)}, f32[128,2048]{1,0:T(8,128)}, u32[]{:S(2)}, u32[]{:S(2)}) collective-permute-start(f32[128,2048]{1,0:T(8,128)} %get-tuple-element.864), channel_id=1, source_target_pairs={{0,2},{2,0},{1,3},{3,1},{4,6},{6,4},{5,7},{7,5}} | collective-permute-start | bytes 3145736 | tf_op jit(solution)/shard_map/ppermute | solution.py:54
  1040.3 67.1 %collective-permute-start.92 = (f32[128,2048]{1,0:T(8,128)}, f32[128,2048]{1,0:T(8,128)}, u32[]{:S(2)}, u32[]{:S(2)}) collective-permute-start(f32[128,2048]{1,0:T(8,128)} %get-tuple-element.878), channel_id=1, source_target_pairs={{0,2},{2,0},{1,3},{3,1},{4,6},{6,4},{5,7},{7,5}} | collective-permute-start | bytes 3145736 | tf_op jit(solution)/shard_map/ppermute | solution.py:54
  1062.5 67.4 %collective-permute-start.103 = (f32[128,2048]{1,0:T(8,128)}, f32[128,2048]{1,0:T(8,128)}, u32[]{:S(2)}, u32[]{:S(2)}) collective-permute-start(f32[128,2048]{1,0:T(8,128)} %get-tuple-element.894), channel_id=1, source_target_pairs={{0,2},{2,0},{1,3},{3,1},{4,6},{6,4},{5,7},{7,5}} | collective-permute-start | bytes 3145736 | tf_op jit(solution)/shard_map/ppermute | solution.py:54
  1084.9 65.1 %collective-permute-start.78 = (f32[128,2048]{1,0:T(8,128)}, f32[128,2048]{1,0:T(8,128)}, u32[]{:S(2)}, u32[]{:S(2)}) collective-permute-start(f32[128,2048]{1,0:T(8,128)} %get-tuple-element.854), channel_id=1, source_target_pairs={{0,2},{2,0},{1,3},{3,1},{4,6},{6,4},{5,7},{7,5}} | collective-permute-start | bytes 3145736 | tf_op jit(solution)/shard_map/ppermute | solution.py:54
  1092.2 47.2 %collective-permute-start.96 = (f32[2,512,128]{2,1,0:T(8,128)}, f32[2,512,128]{2,1,0:T(8,128)S(1)}, u32[]{:S(2)}, u32[]{:S(2)}) collective-permute-start(f32[2,512,128]{2,1,0:T(8,128)} %get-tuple-element.886), channel_id=1, source_target_pairs={{0,5},{1,4},{2,7},{3,6},{4,1},{5,0},{6,3},{7,2}} | collective-permute-start | bytes 1572872 | tf_op jit(solution)/shard_map/ppermute | solution.py:66
  1092.2 48.0 %collective-permute-start.97 = (f32[2,512,128]{2,1,0:T(8,128)}, f32[2,512,128]{2,1,0:T(8,128)S(1)}, u32[]{:S(2)}, u32[]{:S(2)}) collective-permute-start(f32[2,512,128]{2,1,0:T(8,128)} %get-tuple-element.886), channel_id=1, source_target_pairs={{0,1},{1,0},{2,3},{3,2},{4,5},{5,4},{6,7},{7,6}} | collective-permute-start | bytes 1572872 | tf_op jit(solution)/shard_map/ppermute | solution.py:50
  1141.0 47.9 %collective-permute-start.99 = (f32[128,2048]{1,0:T(8,128)}, f32[128,2048]{1,0:T(8,128)S(1)}, u32[]{:S(2)}, u32[]{:S(2)}) collective-permute-start(f32[128,2048]{1,0:T(8,128)} %get-tuple-element.862.refs_23_), channel_id=1, source_target_pairs={{0,4},{4,0},{1,5},{5,1},{2,6},{6,2},{3,7},{7,3}} | collective-permute-start | bytes 3145736 | tf_op jit(solution)/shard_map/ppermute | solution.py:62
  1143.0 57.1 %collective-permute-start.115 = (f32[2,512,128]{2,1,0:T(8,128)}, f32[2,512,128]{2,1,0:T(8,128)S(1)}, u32[]{:S(2)}, u32[]{:S(2)}) collective-permute-start(f32[2,512,128]{2,1,0:T(8,128)} %get-tuple-element.913), channel_id=1, source_target_pairs={{0,4},{4,0},{1,5},{5,1},{2,6},{6,2},{3,7},{7,3}} | collective-permute-start | bytes 1572872 | tf_op jit(solution)/shard_map/ppermute | solution.py:62
  1150.0 60.2 %collective-permute-start.116 = (f32[2,512,128]{2,1,0:T(8,128)}, f32[2,512,128]{2,1,0:T(8,128)S(1)}, u32[]{:S(2)}, u32[]{:S(2)}) collective-permute-start(f32[2,512,128]{2,1,0:T(8,128)} %get-tuple-element.914), channel_id=1, source_target_pairs={{0,5},{1,4},{2,7},{3,6},{4,1},{5,0},{6,3},{7,2}} | collective-permute-start | bytes 1572872 | tf_op jit(solution)/shard_map/ppermute | solution.py:66
  1177.6 57.9 %collective-permute-start.117 = (f32[2,512,128]{2,1,0:T(8,128)}, f32[2,512,128]{2,1,0:T(8,128)}, u32[]{:S(2)}, u32[]{:S(2)}) collective-permute-start(f32[2,512,128]{2,1,0:T(8,128)} %get-tuple-element.914), channel_id=1, source_target_pairs={{0,1},{1,0},{2,3},{3,2},{4,5},{5,4},{6,7},{7,6}} | collective-permute-start | bytes 1572872 | tf_op jit(solution)/shard_map/ppermute | solution.py:50
  1178.0 59.5 %collective-permute-start.98 = (f32[128,2048]{1,0:T(8,128)}, f32[128,2048]{1,0:T(8,128)}, u32[]{:S(2)}, u32[]{:S(2)}) collective-permute-start(f32[128,2048]{1,0:T(8,128)} %get-tuple-element.889), channel_id=1, source_target_pairs={{0,2},{2,0},{1,3},{3,1},{4,6},{6,4},{5,7},{7,5}} | collective-permute-start | bytes 3145736 | tf_op jit(solution)/shard_map/ppermute | solution.py:54
  1188.9 50.7 %collective-permute-start.104 = (f32[128,2048]{1,0:T(8,128)}, f32[128,2048]{1,0:T(8,128)}, u32[]{:S(2)}, u32[]{:S(2)}) collective-permute-start(f32[128,2048]{1,0:T(8,128)} %get-tuple-element.900), channel_id=1, source_target_pairs={{0,2},{2,0},{1,3},{3,1},{4,6},{6,4},{5,7},{7,5}} | collective-permute-start | bytes 3145736 | tf_op jit(solution)/shard_map/ppermute | solution.py:54
  1235.5 47.9 %collective-permute-start.106 = (f32[128,2048]{1,0:T(8,128)}, f32[128,2048]{1,0:T(8,128)}, u32[]{:S(2)}, u32[]{:S(2)}) collective-permute-start(f32[128,2048]{1,0:T(8,128)} %get-tuple-element.906), channel_id=1, source_target_pairs={{0,2},{2,0},{1,3},{3,1},{4,6},{6,4},{5,7},{7,5}} | collective-permute-start | bytes 3145736 | tf_op jit(solution)/shard_map/ppermute | solution.py:54
  1237.6 49.9 %collective-permute-start.118 = (f32[128,2048]{1,0:T(8,128)}, f32[128,2048]{1,0:T(8,128)}, u32[]{:S(2)}, u32[]{:S(2)}) collective-permute-start(f32[128,2048]{1,0:T(8,128)} %get-tuple-element.887.refs_23_), channel_id=1, source_target_pairs={{0,4},{4,0},{1,5},{5,1},{2,6},{6,2},{3,7},{7,3}} | collective-permute-start | bytes 3145736 | tf_op jit(solution)/shard_map/ppermute | solution.py:62
  1249.7 86.6 %collective-permute-start.110 = (f32[128,2048]{1,0:T(8,128)}, f32[128,2048]{1,0:T(8,128)S(1)}, u32[]{:S(2)}, u32[]{:S(2)}) collective-permute-start(f32[128,2048]{1,0:T(8,128)} %get-tuple-element.910), channel_id=1, source_target_pairs={{0,4},{4,0},{1,5},{5,1},{2,6},{6,2},{3,7},{7,3}} | collective-permute-start | bytes 3145736 | tf_op jit(solution)/shard_map/ppermute | solution.py:62
  1260.9 70.7 %collective-permute-start.112 = (f32[2,512,128]{2,1,0:T(8,128)}, f32[2,512,128]{2,1,0:T(8,128)S(1)}, u32[]{:S(2)}, u32[]{:S(2)}) collective-permute-start(f32[2,512,128]{2,1,0:T(8,128)} %get-tuple-element.912), channel_id=1, source_target_pairs={{0,5},{1,4},{2,7},{3,6},{4,1},{5,0},{6,3},{7,2}} | collective-permute-start | bytes 1572872 | tf_op jit(solution)/shard_map/ppermute | solution.py:66
  1283.4 48.3 %collective-permute-start.113 = (f32[2,512,128]{2,1,0:T(8,128)}, f32[2,512,128]{2,1,0:T(8,128)}, u32[]{:S(2)}, u32[]{:S(2)}) collective-permute-start(f32[2,512,128]{2,1,0:T(8,128)} %get-tuple-element.912), channel_id=1, source_target_pairs={{0,1},{1,0},{2,3},{3,2},{4,5},{5,4},{6,7},{7,6}} | collective-permute-start | bytes 1572872 | tf_op jit(solution)/shard_map/ppermute | solution.py:50
  1287.5 88.3 %collective-permute-start.105 = (f32[128,2048]{1,0:T(8,128)}, f32[128,2048]{1,0:T(8,128)S(1)}, u32[]{:S(2)}, u32[]{:S(2)}) collective-permute-start(f32[128,2048]{1,0:T(8,128)} %get-tuple-element.904), channel_id=1, source_target_pairs={{0,4},{4,0},{1,5},{5,1},{2,6},{6,2},{3,7},{7,3}} | collective-permute-start | bytes 3145736 | tf_op jit(solution)/shard_map/ppermute | solution.py:62
  (58 other events, 1587.9 us)

commit v2 on v1

--- a/solution.py
+++ b/solution.py
@@ -15,9 +15,10 @@
 NT = MICRO * REST // TM
 RROWS = MICRO * REST + TM
 FIRST = 3
-PIECES = (4, 4, 3, 2, 1, 1)
-SIZES = (5, 7, 8, 9, 10, 11, 12, 15)
-PARTS = ((0, 4), (0, 3, 4), (0, 2, 4), (0, 1, 4), (0, 1, 4, 5), (0, 1, 3, 4), (0, 1, 2, 4), (0, 1, 2, 3, 4, 5))
+MAIN = (4, 4, 3, 2)
+TAIL = 2
+SIZES = (6, 7, 8, 9, 10, 11, 12, 15)
+PARTS = ((0,), (2, 3), (0, 3), (0, 2), (0, 1), (0, 2, 3), (0, 1, 3), (0, 1, 2, 3))
 G = 4
 M = G * TM
 FB = 256
@@ -133,30 +134,58 @@
 
 
 def pack_rest(x_in, dy, rest, offs):
+    per = REST // TM
+
     def kern(rest_ref, offs_ref, x_ref, d_ref, out_ref, buf, zero, isem, osem, zsem):
-        loads = []
+        def load(k, t):
+            rows = pl.ds(BASE + t * TM, TM)
+            return [
+                pltpu.make_async_copy(ref.at[k, rows, :], buf.at[k, t, a], isem.at[k, t, a])
+                for a, ref in enumerate((x_ref, d_ref))
+            ]
+
+        def put(k, t):
+            o = pl.multiple_of(offs_ref[k] + t * TM, 16)
+            return [
+                pltpu.make_async_copy(buf.at[k, t, a], out_ref.at[a, pl.ds(o, TM), :], osem.at[t, a]) for a in range(2)
+            ]
+
+        def each(k, fn):
+            for t in range(per):
+
+                @pl.when(t * TM < rest_ref[k])
+                def _():
+                    fn(k, t)
+
+        def begin(k, t):
+            for cp in load(k, t):
+                cp.start()
+
+        def move(k, t):
+            for cp in load(k, t):
+                cp.wait()
+            n = rest_ref[k] - t * TM
+
+            @pl.when(n < TM)
+            def _():
+                ragged = pl.multiple_of(n // 16 * 16, 16)
+                row = lax.broadcasted_iota(jnp.int32, (16, D), 0) + ragged
+                blk = buf[k, t, 1, pl.ds(ragged, 16), :]
+                buf[k, t, 1, pl.ds(ragged, 16), :] = jnp.where(row < n, blk, jnp.zeros_like(blk))
+
+            for cp in put(k, t):
+                cp.start()
+
+        def end(k, t):
+            for cp in put(k, t):
+                cp.wait()
+
         for k in range(MICRO):
-            for a, ref in enumerate((x_ref, d_ref)):
-                cp = pltpu.make_async_copy(ref.at[k, pl.ds(BASE, REST), :], buf.at[k, a], isem.at[k, a])
-                cp.start()
-                loads.append(cp)
+            each(k, begin)
         zero[...] = jnp.zeros_like(zero)
         for k in range(MICRO):
-            for a in range(2):
-                loads[2 * k + a].wait()
-            n = rest_ref[k]
-            ragged = pl.multiple_of(jnp.minimum(n // 16 * 16, REST - 16), 16)
-            row = lax.broadcasted_iota(jnp.int32, (16, D), 0) + ragged
-            blk = buf[k, 1, pl.ds(ragged, 16), :]
-            buf[k, 1, pl.ds(ragged, 16), :] = jnp.where(row < n, blk, jnp.zeros_like(blk))
-            o = pl.multiple_of(offs_ref[k], 16)
-            cps = [
-                pltpu.make_async_copy(buf.at[k, a], out_ref.at[a, pl.ds(o, REST), :], osem.at[a]) for a in range(2)
-            ]
-            for cp in cps:
-                cp.start()
-            for cp in cps:
-                cp.wait()
+            each(k, move)
+            each(k, end)
         for o in (pl.multiple_of(offs_ref[MICRO], 16), MICRO * REST):
             cps = [pltpu.make_async_copy(zero, out_ref.at[a, pl.ds(o, TM), :], zsem.at[a]) for a in range(2)]
             for cp in cps:
@@ -170,10 +199,10 @@
         out_specs=ANY,
         out_shape=jax.ShapeDtypeStruct((2, RROWS, D), BF),
         scratch_shapes=[
-            pltpu.VMEM((MICRO, 2, REST, D), BF),
+            pltpu.VMEM((MICRO, per, 2, TM, D), BF),
             pltpu.VMEM((TM, D), BF),
-            pltpu.SemaphoreType.DMA((MICRO, 2)),
-            pltpu.SemaphoreType.DMA((2,)),
+            pltpu.SemaphoreType.DMA((MICRO, per, 2)),
+            pltpu.SemaphoreType.DMA((per, 2)),
             pltpu.SemaphoreType.DMA((2,)),
         ],
         compiler_params=pltpu.CompilerParams(vmem_limit_bytes=GRANT),
@@ -183,12 +212,13 @@
 
 
 def build_send(own, sib, info):
-    np_ = 1 + len(PIECES)
+    sizes = (FIRST, *MAIN, TAIL, TAIL)
+    np_ = len(sizes)
 
     def kern(info_ref, own_ref, sib_ref, *refs):
         outs, (buf, isem, osem) = refs[:np_], refs[np_:]
-        n, mine, shift = info_ref[0], info_ref[1], info_ref[2]
-        starts = [0] + [info_ref[3 + k] for k in range(len(PIECES))]
+        n, keep, mine, shift = info_ref[0], info_ref[1], info_ref[2], info_ref[3]
+        starts = [0] + [info_ref[4 + k] for k in range(np_ - 2)]
 
         def load(i, slot):
             @pl.when(i < mine)
@@ -203,13 +233,16 @@
 
         def store(i, slot):
             for k in range(np_):
-                here = i >= starts[k]
-                if k + 1 < np_:
-                    here = jnp.logical_and(here, i < starts[k + 1])
+                if k == np_ - 1:
+                    here, at = i >= keep, i - keep
+                else:
+                    here, at = jnp.logical_and(i >= starts[k], i < keep), i - starts[k]
+                    if k + 1 < len(starts):
+                        here = jnp.logical_and(here, i < starts[k + 1])
 
                 @pl.when(here)
                 def _():
-                    r = pl.multiple_of((i - starts[k]) * TM, TM)
+                    r = pl.multiple_of(at * TM, TM)
                     pltpu.make_async_copy(buf.at[slot], outs[k].at[:, pl.ds(r, TM), :], osem.at[slot]).start()
 
         def stored(slot):
@@ -246,12 +279,40 @@
         kern,
         in_specs=[SM, ANY, ANY],
         out_specs=[ANY] * np_,
-        out_shape=[jax.ShapeDtypeStruct((2, k * TM, D), BF) for k in (FIRST, *PIECES)],
+        out_shape=[jax.ShapeDtypeStruct((2, k * TM, D), BF) for k in sizes],
         scratch_shapes=[pltpu.VMEM((4, 2, TM, D), BF), pltpu.SemaphoreType.DMA((4,)), pltpu.SemaphoreType.DMA((4,))],
         compiler_params=pltpu.CompilerParams(vmem_limit_bytes=GRANT),
         cost_estimate=cost(10_000_000_000, 36_000_000),
         name="build_send",
     )(info, own, sib)
+
+
+def append(tail, given, take):
+    def kern(take_ref, tail_ref, given_ref, out_ref, buf, sem):
+        for m in range(TAIL):
+
+            @pl.when(m < take_ref[0])
+            def _():
+                src = given_ref.at[:, pl.ds(m * TM, TM), :]
+                dst = out_ref.at[:, pl.ds((TAIL - 1 - m) * TM, TM), :]
+                cp = pltpu.make_async_copy(src, buf, sem)
+                cp.start()
+                cp.wait()
+                cp = pltpu.make_async_copy(buf, dst, sem)
+                cp.start()
+                cp.wait()
+
+    return pl.pallas_call(
+        kern,
+        in_specs=[SM, ANY, ANY],
+        out_specs=ANY,
+        out_shape=jax.ShapeDtypeStruct((2, TAIL * TM, D), BF),
+        scratch_shapes=[pltpu.VMEM((2, TM, D), BF), pltpu.SemaphoreType.DMA],
+        input_output_aliases={1: 0},
+        compiler_params=pltpu.CompilerParams(vmem_limit_bytes=GRANT),
+        cost_estimate=cost(1_000_000_000, 4_000_000),
+        name="append",
+    )(take, tail, given)
 
 
 def gelu_and_slope(u):
@@ -633,17 +694,23 @@
 
 
 def exchange_branch(parts, early):
-    here = [k in parts for k in range(len(PIECES))]
-
-    def run(pieces, *rest):
+    here = [k in parts for k in range(len(MAIN))]
+
+    def run(pieces, tail, give, take, *rest):
         got = []
-        for k in range(len(PIECES)):
-            got.append(y_swap(pieces[k]) if here[k] else nothing(PIECES[k]))
-        acc = early(*rest)
+        for k in range(len(MAIN)):
+            got.append(y_swap(pieces[k]) if here[k] else nothing(MAIN[k]))
+        given = x_swap(give)
+        acc = early(0, *rest)
+        given_s = core_swap(given)
+        tail = append(tail, given, take)
+        last = y_swap(tail)
+        acc = (*acc, *early(1, *rest))
         sib = []
-        for k in range(len(PIECES)):
-            sib.append(core_swap(got[k]) if here[k] else nothing(PIECES[k]))
-        return (*got, *sib, *acc)
+        for k in range(len(MAIN)):
+            sib.append(core_swap(got[k]) if here[k] else nothing(MAIN[k]))
+        last_s = core_swap(last)
+        return (*got, last, *sib, last_s, given, given_s, *acc)
 
     return run
 
@@ -652,11 +719,11 @@
     table = []
     for size, parts in zip(SIZES, PARTS):
         at, row = FIRST, []
-        for k in range(len(PIECES)):
+        for k in range(len(MAIN)):
             row.append(at)
-            at += PIECES[k] if k in parts else 0
-        assert at == FIRST + size
-        table.append(row)
+            at += MAIN[k] if k in parts else 0
+        assert at + TAIL == FIRST + size
+        table.append([*row, at])
     return table
 
 
@@ -698,43 +765,59 @@
         offs = jnp.concatenate([jnp.zeros((1,), jnp.int32), jnp.cumsum(my16)])
         both = tiles[0::2] + tiles[1::2]
         share = jnp.stack([(both + 1) // 2, both // 2], axis=1).reshape(8)
-        which = jnp.sum(jnp.max(share) - FIRST > jnp.array(SIZES[:-1]))
+        gap = share - share[jnp.arange(8) ^ 2]
+        move = jnp.minimum(jnp.abs(gap) // 2, TAIL)
+        keep = share - jnp.where(gap > 0, move, 0)
+        take = jnp.where(gap < 0, move, 0)
+        which = jnp.sum(jnp.max(keep + take) - FIRST > jnp.array(SIZES[:-1]))
         starts = jnp.array(piece_starts())[which]
+        end = starts[-1] + TAIL
 
         def at(v, i):
             return lax.dynamic_index_in_dim(v, i, keepdims=False)
 
         t_own, t_sib = at(tiles, me), at(tiles, me ^ 1)
-        h_own = at(share, me)
-        h_y, h_ys = at(share, me ^ 4), at(share, me ^ 5)
+        h_own, h_sib = at(share, me), at(share, me ^ 1)
+        k_own, k_sib, k_y, k_ys = (at(keep, me ^ k) for k in (0, 1, 4, 5))
+        x_own, x_sib, x_y, x_ys = (at(take, me ^ k) for k in (0, 1, 4, 5))
+
         packed = pack_rest(x_in, dy, my_rest, offs)
         packed_s = core_swap(packed)
         s1_s = core_swap(s1)
-        pa, *pieces = build_send(
-            packed, packed_s, jnp.concatenate([jnp.stack([h_own, t_own, t_sib - h_own]), starts]).astype(jnp.int32)
+        pa, *pieces, tail, give = build_send(
+            packed, packed_s,
+            jnp.concatenate([jnp.stack([h_own, k_own, t_own, t_sib - h_own]), starts]).astype(jnp.int32),
         )
         qa = y_swap(pa)
 
         i = jnp.arange(64)
-        n_own = 12 + t_own + t_sib
+        n_own = 12 + k_own + k_sib
         g_own = (n_own + G - 1) // G
         k = i - g_own * G
-        tab = jnp.where(i < n_own, 3 * 32 + i - 12 - t_own, 2 * 32 + NT)
-        tab = jnp.where(i < 12 + t_own, 2 * 32 + i - 12, tab)
+        m, n = i - 12, i - 12 - k_own
+        tab = jnp.where(n < t_sib, 3 * 32 + n, 2 * 32 + n + t_own - h_sib)
+        tab = jnp.where(n < 0, jnp.where(m < t_own, 2 * 32 + m, 3 * 32 + m + t_sib - h_own), tab)
+        tab = jnp.where(i < n_own, tab, 2 * 32 + NT)
         tab = jnp.where(i < 12, (i // 6) * 32 + i % 6, tab)
         tab = jnp.where((k >= 0) & (k < 12), (4 + k // 6) * 32 + k % 6, tab).astype(jnp.int32)
         info_own = jnp.stack([0, g_own, y, f]).astype(jnp.int32)
         info_all = jnp.stack([g_own, g_own + 3, y, f]).astype(jnp.int32)
 
-        i = jnp.arange(40)
-        own_list = i < h_y
-        t = jnp.where(own_list, i, i - h_y)
+        n_src = 2 + len(MAIN)
+        l_y, l_ys = k_y + x_y, k_ys + x_ys
+        i = jnp.arange(48)
+        first = i < l_y
+        t = jnp.where(first, i, i - l_y)
+        listed = jnp.where(first, k_y, k_ys)
+        t = jnp.where(t < listed, t, end - 1 - (t - listed))
         late = t
-        for n in range(len(PIECES)):
+        for n in range(n_src - 1):
             late = jnp.where(t >= starts[n], (1 + n) * 32 + t - starts[n], late)
-        late = jnp.where(own_list, late, late + (1 + len(PIECES)) * 32)
-        late = jnp.where(i < h_y + h_ys, late, 2 * (1 + len(PIECES)) * 32 + NT).astype(jnp.int32)
-        info_late = jnp.stack([(h_y + h_ys + G - 1) // G, y, f]).astype(jnp.int32)
+        late = jnp.where(first, late, late + n_src * 32)
+        m = i - l_y - l_ys
+        handed = jnp.where(m < x_own, 2 * n_src * 32 + m, (2 * n_src + 1) * 32 + m - x_own)
+        late = jnp.where(m < 0, late, jnp.where(m < x_own + x_sib, handed, (2 * n_src + 2) * 32 + NT)).astype(jnp.int32)
+        info_late = jnp.stack([(l_y + l_ys + x_own + x_sib + G - 1) // G, y, f]).astype(jnp.int32)
         pos = jnp.stack([y, xi, c]).astype(jnp.int32)
 
         own_srcs = (s1, s1_s, packed, packed_s)
@@ -742,22 +825,24 @@
         acc1 = early_grads(tab, info_own, own_srcs, wsets[1:2], 2, 1, (), (late, info_late, pos))
         s1_ys = core_swap(s1_y)
         srcs = (*own_srcs, s1_y, s1_ys)
-        acc2 = early_grads(tab, info_all, srcs, wsets[1:2], 3, 1)
-
-        def early(tab, info, srcs, w, prior):
+
+        def early(step, tab, info, srcs, w, prior):
             sets = [(lo, n, v) for (lo, n), v in zip(WSETS, w)]
-            return early_grads(tab, info, srcs, sets, 4, 4, prior)
+            if step == 0:
+                return early_grads(tab, info, srcs, sets[1:], 3, 2)
+            return early_grads(tab, info, srcs, sets, 5, 3, prior)
 
         got = lax.switch(
             which,
             [exchange_branch(parts, early) for parts in PARTS],
-            pieces, tab, info_all, srcs, [w for _, _, w in wsets], [list(acc0), list(acc1)],
+            pieces, tail, give, x_own.reshape(1).astype(jnp.int32),
+            tab, info_all, srcs, [w for _, _, w in wsets], [list(acc0), list(acc1)],
         )
-        k = len(PIECES)
-        pieces, sib_pieces, acc3 = got[:k], got[k : 2 * k], got[2 * k :]
+        k = len(MAIN) + 1
+        pieces, sib_pieces, given, acc3, acc4 = got[:k], got[k : 2 * k], got[2 * k : 2 * k + 2], got[-4:-2], got[-2:]
         qas = core_swap(qa)
-        srcs = (qa, *pieces, qas, *sib_pieces, packed)
-        prior = [(acc3, 4), (acc3, 5), (acc3, 6), (acc2, 0), *((acc3, k) for k in range(4))]
+        srcs = (qa, *pieces, qas, *sib_pieces, *given, packed)
+        prior = [(acc4, 3), (acc4, 4), (acc4, 5), (acc3, 0), (acc3, 1), (acc4, 0), (acc4, 1), (acc4, 2)]
 
         out_d = out_u = None
         fin = []

time: 1390 us -> 1210 us (0.87)
  waiting for transfers between devices: 677 us -> 502 us
  Pallas kernels: 561 us -> 538 us
    ppermute x22 -> x21, waiting for transfers between devices: 459 us -> 243 us  [y_swap(): return lax.ppermute(v, 'replica', YSWAP)]
    ppermute x8, waiting for transfers between devices: 10.1 us -> 33.7 us  [y_diag(): return lax.ppermute(v, ('replica', 'fsdp'), YDIAG)]
    pallas_call x8, Pallas kernels: 197 us -> 177 us  [chunk_grads(): pl.pallas_call(kern, in_specs=[SM, SM] + [ANY] * (ns + 8 + len(deps)), ou...]
    ppermute x22 -> x23, waiting for transfers between devices: 202 us -> 220 us  [x_swap(): return lax.ppermute(v, 'fsdp', XSWAP)]
    ppermute x22 -> x21, starting transfers between devices: 48 us -> 35.7 us  [y_swap(): return lax.ppermute(v, 'replica', YSWAP)]
  transfers between devices with their start and end apart: 72 -> 72, of which waited for: 23 -> 22; matrix products, arithmetic and copies ran while one was open for 2% -> 3% of each run, Pallas kernels for 37% -> 41%
where the time goes in v2:
time: 1210 us; the launch traced here: 1200 us
  Pallas kernels  538 us (44%)
  waiting for transfers between devices  502 us (41%)
  starting transfers between devices  67.8 us (6%)
  local copies, waits for them, and re-layouts  35.2 us (3%)
  loops' own time  24 us (2%)
  other arithmetic  20.5 us (2%)
  between operations  13.2 us (1%)
    pallas_call x4, Pallas kernels, early_grads(): pl.pallas_call(kern, in_specs=[SM, SM] + [ANY] * (ns + len(flat) + len(pr...  258 us
    ppermute x21, waiting for transfers between devices, y_swap(): return lax.ppermute(v, 'replica', YSWAP)  243 us
    ppermute x23, waiting for transfers between devices, x_swap(): return lax.ppermute(v, 'fsdp', XSWAP)  220 us
    pallas_call x8, Pallas kernels, chunk_grads(): pl.pallas_call(kern, in_specs=[SM, SM] + [ANY] * (ns + 8 + len(deps)), ou...  177 us
    ppermute x21, starting transfers between devices, y_swap(): return lax.ppermute(v, 'replica', YSWAP)  35.7 us
    ppermute x8, waiting for transfers between devices, y_diag(): return lax.ppermute(v, ('replica', 'fsdp'), YDIAG)  33.7 us
    ppermute x23, starting transfers between devices, x_swap(): return lax.ppermute(v, 'fsdp', XSWAP)  26.2 us
    pallas_call x8, Pallas kernels, finish_up(): pl.pallas_call(kern, in_specs=[SM, VM, VM] + [ANY] * len(extra), out_spec...  24.5 us
  transfers between devices with their start and end apart: 72, of which 22 were waited for; matrix products, arithmetic and copies ran while one was open for 3% of the time, Pallas kernels for 41%

profile of v2, /device:TPU:0, one launch (start us, length us, event | category | flops | bytes accessed | tf_op | source)
XLA Modules:
  0.0 1201.7 jit_solution(11479081267198823665)
XLA Ops:
  2.0 8.3 start.1
  13.4 13.8 %pack_rest.1.own_ref.refs_2_.refs_14_ = bf16[2,2432,2048]{2,1,0:T(8,128)(2,1)} custom-call(s32[3]{0:T(128)} %fusion.3.rest_ref, s32[4]{0:T(128)} %pad_add_fusion.2.offs_ref, bf16[3,1024,2048]{2,1,0:T(8,128)(2,1)} %x_ref.3, bf16[3,1024,2048]{2,1,0:T(8,128)(2,1)} %d_ref.3), custom_call_target="tpu_custom_call" | custom-call | flops 15000000512 | bytes 50000000 | tf_op jit(solution)/shard_map/pack_rest/pallas_call | solution.py:196
  61.0 3.2 and_select_fusion.4.tab_ref
  68.9 5.6 compare_select_fusion.17.refs_10_.tab_ref
  79.9 3.2 dynamic-slice_bitcast_fusion
  83.1 9.3 collective-permute-done.84.refs_9_.refs_20_
  94.0 71.5 %collective-permute-done.73 = bf16[2,768,2048]{2,1,0:T(8,128)(2,1)} collective-permute-done((bf16[2,768,2048]{2,1,0:T(8,128)(2,1)}, bf16[2,768,2048]{2,1,0:T(8,128)(2,1)}, u32[]{:S(2)}, u32[]{:S(2)}) %collective-permute-start.73) | collective-permute-done | bytes 6291488 | tf_op jit(solution)/shard_map/ppermute | solution.py:63
  167.7 46.0 %shard_map.86 = (f32[2,256,2048]{2,1,0:T(8,128)}, f32[2,256,2048]{2,1,0:T(8,128)}) custom-call(s32[64]{0:T(128)S(1)} %and_select_fusion.4.tab_ref, s32[4]{0:T(128)} %fusion.10.info_ref, bf16[2,768,2048]{2,1,0:T(8,128)(2,1)} %bitcast.106, bf16[2,768,2048]{2,1,0:T(8,128)(2,1)} %collective-permute-done.72.refs_1_, ...), custom_call_target="tpu_custom_call" | custom-call | flops 47244640256 | bytes 120000000 | tf_op jit(solution)/shard_map/pallas_call | solution.py:509
  215.8 25.1 %shard_map.87 = (f32[1,256,2048]{2,1,0:T(8,128)}, f32[1,256,2048]{2,1,0:T(8,128)}) custom-call(s32[64]{0:T(128)S(1)} %and_select_fusion.4.tab_ref, s32[4]{0:T(128)} %fusion.10.info_ref, bf16[2,768,2048]{2,1,0:T(8,128)(2,1)} %bitcast.107, bf16[2,768,2048]{2,1,0:T(8,128)(2,1)} %collective-permute-done.72.refs_1_, ...), custom_call_target="tpu_custom_call" | custom-call | flops 23622320128 | bytes 60000000 | tf_op jit(solution)/shard_map/pallas_call | solution.py:509
  240.9 9.1 build_send.1
  250.0 34.4 %collective-permute-done.81.refs_20_ = bf16[512,2048]{1,0:T(8,128)(2,1)} collective-permute-done((bf16[512,2048]{1,0:T(8,128)(2,1)}, bf16[512,2048]{1,0:T(8,128)(2,1)}, u32[]{:S(2)}, u32[]{:S(2)}) %collective-permute-start.81) | collective-permute-done | bytes 2097184 | tf_op jit(solution)/shard_map/ppermute | solution.py:55
  284.4 295.5 %conditional.1 = (bf16[2,512,2048]{2,1,0:T(8,128)(2,1)}, bf16[2,512,2048]{2,1,0:T(8,128)(2,1)}, bf16[2,384,2048]{2,1,0:T(8,128)(2,1)}, bf16[2,256,2048]{2,1,0:T(...) conditional(s32[]{:T(128)} %clamp.3, ...), branch_computations={%region_4.5_spmd, %region_5.6_spmd, %region_6.7_spmd, %region_7.8_... | conditional | flops 119111598080 | bytes 446606944 | solution.py:835
  295.7 6.7 collective-permute-start.23
  302.4 40.3 %collective-permute-done.24.given_ref = bf16[2,256,2048]{2,1,0:T(8,128)(2,1)} collective-permute-done((bf16[2,256,2048]{2,1,0:T(8,128)(2,1)}, bf16[2,256,2048]{2,1,0:T(8,128)(2,1)}, u32[]{:S(2)}, u32[]{:S(2)}) %collective-permute-start.24) | collective-permute-done | bytes 2097184 | tf_op jit(solution)/shard_map/cond/branch_3_fun/ppermute | solution.py:55
  343.2 6.7 collective-permute-start.25
  349.9 125.7 %branch_3_fun.11 = (f32[6,256,2048]{2,1,0:T(8,128)}, f32[6,256,2048]{2,1,0:T(8,128)}) custom-call(s32[64]{0:T(128)S(1)} %get-tuple-element.585.tab_ref, s32[4]{0:T(128)S(1)} %get-tuple-element.586.info_ref, bf16[2,768,2048]{2,1,0:T(8,128)(2,1)} %get-tuple-element.587.refs_0_, bf16[2,768,2048]{2,1,0:T(8,128)(2,1)} %get-tuple-element.588.refs_1_, ...), custom_call_target="tpu_custom_call" | custom-call | flops 70866960384 | bytes 180000000 | tf_op jit(solution)/shard_map/cond/branch_3_fun/pallas_call | solution.py:509
  476.1 29.3 %collective-permute-done.25 = bf16[2,256,2048]{2,1,0:T(8,128)(2,1)} collective-permute-done((bf16[2,256,2048]{2,1,0:T(8,128)(2,1)}, bf16[2,256,2048]{2,1,0:T(8,128)(2,1)}, u32[]{:S(2)}, u32[]{:S(2)}) %collective-permute-start.25) | collective-permute-done | bytes 2097184 | tf_op jit(solution)/shard_map/cond/branch_3_fun/ppermute | solution.py:63
  505.9 61.0 %branch_3_fun.10 = (f32[2,256,2048]{2,1,0:T(8,128)}, f32[2,256,2048]{2,1,0:T(8,128)}) custom-call(s32[64]{0:T(128)S(1)} %get-tuple-element.585.tab_ref, s32[4]{0:T(128)S(1)} %get-tuple-element.586.info_ref, bf16[2,768,2048]{2,1,0:T(8,128)(2,1)} %get-tuple-element.587.refs_0_, bf16[2,768,2048]{2,1,0:T(8,128)(2,1)} %get-tuple-element.588.refs_1_, ...), custom_call_target="tpu_custom_call" | custom-call | flops 47244640256 | bytes 120000000 | tf_op jit(solution)/shard_map/cond/branch_3_fun/pallas_call | solution.py:509
  579.9 6.7 collective-permute-start.71
  586.6 68.5 %collective-permute-done.71.refs_0_ = bf16[2,384,2048]{2,1,0:T(8,128)(2,1)S(1)} collective-permute-done((bf16[2,384,2048]{2,1,0:T(8,128)(2,1)}, bf16[2,384,2048]{2,1,0:T(8,128)(2,1)S(1)}, u32[]{:S(2)}, u32[]{:S(2)}) %collective-permute-start.71) | collective-permute-done | bytes 3145760 | tf_op jit(solution)/shard_map/ppermute | solution.py:63
  655.2 5.7 collective-permute-done.85.refs_6_
  662.5 22.0 %shard_map.89 = (f32[128,2048]{1,0:T(8,128)}, f32[128,2048]{1,0:T(8,128)}, f32[128,2048]{1,0:T(8,128)}, f32[128,2048]{1,0:T(8,128)}) custom-call(s32[48]{0:T(128)} %compare_select_fusion.17.refs_10_.tab_ref, s32[3]{0:T(128)} %pad_add_fusion.4.refs_11_.info_ref, bf16[2,384,2048]{2,1,0:T(8,128)(2,1)} %copy-done.19, ...), custom_call_target="tpu_custom_call" | custom-call | flops 12884901888 | bytes 40000000 | tf_op jit(solution)/shard_map/pallas_call | solution.py:569
  684.6 22.0 %shard_map.88 = (f32[128,2048]{1,0:T(8,128)}, f32[128,2048]{1,0:T(8,128)}, f32[128,2048]{1,0:T(8,128)}, f32[128,2048]{1,0:T(8,128)}) custom-call(s32[48]{0:T(128)} %compare_select_fusion.17.refs_10_.tab_ref, s32[3]{0:T(128)} %pad_add_fusion.4.refs_11_.info_ref, bf16[2,384,2048]{2,1,0:T(8,128)(2,1)} %copy-done.19, ...), custom_call_target="tpu_custom_call" | custom-call | flops 12884901888 | bytes 40000000 | tf_op jit(solution)/shard_map/pallas_call | solution.py:569
  714.7 18.2 %collective-permute-done.92.rc = f32[128,2048]{1,0:T(8,128)S(1)} collective-permute-done((f32[128,2048]{1,0:T(8,128)}, f32[128,2048]{1,0:T(8,128)S(1)}, u32[]{:S(2)}, u32[]{:S(2)}) %collective-permute-start.92) | collective-permute-done | bytes 1048608 | tf_op jit(solution)/shard_map/ppermute | solution.py:55
  739.1 16.4 %collective-permute-done.87.rc = f32[128,2048]{1,0:T(8,128)} collective-permute-done((f32[128,2048]{1,0:T(8,128)}, f32[128,2048]{1,0:T(8,128)}, u32[]{:S(2)}, u32[]{:S(2)}) %collective-permute-start.87) | collective-permute-done | bytes 1048608 | tf_op jit(solution)/shard_map/ppermute | solution.py:55
  758.5 18.9 %collective-permute-done.86.rc = f32[128,2048]{1,0:T(8,128)S(1)} collective-permute-done((f32[128,2048]{1,0:T(8,128)}, f32[128,2048]{1,0:T(8,128)S(1)}, u32[]{:S(2)}, u32[]{:S(2)}) %collective-permute-start.86) | collective-permute-done | bytes 1048608 | tf_op jit(solution)/shard_map/ppermute | solution.py:55
  778.4 3.1 shard_map.91
  781.5 21.9 %shard_map.93 = (f32[128,2048]{1,0:T(8,128)}, f32[128,2048]{1,0:T(8,128)}, f32[128,2048]{1,0:T(8,128)}, f32[128,2048]{1,0:T(8,128)}) custom-call(s32[48]{0:T(128)} %compare_select_fusion.17.refs_10_.tab_ref, s32[3]{0:T(128)} %pad_add_fusion.4.refs_11_.info_ref, bf16[2,384,2048]{2,1,0:T(8,128)(2,1)} %copy-done.19, ...), custom_call_target="tpu_custom_call" | custom-call | flops 12884901888 | bytes 40000000 | tf_op jit(solution)/shard_map/pallas_call | solution.py:569
  804.7 22.3 %shard_map.92 = (f32[128,2048]{1,0:T(8,128)}, f32[128,2048]{1,0:T(8,128)}, f32[128,2048]{1,0:T(8,128)}, f32[128,2048]{1,0:T(8,128)}) custom-call(s32[48]{0:T(128)} %compare_select_fusion.17.refs_10_.tab_ref, s32[3]{0:T(128)} %pad_add_fusion.4.refs_11_.info_ref, bf16[2,384,2048]{2,1,0:T(8,128)(2,1)} %copy-done.19, ...), custom_call_target="tpu_custom_call" | custom-call | flops 12884901888 | bytes 40000000 | tf_op jit(solution)/shard_map/pallas_call | solution.py:569
  834.2 22.1 %shard_map.99 = (f32[128,2048]{1,0:T(8,128)}, f32[128,2048]{1,0:T(8,128)}, f32[128,2048]{1,0:T(8,128)}, f32[128,2048]{1,0:T(8,128)}) custom-call(s32[48]{0:T(128)} %compare_select_fusion.17.refs_10_.tab_ref, s32[3]{0:T(128)} %pad_add_fusion.4.refs_11_.info_ref, bf16[2,384,2048]{2,1,0:T(8,128)(2,1)} %copy-done.19, ...), custom_call_target="tpu_custom_call" | custom-call | flops 12884901888 | bytes 40000000 | tf_op jit(solution)/shard_map/pallas_call | solution.py:569
  858.5 21.8 %collective-permute-done.102.rc = f32[128,2048]{1,0:T(8,128)} collective-permute-done((f32[128,2048]{1,0:T(8,128)}, f32[128,2048]{1,0:T(8,128)}, u32[]{:S(2)}, u32[]{:S(2)}) %collective-permute-start.102) | collective-permute-done | bytes 1048608 | tf_op jit(solution)/shard_map/ppermute | solution.py:55
  880.3 22.5 %collective-permute-done.103.rc = f32[128,2048]{1,0:T(8,128)} collective-permute-done((f32[128,2048]{1,0:T(8,128)}, f32[128,2048]{1,0:T(8,128)}, u32[]{:S(2)}, u32[]{:S(2)}) %collective-permute-start.103) | collective-permute-done | bytes 1048608 | tf_op jit(solution)/shard_map/ppermute | solution.py:55
  905.8 3.1 shard_map.100
  918.9 4.2 collective-permute-done.97.rc
  923.4 22.1 %shard_map.96 = (f32[128,2048]{1,0:T(8,128)}, f32[128,2048]{1,0:T(8,128)}, f32[128,2048]{1,0:T(8,128)}, f32[128,2048]{1,0:T(8,128)}) custom-call(s32[48]{0:T(128)} %compare_select_fusion.17.refs_10_.tab_ref, s32[3]{0:T(128)} %pad_add_fusion.4.refs_11_.info_ref, bf16[2,384,2048]{2,1,0:T(8,128)(2,1)} %copy-done.19, ...), custom_call_target="tpu_custom_call" | custom-call | flops 12884901888 | bytes 40000000 | tf_op jit(solution)/shard_map/pallas_call | solution.py:569
  957.5 22.4 %shard_map.108 = (f32[128,2048]{1,0:T(8,128)}, f32[128,2048]{1,0:T(8,128)}, f32[128,2048]{1,0:T(8,128)}, f32[128,2048]{1,0:T(8,128)}) custom-call(s32[48]{0:T(128)} %compare_select_fusion.17.refs_10_.tab_ref, s32[3]{0:T(128)} %pad_add_fusion.4.refs_11_.info_ref, bf16[2,384,2048]{2,1,0:T(8,128)(2,1)} %copy-done.19, ...), custom_call_target="tpu_custom_call" | custom-call | flops 12884901888 | bytes 40000000 | tf_op jit(solution)/shard_map/pallas_call | solution.py:569
  979.9 3.1 shard_map.104
  984.5 19.3 %collective-permute-done.115.rc = f32[128,2048]{1,0:T(8,128)} collective-permute-done((f32[128,2048]{1,0:T(8,128)}, f32[128,2048]{1,0:T(8,128)}, u32[]{:S(2)}, u32[]{:S(2)}) %collective-permute-start.115) | collective-permute-done | bytes 1048608 | tf_op jit(solution)/shard_map/ppermute | solution.py:55
  1012.2 3.1 shard_map.109
  1017.5 6.6 collective-permute-done.131.uc_ref
  1024.3 22.1 %shard_map.107 = (f32[128,2048]{1,0:T(8,128)}, f32[128,2048]{1,0:T(8,128)}, f32[128,2048]{1,0:T(8,128)}, f32[128,2048]{1,0:T(8,128)}) custom-call(s32[48]{0:T(128)} %compare_select_fusion.17.refs_10_.tab_ref, s32[3]{0:T(128)} %pad_add_fusion.4.refs_11_.info_ref, bf16[2,384,2048]{2,1,0:T(8,128)(2,1)} %copy-done.19, ...), custom_call_target="tpu_custom_call" | custom-call | flops 12884901888 | bytes 40000000 | tf_op jit(solution)/shard_map/pallas_call | solution.py:569
  1052.1 12.2 %collective-permute-done.116.rc = f32[128,2048]{1,0:T(8,128)} collective-permute-done((f32[128,2048]{1,0:T(8,128)}, f32[128,2048]{1,0:T(8,128)}, u32[]{:S(2)}, u32[]{:S(2)}) %collective-permute-start.116) | collective-permute-done | bytes 1048608 | tf_op jit(solution)/shard_map/ppermute | solution.py:55
  1064.3 3.3 shard_map.110
  1073.6 32.0 %collective-permute-done.128.uy_ref = f32[2,512,128]{2,1,0:T(8,128)} collective-permute-done((f32[2,512,128]{2,1,0:T(8,128)}, f32[2,512,128]{2,1,0:T(8,128)}, u32[]{:S(2)}, u32[]{:S(2)}) %collective-permute-start.128) | collective-permute-done | bytes 524320 | tf_op jit(solution)/shard_map/ppermute | solution.py:67
  1120.1 3.4 shard_map.116
  1123.5 31.0 %collective-permute-done.123.uc_ref = f32[2,512,128]{2,1,0:T(8,128)} collective-permute-done((f32[2,512,128]{2,1,0:T(8,128)}, f32[2,512,128]{2,1,0:T(8,128)}, u32[]{:S(2)}, u32[]{:S(2)}) %collective-permute-start.123) | collective-permute-done | bytes 524320 | tf_op jit(solution)/shard_map/ppermute | solution.py:63
  1159.7 3.3 shard_map.118
  1162.9 35.9 %collective-permute-done.119.uc_ref = f32[2,512,128]{2,1,0:T(8,128)S(1)} collective-permute-done((f32[2,512,128]{2,1,0:T(8,128)S(1)}, f32[2,512,128]{2,1,0:T(8,128)S(1)}, u32[]{:S(2)}, u32[]{:S(2)}) %collective-permute-start.119) | collective-permute-done | bytes 524320 | tf_op jit(solution)/shard_map/ppermute | solution.py:63
  (267 shorter events, 146.6 us)
Async XLA Ops:
  27.2 140.4 %collective-permute-start.70 = (bf16[2,2432,2048]{2,1,0:T(8,128)(2,1)}, bf16[2,2432,2048]{2,1,0:T(8,128)(2,1)}, u32[]{:S(2)}, u32[]{:S(2)}) collective-permute-start(bf16[2,2432,2048]{2,1,0:T(8,128)(2,1)} %pack_rest.1.own_ref.refs_2_.refs_14_), channel_id=1, source_target_pairs={{0,1},{1,0},{2,3},{3,2},{4,5},{5,4},{6,7},{7,6}} | collective-permute-start | bytes 59768840 | tf_op jit(solution)/shard_map/ppermute | solution.py:51
  27.2 138.2 %collective-permute-start.73 = (bf16[2,768,2048]{2,1,0:T(8,128)(2,1)}, bf16[2,768,2048]{2,1,0:T(8,128)(2,1)}, u32[]{:S(2)}, u32[]{:S(2)}) collective-permute-start(bf16[2,768,2048]{2,1,0:T(8,128)(2,1)} %bitcast.104), channel_id=1, source_target_pairs={{0,4},{4,0},{1,5},{5,1},{2,6},{6,2},{3,7},{7,3}} | collective-permute-start | bytes 18874376 | tf_op jit(solution)/shard_map/ppermute | solution.py:63
  28.5 139.1 %collective-permute-start.72 = (bf16[2,768,2048]{2,1,0:T(8,128)(2,1)}, bf16[2,768,2048]{2,1,0:T(8,128)(2,1)}, u32[]{:S(2)}, u32[]{:S(2)}) collective-permute-start(bf16[2,768,2048]{2,1,0:T(8,128)(2,1)} %bitcast.105), channel_id=1, source_target_pairs={{0,1},{1,0},{2,3},{3,2},{4,5},{5,4},{6,7},{7,6}} | collective-permute-start | bytes 18874376 | tf_op jit(solution)/shard_map/ppermute | solution.py:51
  37.9 56.1 %collective-permute-start.75 = (bf16[2,512,1024]{2,1,0:T(8,128)(2,1)}, bf16[2,512,1024]{2,1,0:T(8,128)(2,1)S(1)}, u32[]{:S(2)}, u32[]{:S(2)}) collective-permute-start(bf16[2,512,1024]{2,1,0:T(8,128)(2,1)} %pad_maximum_fusion), channel_id=1, source_target_pairs={{0,1},{1,0},{2,3},{3,2},{4,5},{5,4},{6,7},{7,6}} | collective-permute-start | bytes 6291464 | tf_op jit(solution)/shard_map/ppermute | solution.py:51
  92.4 121.3 %collective-permute-start.76 = (bf16[2,512,256]{2,1,0:T(8,128)(2,1)}, bf16[2,512,256]{2,1,0:T(8,128)(2,1)}, u32[]{:S(2)}, u32[]{:S(2)}) collective-permute-start(bf16[2,512,256]{2,1,0:T(8,128)(2,1)} %pad_maximum_fusion.3), channel_id=1, source_target_pairs={{0,2},{2,0},{1,3},{3,1},{4,6},{6,4},{5,7},{7,5}} | collective-permute-start | bytes 1572872 | tf_op jit(solution)/shard_map/ppermute | solution.py:55
  94.0 119.7 %collective-permute-start.77 = (bf16[2,512,256]{2,1,0:T(8,128)(2,1)}, bf16[2,512,256]{2,1,0:T(8,128)(2,1)}, u32[]{:S(2)}, u32[]{:S(2)}) collective-permute-start(bf16[2,512,256]{2,1,0:T(8,128)(2,1)} %pad_maximum_fusion.4), channel_id=1, source_target_pairs={{0,3},{3,0},{1,2},{2,1},{4,7},{7,4},{5,6},{6,5}} | collective-permute-start | bytes 1572872 | tf_op jit(solution)/shard_map/ppermute | solution.py:59
  165.5 84.5 %collective-permute-start.79 = (bf16[2,512,512]{2,1,0:T(8,128)(2,1)}, bf16[2,512,512]{2,1,0:T(8,128)(2,1)}, u32[]{:S(2)}, u32[]{:S(2)}) collective-permute-start(bf16[2,512,512]{2,1,0:T(8,128)(2,1)} %pad_maximum_fusion.1), channel_id=1, source_target_pairs={{0,2},{2,0},{1,3},{3,1},{4,6},{6,4},{5,7},{7,5}} | collective-permute-start | bytes 3145736 | tf_op jit(solution)/shard_map/ppermute | solution.py:55
  167.6 48.2 %collective-permute-start.78 = (bf16[256,2048]{1,0:T(8,128)(2,1)}, bf16[256,2048]{1,0:T(8,128)(2,1)S(1)}, u32[]{:S(2)}, u32[]{:S(2)}) collective-permute-start(bf16[256,2048]{1,0:T(8,128)(2,1)} %get-tuple-element.991), channel_id=1, source_target_pairs={{0,2},{2,0},{1,3},{3,1},{4,6},{6,4},{5,7},{7,5}} | collective-permute-start | bytes 3145736 | tf_op jit(solution)/shard_map/ppermute | solution.py:55
  167.6 116.8 %collective-permute-start.74 = (bf16[2,768,2048]{2,1,0:T(8,128)(2,1)}, bf16[2,768,2048]{2,1,0:T(8,128)(2,1)}, u32[]{:S(2)}, u32[]{:S(2)}) collective-permute-start(bf16[2,768,2048]{2,1,0:T(8,128)(2,1)} %collective-permute-done.73), channel_id=1, source_target_pairs={{0,1},{1,0},{2,3},{3,2},{4,5},{5,4},{6,7},{7,6}} | collective-permute-start | bytes 18874376 | tf_op jit(solution)/shard_map/ppermute | solution.py:51
  213.7 70.7 %collective-permute-start.81 = (bf16[512,2048]{1,0:T(8,128)(2,1)}, bf16[512,2048]{1,0:T(8,128)(2,1)}, u32[]{:S(2)}, u32[]{:S(2)}) collective-permute-start(bf16[512,2048]{1,0:T(8,128)(2,1)} %dynamic-slice_bitcast_fusion), channel_id=1, source_target_pairs={{0,2},{2,0},{1,3},{3,1},{4,6},{6,4},{5,7},{7,5}} | collective-permute-start | bytes 6291464 | tf_op jit(solution)/shard_map/ppermute | solution.py:55
  295.3 47.3 %collective-permute-start.24 = (bf16[2,256,2048]{2,1,0:T(8,128)(2,1)}, bf16[2,256,2048]{2,1,0:T(8,128)(2,1)}, u32[]{:S(2)}, u32[]{:S(2)}) collective-permute-start(bf16[2,256,2048]{2,1,0:T(8,128)(2,1)} %get-tuple-element.584), channel_id=1, source_target_pairs={{0,2},{2,0},{1,3},{3,1},{4,6},{6,4},{5,7},{7,5}} | collective-permute-start | bytes 6291464 | tf_op jit(solution)/shard_map/cond/branch_3_fun/ppermute | solution.py:55
  295.7 179.9 %collective-permute-start.23 = (bf16[2,384,2048]{2,1,0:T(8,128)(2,1)}, bf16[2,384,2048]{2,1,0:T(8,128)(2,1)}, u32[]{:S(2)}, u32[]{:S(2)}) collective-permute-start(bf16[2,384,2048]{2,1,0:T(8,128)(2,1)} %get-tuple-element.581), channel_id=1, source_target_pairs={{0,4},{4,0},{1,5},{5,1},{2,6},{6,2},{3,7},{7,3}} | collective-permute-start | bytes 9437192 | tf_op jit(solution)/shard_map/cond/branch_3_fun/ppermute | solution.py:63
  302.4 203.0 %collective-permute-start.22 = (bf16[2,512,2048]{2,1,0:T(8,128)(2,1)}, bf16[2,512,2048]{2,1,0:T(8,128)(2,1)}, u32[]{:S(2)}, u32[]{:S(2)}) collective-permute-start(bf16[2,512,2048]{2,1,0:T(8,128)(2,1)} %get-tuple-element.580), channel_id=1, source_target_pairs={{0,4},{4,0},{1,5},{5,1},{2,6},{6,2},{3,7},{7,3}} | collective-permute-start | bytes 12582920 | tf_op jit(solution)/shard_map/cond/branch_3_fun/ppermute | solution.py:63
  343.2 162.1 %collective-permute-start.25 = (bf16[2,256,2048]{2,1,0:T(8,128)(2,1)}, bf16[2,256,2048]{2,1,0:T(8,128)(2,1)}, u32[]{:S(2)}, u32[]{:S(2)}) collective-permute-start(bf16[2,256,2048]{2,1,0:T(8,128)(2,1)} %append.11), channel_id=1, source_target_pairs={{0,4},{4,0},{1,5},{5,1},{2,6},{6,2},{3,7},{7,3}} | collective-permute-start | bytes 6291464 | tf_op jit(solution)/shard_map/cond/branch_3_fun/ppermute | solution.py:63
  475.6 91.3 %collective-permute-start.29 = (bf16[2,256,2048]{2,1,0:T(8,128)(2,1)}, bf16[2,256,2048]{2,1,0:T(8,128)(2,1)}, u32[]{:S(2)}, u32[]{:S(2)}) collective-permute-start(bf16[2,256,2048]{2,1,0:T(8,128)(2,1)} %collective-permute-done.24.given_ref), channel_id=1, source_target_pairs={{0,1},{1,0},{2,3},{3,2},{4,5},{5,4},{6,7},{7,6}} | collective-permute-start | bytes 6291464 | tf_op jit(solution)/shard_map/cond/branch_3_fun/ppermute | solution.py:51
  475.6 91.3 %collective-permute-start.27 = (bf16[2,384,2048]{2,1,0:T(8,128)(2,1)}, bf16[2,384,2048]{2,1,0:T(8,128)(2,1)}, u32[]{:S(2)}, u32[]{:S(2)}) collective-permute-start(bf16[2,384,2048]{2,1,0:T(8,128)(2,1)} %collective-permute-done.23), channel_id=1, source_target_pairs={{0,1},{1,0},{2,3},{3,2},{4,5},{5,4},{6,7},{7,6}} | collective-permute-start | bytes 9437192 | tf_op jit(solution)/shard_map/cond/branch_3_fun/ppermute | solution.py:51
  505.4 61.5 %collective-permute-start.28 = (bf16[2,256,2048]{2,1,0:T(8,128)(2,1)}, bf16[2,256,2048]{2,1,0:T(8,128)(2,1)}, u32[]{:S(2)}, u32[]{:S(2)}) collective-permute-start(bf16[2,256,2048]{2,1,0:T(8,128)(2,1)} %collective-permute-done.25), channel_id=1, source_target_pairs={{0,1},{1,0},{2,3},{3,2},{4,5},{5,4},{6,7},{7,6}} | collective-permute-start | bytes 6291464 | tf_op jit(solution)/shard_map/cond/branch_3_fun/ppermute | solution.py:51
  505.4 61.6 %collective-permute-start.26 = (bf16[2,512,2048]{2,1,0:T(8,128)(2,1)}, bf16[2,512,2048]{2,1,0:T(8,128)(2,1)}, u32[]{:S(2)}, u32[]{:S(2)}) collective-permute-start(bf16[2,512,2048]{2,1,0:T(8,128)(2,1)} %collective-permute-done.22), channel_id=1, source_target_pairs={{0,1},{1,0},{2,3},{3,2},{4,5},{5,4},{6,7},{7,6}} | collective-permute-start | bytes 12582920 | tf_op jit(solution)/shard_map/cond/branch_3_fun/ppermute | solution.py:51
  579.9 75.2 %collective-permute-start.71 = (bf16[2,384,2048]{2,1,0:T(8,128)(2,1)}, bf16[2,384,2048]{2,1,0:T(8,128)(2,1)S(1)}, u32[]{:S(2)}, u32[]{:S(2)}) collective-permute-start(bf16[2,384,2048]{2,1,0:T(8,128)(2,1)} %get-tuple-element.869), channel_id=1, source_target_pairs={{0,4},{4,0},{1,5},{5,1},{2,6},{6,2},{3,7},{7,3}} | collective-permute-start | bytes 9437192 | tf_op jit(solution)/shard_map/ppermute | solution.py:63
  708.6 46.8 %collective-permute-start.87 = (f32[128,2048]{1,0:T(8,128)}, f32[128,2048]{1,0:T(8,128)}, u32[]{:S(2)}, u32[]{:S(2)}) collective-permute-start(f32[128,2048]{1,0:T(8,128)} %get-tuple-element.900), channel_id=1, source_target_pairs={{0,2},{2,0},{1,3},{3,1},{4,6},{6,4},{5,7},{7,5}} | collective-permute-start | bytes 3145736 | tf_op jit(solution)/shard_map/ppermute | solution.py:55
  708.7 68.7 %collective-permute-start.86 = (f32[128,2048]{1,0:T(8,128)}, f32[128,2048]{1,0:T(8,128)S(1)}, u32[]{:S(2)}, u32[]{:S(2)}) collective-permute-start(f32[128,2048]{1,0:T(8,128)} %get-tuple-element.898), channel_id=1, source_target_pairs={{0,2},{2,0},{1,3},{3,1},{4,6},{6,4},{5,7},{7,5}} | collective-permute-start | bytes 3145736 | tf_op jit(solution)/shard_map/ppermute | solution.py:55
  736.9 95.2 %collective-permute-start.96 = (f32[2,512,128]{2,1,0:T(8,128)}, f32[2,512,128]{2,1,0:T(8,128)S(1)}, u32[]{:S(2)}, u32[]{:S(2)}) collective-permute-start(f32[2,512,128]{2,1,0:T(8,128)} %get-tuple-element.919), channel_id=1, source_target_pairs={{0,1},{1,0},{2,3},{3,2},{4,5},{5,4},{6,7},{7,6}} | collective-permute-start | bytes 1572872 | tf_op jit(solution)/shard_map/ppermute | solution.py:51
  737.0 96.6 %collective-permute-start.95 = (f32[2,512,128]{2,1,0:T(8,128)}, f32[2,512,128]{2,1,0:T(8,128)S(1)}, u32[]{:S(2)}, u32[]{:S(2)}) collective-permute-start(f32[2,512,128]{2,1,0:T(8,128)} %get-tuple-element.919), channel_id=1, source_target_pairs={{0,5},{1,4},{2,7},{3,6},{4,1},{5,0},{6,3},{7,2}} | collective-permute-start | bytes 1572872 | tf_op jit(solution)/shard_map/ppermute | solution.py:67
  737.0 94.5 %collective-permute-start.94 = (f32[2,512,128]{2,1,0:T(8,128)}, f32[2,512,128]{2,1,0:T(8,128)S(1)}, u32[]{:S(2)}, u32[]{:S(2)}) collective-permute-start(f32[2,512,128]{2,1,0:T(8,128)} %get-tuple-element.918), channel_id=1, source_target_pairs={{0,4},{4,0},{1,5},{5,1},{2,6},{6,2},{3,7},{7,3}} | collective-permute-start | bytes 1572872 | tf_op jit(solution)/shard_map/ppermute | solution.py:63
  781.4 135.1 %collective-permute-start.91 = (f32[128,2048]{1,0:T(8,128)}, f32[128,2048]{1,0:T(8,128)S(1)}, u32[]{:S(2)}, u32[]{:S(2)}) collective-permute-start(f32[128,2048]{1,0:T(8,128)} %get-tuple-element.902.refs_23_), channel_id=1, source_target_pairs={{0,4},{4,0},{1,5},{5,1},{2,6},{6,2},{3,7},{7,3}} | collective-permute-start | bytes 3145736 | tf_op jit(solution)/shard_map/ppermute | solution.py:63
  832.2 48.1 %collective-permute-start.102 = (f32[128,2048]{1,0:T(8,128)}, f32[128,2048]{1,0:T(8,128)}, u32[]{:S(2)}, u32[]{:S(2)}) collective-permute-start(f32[128,2048]{1,0:T(8,128)} %get-tuple-element.927), channel_id=1, source_target_pairs={{0,2},{2,0},{1,3},{3,1},{4,6},{6,4},{5,7},{7,5}} | collective-permute-start | bytes 3145736 | tf_op jit(solution)/shard_map/ppermute | solution.py:55
  833.5 69.2 %collective-permute-start.103 = (f32[128,2048]{1,0:T(8,128)}, f32[128,2048]{1,0:T(8,128)}, u32[]{:S(2)}, u32[]{:S(2)}) collective-permute-start(f32[128,2048]{1,0:T(8,128)} %get-tuple-element.929), channel_id=1, source_target_pairs={{0,2},{2,0},{1,3},{3,1},{4,6},{6,4},{5,7},{7,5}} | collective-permute-start | bytes 3145736 | tf_op jit(solution)/shard_map/ppermute | solution.py:55
  856.4 62.5 %collective-permute-start.98 = (f32[128,2048]{1,0:T(8,128)}, f32[128,2048]{1,0:T(8,128)S(1)}, u32[]{:S(2)}, u32[]{:S(2)}) collective-permute-start(f32[128,2048]{1,0:T(8,128)} %get-tuple-element.905.refs_23_), channel_id=1, source_target_pairs={{0,4},{4,0},{1,5},{5,1},{2,6},{6,2},{3,7},{7,3}} | collective-permute-start | bytes 3145736 | tf_op jit(solution)/shard_map/ppermute | solution.py:63
  857.8 65.3 %collective-permute-start.97 = (f32[128,2048]{1,0:T(8,128)}, f32[128,2048]{1,0:T(8,128)}, u32[]{:S(2)}, u32[]{:S(2)}) collective-permute-start(f32[128,2048]{1,0:T(8,128)} %get-tuple-element.922), channel_id=1, source_target_pairs={{0,2},{2,0},{1,3},{3,1},{4,6},{6,4},{5,7},{7,5}} | collective-permute-start | bytes 3145736 | tf_op jit(solution)/shard_map/ppermute | solution.py:55
  912.7 40.7 %collective-permute-start.109 = (f32[2,512,128]{2,1,0:T(8,128)}, f32[2,512,128]{2,1,0:T(8,128)S(1)}, u32[]{:S(2)}, u32[]{:S(2)}) collective-permute-start(f32[2,512,128]{2,1,0:T(8,128)} %get-tuple-element.944), channel_id=1, source_target_pairs={{0,1},{1,0},{2,3},{3,2},{4,5},{5,4},{6,7},{7,6}} | collective-permute-start | bytes 1572872 | tf_op jit(solution)/shard_map/ppermute | solution.py:51
  953.4 62.1 %collective-permute-start.106 = (f32[128,2048]{1,0:T(8,128)}, f32[128,2048]{1,0:T(8,128)S(1)}, u32[]{:S(2)}, u32[]{:S(2)}) collective-permute-start(f32[128,2048]{1,0:T(8,128)} %get-tuple-element.910.refs_23_), channel_id=1, source_target_pairs={{0,4},{4,0},{1,5},{5,1},{2,6},{6,2},{3,7},{7,3}} | collective-permute-start | bytes 3145736 | tf_op jit(solution)/shard_map/ppermute | solution.py:63
  953.4 63.8 %collective-permute-start.111 = (f32[128,2048]{1,0:T(8,128)}, f32[128,2048]{1,0:T(8,128)S(1)}, u32[]{:S(2)}, u32[]{:S(2)}) collective-permute-start(f32[128,2048]{1,0:T(8,128)} %get-tuple-element.920.refs_23_), channel_id=1, source_target_pairs={{0,4},{4,0},{1,5},{5,1},{2,6},{6,2},{3,7},{7,3}} | collective-permute-start | bytes 3145736 | tf_op jit(solution)/shard_map/ppermute | solution.py:63
  957.2 46.6 %collective-permute-start.115 = (f32[128,2048]{1,0:T(8,128)}, f32[128,2048]{1,0:T(8,128)}, u32[]{:S(2)}, u32[]{:S(2)}) collective-permute-start(f32[128,2048]{1,0:T(8,128)} %get-tuple-element.952), channel_id=1, source_target_pairs={{0,2},{2,0},{1,3},{3,1},{4,6},{6,4},{5,7},{7,5}} | collective-permute-start | bytes 3145736 | tf_op jit(solution)/shard_map/ppermute | solution.py:55
  983.0 41.1 %collective-permute-start.131 = (f32[2,512,128]{2,1,0:T(8,128)}, f32[2,512,128]{2,1,0:T(8,128)}, u32[]{:S(2)}, u32[]{:S(2)}) collective-permute-start(f32[2,512,128]{2,1,0:T(8,128)} %get-tuple-element.973), channel_id=1, source_target_pairs={{0,4},{4,0},{1,5},{5,1},{2,6},{6,2},{3,7},{7,3}} | collective-permute-start | bytes 1572872 | tf_op jit(solution)/shard_map/ppermute | solution.py:63
  1017.2 47.1 %collective-permute-start.116 = (f32[128,2048]{1,0:T(8,128)}, f32[128,2048]{1,0:T(8,128)}, u32[]{:S(2)}, u32[]{:S(2)}) collective-permute-start(f32[128,2048]{1,0:T(8,128)} %get-tuple-element.958), channel_id=1, source_target_pairs={{0,2},{2,0},{1,3},{3,1},{4,6},{6,4},{5,7},{7,5}} | collective-permute-start | bytes 3145736 | tf_op jit(solution)/shard_map/ppermute | solution.py:55
  1046.4 63.9 %collective-permute-start.130 = (f32[128,2048]{1,0:T(8,128)}, f32[128,2048]{1,0:T(8,128)}, u32[]{:S(2)}, u32[]{:S(2)}) collective-permute-start(f32[128,2048]{1,0:T(8,128)} %get-tuple-element.945.refs_23_), channel_id=1, source_target_pairs={{0,4},{4,0},{1,5},{5,1},{2,6},{6,2},{3,7},{7,3}} | collective-permute-start | bytes 3145736 | tf_op jit(solution)/shard_map/ppermute | solution.py:63
  1047.2 63.1 %collective-permute-start.105 = (f32[128,2048]{1,0:T(8,128)}, f32[128,2048]{1,0:T(8,128)}, u32[]{:S(2)}, u32[]{:S(2)}) collective-permute-start(f32[128,2048]{1,0:T(8,128)} %get-tuple-element.942), channel_id=1, source_target_pairs={{0,2},{2,0},{1,3},{3,1},{4,6},{6,4},{5,7},{7,5}} | collective-permute-start | bytes 3145736 | tf_op jit(solution)/shard_map/ppermute | solution.py:55
  1049.8 62.1 %collective-permute-start.118 = (f32[128,2048]{1,0:T(8,128)}, f32[128,2048]{1,0:T(8,128)}, u32[]{:S(2)}, u32[]{:S(2)}) collective-permute-start(f32[128,2048]{1,0:T(8,128)} %get-tuple-element.964), channel_id=1, source_target_pairs={{0,2},{2,0},{1,3},{3,1},{4,6},{6,4},{5,7},{7,5}} | collective-permute-start | bytes 3145736 | tf_op jit(solution)/shard_map/ppermute | solution.py:55
  1050.1 65.4 %collective-permute-start.126 = (f32[128,2048]{1,0:T(8,128)}, f32[128,2048]{1,0:T(8,128)S(1)}, u32[]{:S(2)}, u32[]{:S(2)}) collective-permute-start(f32[128,2048]{1,0:T(8,128)} %get-tuple-element.940.refs_23_), channel_id=1, source_target_pairs={{0,4},{4,0},{1,5},{5,1},{2,6},{6,2},{3,7},{7,3}} | collective-permute-start | bytes 3145736 | tf_op jit(solution)/shard_map/ppermute | solution.py:63
  1064.3 41.4 %collective-permute-start.128 = (f32[2,512,128]{2,1,0:T(8,128)}, f32[2,512,128]{2,1,0:T(8,128)}, u32[]{:S(2)}, u32[]{:S(2)}) collective-permute-start(f32[2,512,128]{2,1,0:T(8,128)} %get-tuple-element.972), channel_id=1, source_target_pairs={{0,5},{1,4},{2,7},{3,6},{4,1},{5,0},{6,3},{7,2}} | collective-permute-start | bytes 1572872 | tf_op jit(solution)/shard_map/ppermute | solution.py:67
  1105.7 54.0 %collective-permute-start.122 = (f32[128,2048]{1,0:T(8,128)}, f32[128,2048]{1,0:T(8,128)S(1)}, u32[]{:S(2)}, u32[]{:S(2)}) collective-permute-start(f32[128,2048]{1,0:T(8,128)} %get-tuple-element.968), channel_id=1, source_target_pairs={{0,4},{4,0},{1,5},{5,1},{2,6},{6,2},{3,7},{7,3}} | collective-permute-start | bytes 3145736 | tf_op jit(solution)/shard_map/ppermute | solution.py:63
  1110.3 44.2 %collective-permute-start.125 = (f32[2,512,128]{2,1,0:T(8,128)}, f32[2,512,128]{2,1,0:T(8,128)S(1)}, u32[]{:S(2)}, u32[]{:S(2)}) collective-permute-start(f32[2,512,128]{2,1,0:T(8,128)} %get-tuple-element.970), channel_id=1, source_target_pairs={{0,1},{1,0},{2,3},{3,2},{4,5},{5,4},{6,7},{7,6}} | collective-permute-start | bytes 1572872 | tf_op jit(solution)/shard_map/ppermute | solution.py:51
  1110.4 44.8 %collective-permute-start.124 = (f32[2,512,128]{2,1,0:T(8,128)}, f32[2,512,128]{2,1,0:T(8,128)}, u32[]{:S(2)}, u32[]{:S(2)}) collective-permute-start(f32[2,512,128]{2,1,0:T(8,128)} %get-tuple-element.970), channel_id=1, source_target_pairs={{0,5},{1,4},{2,7},{3,6},{4,1},{5,0},{6,3},{7,2}} | collective-permute-start | bytes 1572872 | tf_op jit(solution)/shard_map/ppermute | solution.py:67
  1111.9 42.6 %collective-permute-start.123 = (f32[2,512,128]{2,1,0:T(8,128)}, f32[2,512,128]{2,1,0:T(8,128)}, u32[]{:S(2)}, u32[]{:S(2)}) collective-permute-start(f32[2,512,128]{2,1,0:T(8,128)} %get-tuple-element.969), channel_id=1, source_target_pairs={{0,4},{4,0},{1,5},{5,1},{2,6},{6,2},{3,7},{7,3}} | collective-permute-start | bytes 1572872 | tf_op jit(solution)/shard_map/ppermute | solution.py:63
  1115.5 83.4 %collective-permute-start.117 = (f32[128,2048]{1,0:T(8,128)}, f32[128,2048]{1,0:T(8,128)S(1)}, u32[]{:S(2)}, u32[]{:S(2)}) collective-permute-start(f32[128,2048]{1,0:T(8,128)} %get-tuple-element.962), channel_id=1, source_target_pairs={{0,4},{4,0},{1,5},{5,1},{2,6},{6,2},{3,7},{7,3}} | collective-permute-start | bytes 3145736 | tf_op jit(solution)/shard_map/ppermute | solution.py:63
  1154.5 44.4 %collective-permute-start.121 = (f32[2,512,128]{2,1,0:T(8,128)S(1)}, f32[2,512,128]{2,1,0:T(8,128)S(1)}, u32[]{:S(2)}, u32[]{:S(2)}) collective-permute-start(f32[2,512,128]{2,1,0:T(8,128)S(1)} %copy-done.36), channel_id=1, source_target_pairs={{0,1},{1,0},{2,3},{3,2},{4,5},{5,4},{6,7},{7,6}} | collective-permute-start | bytes 1572872 | tf_op jit(solution)/shard_map/ppermute | solution.py:51
  1154.5 44.4 %collective-permute-start.120 = (f32[2,512,128]{2,1,0:T(8,128)S(1)}, f32[2,512,128]{2,1,0:T(8,128)S(1)}, u32[]{:S(2)}, u32[]{:S(2)}) collective-permute-start(f32[2,512,128]{2,1,0:T(8,128)S(1)} %copy-done.36), channel_id=1, source_target_pairs={{0,5},{1,4},{2,7},{3,6},{4,1},{5,0},{6,3},{7,2}} | collective-permute-start | bytes 1572872 | tf_op jit(solution)/shard_map/ppermute | solution.py:67
  1155.2 43.7 %collective-permute-start.119 = (f32[2,512,128]{2,1,0:T(8,128)S(1)}, f32[2,512,128]{2,1,0:T(8,128)S(1)}, u32[]{:S(2)}, u32[]{:S(2)}) collective-permute-start(f32[2,512,128]{2,1,0:T(8,128)S(1)} %copy-done.37), channel_id=1, source_target_pairs={{0,4},{4,0},{1,5},{5,1},{2,6},{6,2},{3,7},{7,3}} | collective-permute-start | bytes 1572872 | tf_op jit(solution)/shard_map/ppermute | solution.py:63
  (63 other events, 1577.2 us)

commit v3 on v2

--- a/solution.py
+++ b/solution.py
@@ -17,8 +17,9 @@
 FIRST = 3
 MAIN = (4, 4, 3, 2)
 TAIL = 2
-SIZES = (6, 7, 8, 9, 10, 11, 12, 15)
-PARTS = ((0,), (2, 3), (0, 3), (0, 2), (0, 1), (0, 2, 3), (0, 1, 3), (0, 1, 2, 3))
+SIZES = (15, 12, 6, 11, 10, 7, 9, 8)
+PARTS = ((0, 1, 2, 3), (0, 1, 3), (0,), (0, 2, 3), (0, 1), (2, 3), (0, 2), (0, 3))
+N_TAB, N_LATE = 64, 48
 G = 4
 M = G * TM
 FB = 256
@@ -108,9 +109,9 @@
             outs.append(cp)
         for cp in cps:
             cp.wait()
-        all_ref[0] = len_ref[...]
+        all_ref[0:1, :] = len_ref[0:1, :]
         for k in range(7):
-            all_ref[k + 1] = land[k]
+            all_ref[k + 1 : k + 2, :] = land[k, 0:1, :]
         for cp in outs:
             cp.wait()
 
@@ -118,7 +119,7 @@
         kern,
         in_specs=[VM, ANY, ANY],
         out_specs=[VM, ANY],
-        out_shape=[jax.ShapeDtypeStruct((8, 8, 128), jnp.int32), jax.ShapeDtypeStruct((2, MICRO, BASE, D), BF)],
+        out_shape=[jax.ShapeDtypeStruct((8, 128), jnp.int32), jax.ShapeDtypeStruct((2, MICRO, BASE, D), BF)],
         scratch_shapes=[
             pltpu.VMEM((7, 8, 128), jnp.int32),
             pltpu.VMEM((2, MICRO, BASE, D), BF),
@@ -131,6 +132,110 @@
         cost_estimate=cost(10_000_000_000, 13_000_000),
         name="start",
     )(lens, x_in, dy)
+
+
+def plan(around):
+    names = dict(
+        rest=MICRO, offs=MICRO + 1, send=4 + len(MAIN) + 1, take=1, which=1, tab=N_TAB, own=4, every=4, late=N_LATE,
+        info=3, pos=3,
+    )
+
+    def kern(all_ref, rest_ref, offs_ref, send_ref, take_ref, which_ref, tab_ref, own_ref, every_ref, late_ref, info_ref,
+             pos_ref):
+        y, f = lax.axis_index("replica"), lax.axis_index("fsdp")
+        xi, c = f // 2, lax.rem(f, 2)
+        me = y * 4 + f
+
+        def at(values, i):
+            return sum(jnp.where(i == d, v, 0) for d, v in enumerate(values))
+
+        o = jnp.int32(0)
+        for k in range(MICRO):
+            n = all_ref[0, k] - BASE
+            rest_ref[k], offs_ref[k] = n, o
+            o = o + (n + 15) // 16 * 16
+        offs_ref[MICRO] = o
+        tiles = []
+        for d in range(8):
+            row = lax.rem(me - d + 8, 8)
+            n = sum((all_ref[row, k] - BASE + 15) // 16 * 16 for k in range(MICRO))
+            tiles.append((n + TM - 1) // TM)
+        share = []
+        for q in range(4):
+            both = tiles[2 * q] + tiles[2 * q + 1]
+            share += [(both + 1) // 2, both // 2]
+        keep, take = [], []
+        for d in range(8):
+            gap = share[d] - share[d ^ 2]
+            move = jnp.minimum(jnp.abs(gap) // 2, TAIL)
+            keep.append(share[d] - jnp.where(gap > 0, move, 0))
+            take.append(jnp.where(gap < 0, move, 0))
+        longest = keep[0] + take[0]
+        for d in range(1, 8):
+            longest = jnp.maximum(longest, keep[d] + take[d])
+        order = sorted(range(len(SIZES)), key=lambda k: SIZES[k])
+        rank = sum(jnp.where(longest - FIRST > SIZES[k], 1, 0) for k in order[:-1])
+        which = at(order, rank)
+        table = piece_starts()
+        starts = [at([row[k] for row in table], which) for k in range(len(MAIN) + 1)]
+        end = starts[-1] + TAIL
+        t_own, t_sib = at(tiles, me), at(tiles, me ^ 1)
+        h_own, h_sib = at(share, me), at(share, me ^ 1)
+        k_own, k_sib, k_y, k_ys = (at(keep, me ^ k) for k in (0, 1, 4, 5))
+        x_own, x_sib, x_y, x_ys = (at(take, me ^ k) for k in (0, 1, 4, 5))
+        for k, v in enumerate((h_own, k_own, t_own, t_sib - h_own, *starts)):
+            send_ref[k] = v
+        take_ref[0], which_ref[0] = x_own, which
+
+        n_own = 12 + k_own + k_sib
+        g_own = (n_own + G - 1) // G
+
+        def early_entry(i, _):
+            k, m, n = i - g_own * G, i - 12, i - 12 - k_own
+            e = jnp.where(n < t_sib, 3 * 32 + n, 2 * 32 + n + t_own - h_sib)
+            e = jnp.where(n < 0, jnp.where(m < t_own, 2 * 32 + m, 3 * 32 + m + t_sib - h_own), e)
+            e = jnp.where(i < n_own, e, 2 * 32 + NT)
+            e = jnp.where(i < 6, i, jnp.where(i < 12, 32 + i - 6, e))
+            e = jnp.where(k >= 0, jnp.where(k < 6, 4 * 32 + k, 5 * 32 + k - 6), e)
+            tab_ref[i] = jnp.where(k >= 12, 2 * 32 + NT, e)
+            return 0
+
+        lax.fori_loop(0, N_TAB, early_entry, 0)
+        for k, (a, b) in enumerate(((0, g_own), (g_own, g_own + 3), (y, y), (f, f))):
+            own_ref[k], every_ref[k] = a, b
+
+        n_src = 2 + len(MAIN)
+        l_y, l_ys = k_y + x_y, k_ys + x_ys
+
+        def late_entry(i, _):
+            first = i < l_y
+            t = jnp.where(first, i, i - l_y)
+            listed = jnp.where(first, k_y, k_ys)
+            t = jnp.where(t < listed, t, end - 1 - (t - listed))
+            e = t
+            for n in range(n_src - 1):
+                e = jnp.where(t >= starts[n], (1 + n) * 32 + t - starts[n], e)
+            e = jnp.where(first, e, e + n_src * 32)
+            m = i - l_y - l_ys
+            handed = jnp.where(m < x_own, 2 * n_src * 32 + m, (2 * n_src + 1) * 32 + m - x_own)
+            late_ref[i] = jnp.where(m < 0, e, jnp.where(m < x_own + x_sib, handed, (2 * n_src + 2) * 32 + NT))
+            return 0
+
+        lax.fori_loop(0, N_LATE, late_entry, 0)
+        for k, v in enumerate(((l_y + l_ys + x_own + x_sib + G - 1) // G, y, f)):
+            info_ref[k] = v
+        for k, v in enumerate((y, xi, c)):
+            pos_ref[k] = v
+
+    outs = pl.pallas_call(
+        kern,
+        in_specs=[SM],
+        out_specs=[SM] * len(names),
+        out_shape=[jax.ShapeDtypeStruct((n,), jnp.int32) for n in names.values()],
+        cost_estimate=cost(3_000_000_000, 10_000),
+        name="plan",
+    )(around)
+    return dict(zip(names, outs))
 
 
 def pack_rest(x_in, dy, rest, offs):
@@ -737,12 +842,10 @@
         xi, c = f // 2, f % 2
         w_up, w_down = w_up[0], w_down[0]
 
-        row = jnp.zeros((8, 128), jnp.int32).at[:MICRO, 0].set(lengths[:, 0].astype(jnp.int32))
+        row = jnp.zeros((8, 128), jnp.int32).at[0, :MICRO].set(lengths[:, 0].astype(jnp.int32))
         around, s1 = start(row, x_in, dy)
         s1 = s1.reshape(2, MICRO * BASE, D)
         s1_y = y_swap(s1)
-        me = y * 4 + f
-        lens = around[(me - jnp.arange(8)) % 8][:, :MICRO, 0]
 
         def cols(xd, cd, lo=0, n=HALF):
             own = lax.dynamic_slice(w_up, (0, ((2 * xd + cd) * 2 + y) * HALF + lo), (512, n))
@@ -757,92 +860,38 @@
             d = x_swap(lax.dynamic_slice(w_down, (y * HALF + lo * HB, 0), (n * HB, D)))
             wsets.append((lo, n, [w_up, from_s, a, b, w_down, d]))
 
-        rest = lens - BASE
-        r16 = (rest + 15) // 16 * 16
-        tiles = (jnp.sum(r16, axis=1) + TM - 1) // TM
-        my_rest = lax.dynamic_index_in_dim(rest, me, keepdims=False)
-        my16 = lax.dynamic_index_in_dim(r16, me, keepdims=False)
-        offs = jnp.concatenate([jnp.zeros((1,), jnp.int32), jnp.cumsum(my16)])
-        both = tiles[0::2] + tiles[1::2]
-        share = jnp.stack([(both + 1) // 2, both // 2], axis=1).reshape(8)
-        gap = share - share[jnp.arange(8) ^ 2]
-        move = jnp.minimum(jnp.abs(gap) // 2, TAIL)
-        keep = share - jnp.where(gap > 0, move, 0)
-        take = jnp.where(gap < 0, move, 0)
-        which = jnp.sum(jnp.max(keep + take) - FIRST > jnp.array(SIZES[:-1]))
-        starts = jnp.array(piece_starts())[which]
-        end = starts[-1] + TAIL
-
-        def at(v, i):
-            return lax.dynamic_index_in_dim(v, i, keepdims=False)
-
-        t_own, t_sib = at(tiles, me), at(tiles, me ^ 1)
-        h_own, h_sib = at(share, me), at(share, me ^ 1)
-        k_own, k_sib, k_y, k_ys = (at(keep, me ^ k) for k in (0, 1, 4, 5))
-        x_own, x_sib, x_y, x_ys = (at(take, me ^ k) for k in (0, 1, 4, 5))
-
-        packed = pack_rest(x_in, dy, my_rest, offs)
+        todo = plan(around)
+        packed = pack_rest(x_in, dy, todo["rest"], todo["offs"])
         packed_s = core_swap(packed)
         s1_s = core_swap(s1)
-        pa, *pieces, tail, give = build_send(
-            packed, packed_s,
-            jnp.concatenate([jnp.stack([h_own, k_own, t_own, t_sib - h_own]), starts]).astype(jnp.int32),
-        )
+        pa, *pieces, tail, give = build_send(packed, packed_s, todo["send"])
         qa = y_swap(pa)
 
-        i = jnp.arange(64)
-        n_own = 12 + k_own + k_sib
-        g_own = (n_own + G - 1) // G
-        k = i - g_own * G
-        m, n = i - 12, i - 12 - k_own
-        tab = jnp.where(n < t_sib, 3 * 32 + n, 2 * 32 + n + t_own - h_sib)
-        tab = jnp.where(n < 0, jnp.where(m < t_own, 2 * 32 + m, 3 * 32 + m + t_sib - h_own), tab)
-        tab = jnp.where(i < n_own, tab, 2 * 32 + NT)
-        tab = jnp.where(i < 12, (i // 6) * 32 + i % 6, tab)
-        tab = jnp.where((k >= 0) & (k < 12), (4 + k // 6) * 32 + k % 6, tab).astype(jnp.int32)
-        info_own = jnp.stack([0, g_own, y, f]).astype(jnp.int32)
-        info_all = jnp.stack([g_own, g_own + 3, y, f]).astype(jnp.int32)
-
-        n_src = 2 + len(MAIN)
-        l_y, l_ys = k_y + x_y, k_ys + x_ys
-        i = jnp.arange(48)
-        first = i < l_y
-        t = jnp.where(first, i, i - l_y)
-        listed = jnp.where(first, k_y, k_ys)
-        t = jnp.where(t < listed, t, end - 1 - (t - listed))
-        late = t
-        for n in range(n_src - 1):
-            late = jnp.where(t >= starts[n], (1 + n) * 32 + t - starts[n], late)
-        late = jnp.where(first, late, late + n_src * 32)
-        m = i - l_y - l_ys
-        handed = jnp.where(m < x_own, 2 * n_src * 32 + m, (2 * n_src + 1) * 32 + m - x_own)
-        late = jnp.where(m < 0, late, jnp.where(m < x_own + x_sib, handed, (2 * n_src + 2) * 32 + NT)).astype(jnp.int32)
-        info_late = jnp.stack([(l_y + l_ys + x_own + x_sib + G - 1) // G, y, f]).astype(jnp.int32)
-        pos = jnp.stack([y, xi, c]).astype(jnp.int32)
-
         own_srcs = (s1, s1_s, packed, packed_s)
-        acc0 = early_grads(tab, info_own, own_srcs, wsets[:1], 0, 2)
-        acc1 = early_grads(tab, info_own, own_srcs, wsets[1:2], 2, 1, (), (late, info_late, pos))
+        tab, late, info_late, pos = (todo[k] for k in ("tab", "late", "info", "pos"))
+        acc0 = early_grads(tab, todo["own"], own_srcs, wsets[:1], 0, 2)
+        acc1 = early_grads(tab, todo["own"], own_srcs, wsets[1:2], 2, 1)
         s1_ys = core_swap(s1_y)
         srcs = (*own_srcs, s1_y, s1_ys)
+        acc2 = early_grads(tab, todo["every"], srcs, wsets[1:2], 3, 1)
 
         def early(step, tab, info, srcs, w, prior):
             sets = [(lo, n, v) for (lo, n), v in zip(WSETS, w)]
             if step == 0:
-                return early_grads(tab, info, srcs, sets[1:], 3, 2)
-            return early_grads(tab, info, srcs, sets, 5, 3, prior)
+                return early_grads(tab, info, srcs, sets[2:], 4, 2)
+            return early_grads(tab, info, srcs, sets, 6, 2, prior)
 
         got = lax.switch(
-            which,
+            todo["which"][0],
             [exchange_branch(parts, early) for parts in PARTS],
-            pieces, tail, give, x_own.reshape(1).astype(jnp.int32),
-            tab, info_all, srcs, [w for _, _, w in wsets], [list(acc0), list(acc1)],
+            pieces, tail, give, todo["take"],
+            tab, todo["every"], srcs, [w for _, _, w in wsets], [list(acc0), list(acc1)],
         )
         k = len(MAIN) + 1
         pieces, sib_pieces, given, acc3, acc4 = got[:k], got[k : 2 * k], got[2 * k : 2 * k + 2], got[-4:-2], got[-2:]
         qas = core_swap(qa)
         srcs = (qa, *pieces, qas, *sib_pieces, *given, packed)
-        prior = [(acc4, 3), (acc4, 4), (acc4, 5), (acc3, 0), (acc3, 1), (acc4, 0), (acc4, 1), (acc4, 2)]
+        prior = [(acc4, 2), (acc4, 3), (acc4, 4), (acc2, 0), (acc3, 0), (acc3, 1), (acc4, 0), (acc4, 1)]
 
         out_d = out_u = None
         fin = []
@@ -856,13 +905,13 @@
             recv_u = x_swap(send_u)
             out_d, fd = finish_down(j, pos, keep_d, recv_d, out_d)
             rd = y_swap(fd)
+            if p >= LAG:
+                out_d, out_u = store(ORDER[p - LAG], pos, *fin[p - LAG][1], (out_d, out_u))
             out_u, fuc, fus = finish_up(j, pos, keep_u, recv_u, out_u)
             ruc = y_swap(fuc)
             ruy = y_diag(fus)
             rus = core_swap(fus)
-            fin.append((fd, (rd, ruc, ruy, rus)))
-            if p >= LAG:
-                out_d, out_u = store(ORDER[p - LAG], pos, *fin[p - LAG][1], (out_d, out_u))
+            fin.append((fuc, (rd, ruc, ruy, rus)))
         for p in range(NCH - LAG, NCH):
             out_d, out_u = store(ORDER[p], pos, *fin[p][1], (out_d, out_u))
         return out_u[None], out_d[None]

time: 1210 us -> 1270 us (1.050)
  waiting for transfers between devices: 502 us -> 589 us
  other arithmetic: 20.5 us -> 7.39 us
    ppermute x21, waiting for transfers between devices: 243 us -> 324 us  [y_swap(): return lax.ppermute(v, 'replica', YSWAP)]
    pallas_call x4 -> x5, Pallas kernels: 258 us -> 262 us  [early_grads(): pl.pallas_call(kern, in_specs=[SM, SM] + [ANY] * (ns + len(flat) + len(pr...]
  transfers between devices with their start and end apart: 72 -> 72, of which waited for: 22 -> 25; matrix products, arithmetic and copies ran while one was open for 3% -> 2% of each run, Pallas kernels for 41% -> 39%
where the time goes in v3:
time: 1270 us; the launch traced here: 1260 us
  waiting for transfers between devices  589 us (46%)
  Pallas kernels  546 us (43%)
  starting transfers between devices  69.5 us (5%)
  local copies, waits for them, and re-layouts  25.4 us (2%)
  loops' own time  24.1 us (2%)
    ppermute x21, waiting for transfers between devices, y_swap(): return lax.ppermute(v, 'replica', YSWAP)  324 us
    pallas_call x5, Pallas kernels, early_grads(): pl.pallas_call(kern, in_specs=[SM, SM] + [ANY] * (ns + len(flat) + len(pr...  262 us
    ppermute x23, waiting for transfers between devices, x_swap(): return lax.ppermute(v, 'fsdp', XSWAP)  209 us
    pallas_call x8, Pallas kernels, chunk_grads(): pl.pallas_call(kern, in_specs=[SM, SM] + [ANY] * (ns + 8 + len(deps)), ou...  176 us
    ppermute x8, waiting for transfers between devices, y_diag(): return lax.ppermute(v, ('replica', 'fsdp'), YDIAG)  45.6 us
    ppermute x21, starting transfers between devices, y_swap(): return lax.ppermute(v, 'replica', YSWAP)  36.4 us
    ppermute x23, starting transfers between devices, x_swap(): return lax.ppermute(v, 'fsdp', XSWAP)  25.8 us
  transfers between devices with their start and end apart: 72, of which 25 were waited for; matrix products, arithmetic and copies ran while one was open for 2% of the time, Pallas kernels for 39%

profile of v3, /device:TPU:0, one launch (start us, length us, event | category | flops | bytes accessed | tf_op | source)
XLA Modules:
  0.0 1263.4 jit_solution(7174187977811285491)
XLA Ops:
  1.9 8.3 start.1
  10.2 3.8 plan.1
  14.0 13.8 %pack_rest.1.own_ref.refs_2_.refs_14_ = bf16[2,2432,2048]{2,1,0:T(8,128)(2,1)} custom-call(s32[3]{0:T(128)} %get-tuple-element.886.rest_ref, s32[4]{0:T(128)} %get-tuple-element.887.offs_ref, bf16[3,1024,2048]{2,1,0:T(8,128)(2,1)} %x_ref.3, bf16[3,1024,2048]{2,1,0:T(8,128)(2,1)} %d_ref.3), custom_call_target="tpu_custom_call" | custom-call | flops 15000000512 | bytes 50000000 | tf_op jit(solution)/shard_map/pack_rest/pallas_call | solution.py:301
  38.0 8.7 collective-permute-done.79.refs_6_.refs_17_
  50.1 10.6 collective-permute-done.80.refs_7_.refs_18_
  70.7 3.2 dynamic-slice_bitcast_fusion
  73.9 13.3 %collective-permute-done.81.refs_9_.refs_20_ = bf16[256,2048]{1,0:T(8,128)(2,1)S(1)} collective-permute-done((bf16[256,2048]{1,0:T(8,128)(2,1)}, bf16[256,2048]{1,0:T(8,128)(2,1)S(1)}, u32[]{:S(2)}, u32[]{:S(2)}) %collective-permute-start.81) | collective-permute-done | bytes 1048608 | tf_op jit(solution)/shard_map/ppermute | solution.py:56
  89.3 76.8 %collective-permute-done.73.refs_4_ = bf16[2,768,2048]{2,1,0:T(8,128)(2,1)} collective-permute-done((bf16[2,768,2048]{2,1,0:T(8,128)(2,1)}, bf16[2,768,2048]{2,1,0:T(8,128)(2,1)}, u32[]{:S(2)}, u32[]{:S(2)}) %collective-permute-start.73) | collective-permute-done | bytes 6291488 | tf_op jit(solution)/shard_map/ppermute | solution.py:64
  168.3 46.1 %shard_map.68 = (f32[2,256,2048]{2,1,0:T(8,128)}, f32[2,256,2048]{2,1,0:T(8,128)}) custom-call(s32[64]{0:T(128)S(1)} %get-tuple-element.897.tab_ref, s32[4]{0:T(128)} %get-tuple-element.900.info_ref, bf16[2,768,2048]{2,1,0:T(8,128)(2,1)} %bitcast.56, bf16[2,768,2048]{2,1,0:T(8,128)(2,1)} %collective-permute-done.72.refs_1_, ...), custom_call_target="tpu_custom_call" | custom-call | flops 47244640256 | bytes 120000000 | tf_op jit(solution)/shard_map/pallas_call | solution.py:614
  216.5 25.0 %shard_map.69 = (f32[1,256,2048]{2,1,0:T(8,128)}, f32[1,256,2048]{2,1,0:T(8,128)}) custom-call(s32[64]{0:T(128)S(1)} %get-tuple-element.897.tab_ref, s32[4]{0:T(128)} %get-tuple-element.900.info_ref, bf16[2,768,2048]{2,1,0:T(8,128)(2,1)} %bitcast.57, bf16[2,768,2048]{2,1,0:T(8,128)(2,1)} %collective-permute-done.72.refs_1_, ...), custom_call_target="tpu_custom_call" | custom-call | flops 23622320128 | bytes 60000000 | tf_op jit(solution)/shard_map/pallas_call | solution.py:614
  241.5 9.1 build_send.1
  250.6 34.5 %collective-permute-done.78.refs_20_ = bf16[512,2048]{1,0:T(8,128)(2,1)} collective-permute-done((bf16[512,2048]{1,0:T(8,128)(2,1)}, bf16[512,2048]{1,0:T(8,128)(2,1)}, u32[]{:S(2)}, u32[]{:S(2)}) %collective-permute-start.78) | collective-permute-done | bytes 2097184 | tf_op jit(solution)/shard_map/ppermute | solution.py:56
  285.1 331.2 %conditional.1 = (bf16[2,512,2048]{2,1,0:T(8,128)(2,1)}, bf16[2,512,2048]{2,1,0:T(8,128)(2,1)}, bf16[2,384,2048]{2,1,0:T(8,128)(2,1)}, bf16[2,256,2048]{2,1,0:T(...) conditional(s32[]{:T(128)} %bitcast.1, ...), branch_computations={%region_0.1_spmd, %region_1.2_spmd, %region_2.3_spmd, %region_3.4_... | conditional | flops 95489277952 | bytes 386606944 | solution.py:884
  300.8 6.6 collective-permute-start.54
  307.4 40.2 %collective-permute-done.56.given_ref = bf16[2,256,2048]{2,1,0:T(8,128)(2,1)} collective-permute-done((bf16[2,256,2048]{2,1,0:T(8,128)(2,1)}, bf16[2,256,2048]{2,1,0:T(8,128)(2,1)}, u32[]{:S(2)}, u32[]{:S(2)}) %collective-permute-start.56) | collective-permute-done | bytes 2097184 | tf_op jit(solution)/shard_map/cond/branch_6_fun/ppermute | solution.py:56
  348.3 6.7 collective-permute-start.57
  355.0 61.1 %branch_6_fun.10 = (f32[2,256,2048]{2,1,0:T(8,128)}, f32[2,256,2048]{2,1,0:T(8,128)}) custom-call(s32[64]{0:T(128)S(1)} %get-tuple-element.688.tab_ref, s32[4]{0:T(128)S(1)} %get-tuple-element.689.info_ref, bf16[2,768,2048]{2,1,0:T(8,128)(2,1)} %get-tuple-element.690.refs_0_, bf16[2,768,2048]{2,1,0:T(8,128)(2,1)} %get-tuple-element.691.refs_1_, ...), custom_call_target="tpu_custom_call" | custom-call | flops 47244640256 | bytes 120000000 | tf_op jit(solution)/shard_map/cond/branch_6_fun/pallas_call | solution.py:614
  416.1 50.4 %collective-permute-done.55 = bf16[2,384,2048]{2,1,0:T(8,128)(2,1)} collective-permute-done((bf16[2,384,2048]{2,1,0:T(8,128)(2,1)}, bf16[2,384,2048]{2,1,0:T(8,128)(2,1)}, u32[]{:S(2)}, u32[]{:S(2)}) %collective-permute-start.55) | collective-permute-done | bytes 3145760 | tf_op jit(solution)/shard_map/cond/branch_6_fun/ppermute | solution.py:64
  467.1 43.4 %collective-permute-done.57 = bf16[2,256,2048]{2,1,0:T(8,128)(2,1)} collective-permute-done((bf16[2,256,2048]{2,1,0:T(8,128)(2,1)S(1)}, bf16[2,256,2048]{2,1,0:T(8,128)(2,1)}, u32[]{:S(2)}, u32[]{:S(2)}) %collective-permute-start.57) | collective-permute-done | bytes 2097184 | tf_op jit(solution)/shard_map/cond/branch_6_fun/ppermute | solution.py:64
  510.4 97.0 %branch_6_fun.11 = (f32[5,256,2048]{2,1,0:T(8,128)}, f32[5,256,2048]{2,1,0:T(8,128)}) custom-call(s32[64]{0:T(128)S(1)} %get-tuple-element.688.tab_ref, s32[4]{0:T(128)S(1)} %get-tuple-element.689.info_ref, bf16[2,768,2048]{2,1,0:T(8,128)(2,1)} %get-tuple-element.690.refs_0_, bf16[2,768,2048]{2,1,0:T(8,128)(2,1)} %get-tuple-element.691.refs_1_, ...), custom_call_target="tpu_custom_call" | custom-call | flops 47244640256 | bytes 120000000 | tf_op jit(solution)/shard_map/cond/branch_6_fun/pallas_call | solution.py:614
  616.3 6.7 collective-permute-start.71
  623.0 69.0 %collective-permute-done.71.refs_0_ = bf16[2,384,2048]{2,1,0:T(8,128)(2,1)S(1)} collective-permute-done((bf16[2,384,2048]{2,1,0:T(8,128)(2,1)}, bf16[2,384,2048]{2,1,0:T(8,128)(2,1)S(1)}, u32[]{:S(2)}, u32[]{:S(2)}) %collective-permute-start.71) | collective-permute-done | bytes 3145760 | tf_op jit(solution)/shard_map/ppermute | solution.py:64
  692.0 33.2 %shard_map.71 = (f32[1,256,2048]{2,1,0:T(8,128)}, f32[1,256,2048]{2,1,0:T(8,128)}) custom-call(s32[64]{0:T(128)S(1)} %get-tuple-element.897.tab_ref, s32[4]{0:T(128)S(1)} %get-tuple-element.898.info_ref, bf16[2,768,2048]{2,1,0:T(8,128)(2,1)} %bitcast.66, bf16[2,768,2048]{2,1,0:T(8,128)(2,1)} %collective-permute-done.72.refs_1_, ...), custom_call_target="tpu_custom_call" | custom-call | flops 23622320128 | bytes 60000000 | tf_op jit(solution)/shard_map/pallas_call | solution.py:614
  725.3 22.1 %shard_map.72 = (f32[128,2048]{1,0:T(8,128)}, f32[128,2048]{1,0:T(8,128)}, f32[128,2048]{1,0:T(8,128)}, f32[128,2048]{1,0:T(8,128)}) custom-call(s32[48]{0:T(128)} %get-tuple-element.883.tab_ref, s32[3]{0:T(128)} %get-tuple-element.884.info_ref, bf16[2,384,2048]{2,1,0:T(8,128)(2,1)} %copy-done.26, bf16[2,512,2048]{2,1,0:T(8,128)(2,1)} %get-tuple-element.905.refs_1_, ...), custom_call_target="tpu_custom_call" | custom-call | flops 12884901888 | bytes 40000000 | tf_op jit(solution)/shard_map/pallas_call | solution.py:674
  747.5 22.0 %shard_map.70 = (f32[128,2048]{1,0:T(8,128)}, f32[128,2048]{1,0:T(8,128)}, f32[128,2048]{1,0:T(8,128)}, f32[128,2048]{1,0:T(8,128)}) custom-call(s32[48]{0:T(128)} %get-tuple-element.883.tab_ref, s32[3]{0:T(128)} %get-tuple-element.884.info_ref, bf16[2,384,2048]{2,1,0:T(8,128)(2,1)} %copy-done.26, bf16[2,512,2048]{2,1,0:T(8,128)(2,1)} %get-tuple-element.905.refs_1_, ...), custom_call_target="tpu_custom_call" | custom-call | flops 12884901888 | bytes 40000000 | tf_op jit(solution)/shard_map/pallas_call | solution.py:674
  778.6 22.0 %shard_map.77 = (f32[128,2048]{1,0:T(8,128)}, f32[128,2048]{1,0:T(8,128)}, f32[128,2048]{1,0:T(8,128)}, f32[128,2048]{1,0:T(8,128)}) custom-call(s32[48]{0:T(128)} %get-tuple-element.883.tab_ref, s32[3]{0:T(128)} %get-tuple-element.884.info_ref, bf16[2,384,2048]{2,1,0:T(8,128)(2,1)} %copy-done.26, bf16[2,512,2048]{2,1,0:T(8,128)(2,1)} %get-tuple-element.905.refs_1_, ...), custom_call_target="tpu_custom_call" | custom-call | flops 12884901888 | bytes 40000000 | tf_op jit(solution)/shard_map/pallas_call | solution.py:674
  805.7 22.0 %shard_map.75 = (f32[128,2048]{1,0:T(8,128)}, f32[128,2048]{1,0:T(8,128)}, f32[128,2048]{1,0:T(8,128)}, f32[128,2048]{1,0:T(8,128)}) custom-call(s32[48]{0:T(128)} %get-tuple-element.883.tab_ref, s32[3]{0:T(128)} %get-tuple-element.884.info_ref, bf16[2,384,2048]{2,1,0:T(8,128)(2,1)} %copy-done.26, bf16[2,512,2048]{2,1,0:T(8,128)(2,1)} %get-tuple-element.905.refs_1_, ...), custom_call_target="tpu_custom_call" | custom-call | flops 12884901888 | bytes 40000000 | tf_op jit(solution)/shard_map/pallas_call | solution.py:674
  830.7 10.1 collective-permute-done.96.rc
  843.8 41.4 %collective-permute-done.97.rc = f32[128,2048]{1,0:T(8,128)} collective-permute-done((f32[128,2048]{1,0:T(8,128)}, f32[128,2048]{1,0:T(8,128)}, u32[]{:S(2)}, u32[]{:S(2)}) %collective-permute-start.97) | collective-permute-done | bytes 1048608 | tf_op jit(solution)/shard_map/ppermute | solution.py:56
  892.0 22.0 %shard_map.85 = (f32[128,2048]{1,0:T(8,128)}, f32[128,2048]{1,0:T(8,128)}, f32[128,2048]{1,0:T(8,128)}, f32[128,2048]{1,0:T(8,128)}) custom-call(s32[48]{0:T(128)} %get-tuple-element.883.tab_ref, s32[3]{0:T(128)} %get-tuple-element.884.info_ref, bf16[2,384,2048]{2,1,0:T(8,128)(2,1)} %copy-done.26, bf16[2,512,2048]{2,1,0:T(8,128)(2,1)} %get-tuple-element.905.refs_1_, ...), custom_call_target="tpu_custom_call" | custom-call | flops 12884901888 | bytes 40000000 | tf_op jit(solution)/shard_map/pallas_call | solution.py:674
  917.0 15.7 %collective-permute-done.94.rc = f32[128,2048]{1,0:T(8,128)} collective-permute-done((f32[128,2048]{1,0:T(8,128)}, f32[128,2048]{1,0:T(8,128)}, u32[]{:S(2)}, u32[]{:S(2)}) %collective-permute-start.94) | collective-permute-done | bytes 1048608 | tf_op jit(solution)/shard_map/ppermute | solution.py:56
  943.8 3.2 shard_map.83
  948.5 21.7 %shard_map.84 = (f32[128,2048]{1,0:T(8,128)}, f32[128,2048]{1,0:T(8,128)}, f32[128,2048]{1,0:T(8,128)}, f32[128,2048]{1,0:T(8,128)}) custom-call(s32[48]{0:T(128)} %get-tuple-element.883.tab_ref, s32[3]{0:T(128)} %get-tuple-element.884.info_ref, bf16[2,384,2048]{2,1,0:T(8,128)(2,1)} %copy-done.26, bf16[2,512,2048]{2,1,0:T(8,128)(2,1)} %get-tuple-element.905.refs_1_, ...), custom_call_target="tpu_custom_call" | custom-call | flops 12884901888 | bytes 40000000 | tf_op jit(solution)/shard_map/pallas_call | solution.py:674
  970.8 10.6 collective-permute-done.104.d_ref
  985.6 3.3 shard_map.87
  996.1 6.5 collective-permute-done.101.uy_ref
  1004.9 10.2 collective-permute-done.112.uc_ref
  1015.1 22.3 %shard_map.93 = (f32[128,2048]{1,0:T(8,128)}, f32[128,2048]{1,0:T(8,128)}, f32[128,2048]{1,0:T(8,128)}, f32[128,2048]{1,0:T(8,128)}) custom-call(s32[48]{0:T(128)} %get-tuple-element.883.tab_ref, s32[3]{0:T(128)} %get-tuple-element.884.info_ref, bf16[2,384,2048]{2,1,0:T(8,128)(2,1)} %copy-done.26, bf16[2,512,2048]{2,1,0:T(8,128)(2,1)} %get-tuple-element.905.refs_1_, ...), custom_call_target="tpu_custom_call" | custom-call | flops 12884901888 | bytes 40000000 | tf_op jit(solution)/shard_map/pallas_call | solution.py:674
  1037.4 29.9 %collective-permute-done.113.uy_ref = f32[2,512,128]{2,1,0:T(8,128)S(1)} collective-permute-done((f32[2,512,128]{2,1,0:T(8,128)}, f32[2,512,128]{2,1,0:T(8,128)S(1)}, u32[]{:S(2)}, u32[]{:S(2)}) %collective-permute-start.113) | collective-permute-done | bytes 524320 | tf_op jit(solution)/shard_map/ppermute | solution.py:68
  1085.0 9.2 collective-permute-done.120.uy_ref
  1095.6 22.0 %shard_map.92 = (f32[128,2048]{1,0:T(8,128)}, f32[128,2048]{1,0:T(8,128)}, f32[128,2048]{1,0:T(8,128)}, f32[128,2048]{1,0:T(8,128)}) custom-call(s32[48]{0:T(128)} %get-tuple-element.883.tab_ref, s32[3]{0:T(128)} %get-tuple-element.884.info_ref, bf16[2,384,2048]{2,1,0:T(8,128)(2,1)} %copy-done.26, bf16[2,512,2048]{2,1,0:T(8,128)(2,1)} %get-tuple-element.905.refs_1_, ...), custom_call_target="tpu_custom_call" | custom-call | flops 12884901888 | bytes 40000000 | tf_op jit(solution)/shard_map/pallas_call | solution.py:674
  1130.3 3.2 collective-permute-done.122.rc
  1137.4 18.6 %collective-permute-done.110.rc = f32[128,2048]{1,0:T(8,128)} collective-permute-done((f32[128,2048]{1,0:T(8,128)}, f32[128,2048]{1,0:T(8,128)}, u32[]{:S(2)}, u32[]{:S(2)}) %collective-permute-start.110) | collective-permute-done | bytes 1048608 | tf_op jit(solution)/shard_map/ppermute | solution.py:56
  1156.0 21.0 %collective-permute-done.117.rc = f32[128,2048]{1,0:T(8,128)} collective-permute-done((f32[128,2048]{1,0:T(8,128)}, f32[128,2048]{1,0:T(8,128)}, u32[]{:S(2)}, u32[]{:S(2)}) %collective-permute-start.117) | collective-permute-done | bytes 1048608 | tf_op jit(solution)/shard_map/ppermute | solution.py:56
  1189.3 25.7 %collective-permute-done.127.uc_ref = f32[2,512,128]{2,1,0:T(8,128)} collective-permute-done((f32[2,512,128]{2,1,0:T(8,128)}, f32[2,512,128]{2,1,0:T(8,128)}, u32[]{:S(2)}, u32[]{:S(2)}) %collective-permute-start.127) | collective-permute-done | bytes 524320 | tf_op jit(solution)/shard_map/ppermute | solution.py:64
  1220.3 3.3 shard_map.101
  1223.5 36.3 %collective-permute-done.123.uc_ref = f32[2,512,128]{2,1,0:T(8,128)S(1)} collective-permute-done((f32[2,512,128]{2,1,0:T(8,128)}, f32[2,512,128]{2,1,0:T(8,128)S(1)}, u32[]{:S(2)}, u32[]{:S(2)}) %collective-permute-start.123) | collective-permute-done | bytes 524320 | tf_op jit(solution)/shard_map/ppermute | solution.py:64
  1259.8 3.3 shard_map.102
  (230 shorter events, 141.9 us)
Async XLA Ops:
  27.8 140.5 %collective-permute-start.70 = (bf16[2,2432,2048]{2,1,0:T(8,128)(2,1)}, bf16[2,2432,2048]{2,1,0:T(8,128)(2,1)}, u32[]{:S(2)}, u32[]{:S(2)}) collective-permute-start(bf16[2,2432,2048]{2,1,0:T(8,128)(2,1)} %pack_rest.1.own_ref.refs_2_.refs_14_), channel_id=1, source_target_pairs={{0,1},{1,0},{2,3},{3,2},{4,5},{5,4},{6,7},{7,6}} | collective-permute-start | bytes 59768840 | tf_op jit(solution)/shard_map/ppermute | solution.py:52
  27.8 61.5 %collective-permute-start.72 = (bf16[2,768,2048]{2,1,0:T(8,128)(2,1)}, bf16[2,768,2048]{2,1,0:T(8,128)(2,1)}, u32[]{:S(2)}, u32[]{:S(2)}) collective-permute-start(bf16[2,768,2048]{2,1,0:T(8,128)(2,1)} %bitcast.54), channel_id=1, source_target_pairs={{0,1},{1,0},{2,3},{3,2},{4,5},{5,4},{6,7},{7,6}} | collective-permute-start | bytes 18874376 | tf_op jit(solution)/shard_map/ppermute | solution.py:52
  28.3 137.8 %collective-permute-start.73 = (bf16[2,768,2048]{2,1,0:T(8,128)(2,1)}, bf16[2,768,2048]{2,1,0:T(8,128)(2,1)}, u32[]{:S(2)}, u32[]{:S(2)}) collective-permute-start(bf16[2,768,2048]{2,1,0:T(8,128)(2,1)} %bitcast.55), channel_id=1, source_target_pairs={{0,4},{4,0},{1,5},{5,1},{2,6},{6,2},{3,7},{7,3}} | collective-permute-start | bytes 18874376 | tf_op jit(solution)/shard_map/ppermute | solution.py:64
  38.0 49.6 %collective-permute-start.75 = (bf16[2,512,1024]{2,1,0:T(8,128)(2,1)}, bf16[2,512,1024]{2,1,0:T(8,128)(2,1)S(1)}, u32[]{:S(2)}, u32[]{:S(2)}) collective-permute-start(bf16[2,512,1024]{2,1,0:T(8,128)(2,1)} %pad_maximum_fusion), channel_id=1, source_target_pairs={{0,1},{1,0},{2,3},{3,2},{4,5},{5,4},{6,7},{7,6}} | collective-permute-start | bytes 6291464 | tf_op jit(solution)/shard_map/ppermute | solution.py:52
  87.3 163.3 %collective-permute-start.76 = (bf16[2,512,512]{2,1,0:T(8,128)(2,1)}, bf16[2,512,512]{2,1,0:T(8,128)(2,1)}, u32[]{:S(2)}, u32[]{:S(2)}) collective-permute-start(bf16[2,512,512]{2,1,0:T(8,128)(2,1)} %pad_maximum_fusion.1), channel_id=1, source_target_pairs={{0,2},{2,0},{1,3},{3,1},{4,6},{6,4},{5,7},{7,5}} | collective-permute-start | bytes 3145736 | tf_op jit(solution)/shard_map/ppermute | solution.py:56
  87.6 126.8 %collective-permute-start.82 = (bf16[2,512,256]{2,1,0:T(8,128)(2,1)}, bf16[2,512,256]{2,1,0:T(8,128)(2,1)S(1)}, u32[]{:S(2)}, u32[]{:S(2)}) collective-permute-start(bf16[2,512,256]{2,1,0:T(8,128)(2,1)} %pad_maximum_fusion.5), channel_id=1, source_target_pairs={{0,2},{2,0},{1,3},{3,1},{4,6},{6,4},{5,7},{7,5}} | collective-permute-start | bytes 1572872 | tf_op jit(solution)/shard_map/ppermute | solution.py:56
  89.3 125.1 %collective-permute-start.83 = (bf16[2,512,256]{2,1,0:T(8,128)(2,1)}, bf16[2,512,256]{2,1,0:T(8,128)(2,1)}, u32[]{:S(2)}, u32[]{:S(2)}) collective-permute-start(bf16[2,512,256]{2,1,0:T(8,128)(2,1)} %pad_maximum_fusion.6), channel_id=1, source_target_pairs={{0,3},{3,0},{1,2},{2,1},{4,7},{7,4},{5,6},{6,5}} | collective-permute-start | bytes 1572872 | tf_op jit(solution)/shard_map/ppermute | solution.py:60
  166.1 50.4 %collective-permute-start.84 = (bf16[256,2048]{1,0:T(8,128)(2,1)}, bf16[256,2048]{1,0:T(8,128)(2,1)S(1)}, u32[]{:S(2)}, u32[]{:S(2)}) collective-permute-start(bf16[256,2048]{1,0:T(8,128)(2,1)} %get-tuple-element.1011), channel_id=1, source_target_pairs={{0,2},{2,0},{1,3},{3,1},{4,6},{6,4},{5,7},{7,5}} | collective-permute-start | bytes 3145736 | tf_op jit(solution)/shard_map/ppermute | solution.py:56
  168.3 116.8 %collective-permute-start.74 = (bf16[2,768,2048]{2,1,0:T(8,128)(2,1)}, bf16[2,768,2048]{2,1,0:T(8,128)(2,1)}, u32[]{:S(2)}, u32[]{:S(2)}) collective-permute-start(bf16[2,768,2048]{2,1,0:T(8,128)(2,1)} %collective-permute-done.73.refs_4_), channel_id=1, source_target_pairs={{0,1},{1,0},{2,3},{3,2},{4,5},{5,4},{6,7},{7,6}} | collective-permute-start | bytes 18874376 | tf_op jit(solution)/shard_map/ppermute | solution.py:52
  214.4 70.7 %collective-permute-start.78 = (bf16[512,2048]{1,0:T(8,128)(2,1)}, bf16[512,2048]{1,0:T(8,128)(2,1)}, u32[]{:S(2)}, u32[]{:S(2)}) collective-permute-start(bf16[512,2048]{1,0:T(8,128)(2,1)} %dynamic-slice_bitcast_fusion), channel_id=1, source_target_pairs={{0,2},{2,0},{1,3},{3,1},{4,6},{6,4},{5,7},{7,5}} | collective-permute-start | bytes 6291464 | tf_op jit(solution)/shard_map/ppermute | solution.py:56
  300.4 47.3 %collective-permute-start.56 = (bf16[2,256,2048]{2,1,0:T(8,128)(2,1)}, bf16[2,256,2048]{2,1,0:T(8,128)(2,1)}, u32[]{:S(2)}, u32[]{:S(2)}) collective-permute-start(bf16[2,256,2048]{2,1,0:T(8,128)(2,1)} %get-tuple-element.687), channel_id=1, source_target_pairs={{0,2},{2,0},{1,3},{3,1},{4,6},{6,4},{5,7},{7,5}} | collective-permute-start | bytes 6291464 | tf_op jit(solution)/shard_map/cond/branch_6_fun/ppermute | solution.py:56
  300.8 165.8 %collective-permute-start.54 = (bf16[2,512,2048]{2,1,0:T(8,128)(2,1)}, bf16[2,512,2048]{2,1,0:T(8,128)(2,1)}, u32[]{:S(2)}, u32[]{:S(2)}) collective-permute-start(bf16[2,512,2048]{2,1,0:T(8,128)(2,1)} %get-tuple-element.683), channel_id=1, source_target_pairs={{0,4},{4,0},{1,5},{5,1},{2,6},{6,2},{3,7},{7,3}} | collective-permute-start | bytes 12582920 | tf_op jit(solution)/shard_map/cond/branch_6_fun/ppermute | solution.py:64
  307.4 159.1 %collective-permute-start.55 = (bf16[2,384,2048]{2,1,0:T(8,128)(2,1)}, bf16[2,384,2048]{2,1,0:T(8,128)(2,1)}, u32[]{:S(2)}, u32[]{:S(2)}) collective-permute-start(bf16[2,384,2048]{2,1,0:T(8,128)(2,1)} %get-tuple-element.684), channel_id=1, source_target_pairs={{0,4},{4,0},{1,5},{5,1},{2,6},{6,2},{3,7},{7,3}} | collective-permute-start | bytes 9437192 | tf_op jit(solution)/shard_map/cond/branch_6_fun/ppermute | solution.py:64
  348.3 162.2 %collective-permute-start.57 = (bf16[2,256,2048]{2,1,0:T(8,128)(2,1)S(1)}, bf16[2,256,2048]{2,1,0:T(8,128)(2,1)}, u32[]{:S(2)}, u32[]{:S(2)}) collective-permute-start(bf16[2,256,2048]{2,1,0:T(8,128)(2,1)S(1)} %append.14), channel_id=1, source_target_pairs={{0,4},{4,0},{1,5},{5,1},{2,6},{6,2},{3,7},{7,3}} | collective-permute-start | bytes 6291464 | tf_op jit(solution)/shard_map/cond/branch_6_fun/ppermute | solution.py:64
  416.1 191.4 %collective-permute-start.61 = (bf16[2,256,2048]{2,1,0:T(8,128)(2,1)}, bf16[2,256,2048]{2,1,0:T(8,128)(2,1)}, u32[]{:S(2)}, u32[]{:S(2)}) collective-permute-start(bf16[2,256,2048]{2,1,0:T(8,128)(2,1)} %collective-permute-done.56.given_ref), channel_id=1, source_target_pairs={{0,1},{1,0},{2,3},{3,2},{4,5},{5,4},{6,7},{7,6}} | collective-permute-start | bytes 6291464 | tf_op jit(solution)/shard_map/cond/branch_6_fun/ppermute | solution.py:52
  466.6 140.9 %collective-permute-start.59 = (bf16[2,384,2048]{2,1,0:T(8,128)(2,1)}, bf16[2,384,2048]{2,1,0:T(8,128)(2,1)}, u32[]{:S(2)}, u32[]{:S(2)}) collective-permute-start(bf16[2,384,2048]{2,1,0:T(8,128)(2,1)} %collective-permute-done.55), channel_id=1, source_target_pairs={{0,1},{1,0},{2,3},{3,2},{4,5},{5,4},{6,7},{7,6}} | collective-permute-start | bytes 9437192 | tf_op jit(solution)/shard_map/cond/branch_6_fun/ppermute | solution.py:52
  466.6 140.9 %collective-permute-start.58 = (bf16[2,512,2048]{2,1,0:T(8,128)(2,1)}, bf16[2,512,2048]{2,1,0:T(8,128)(2,1)}, u32[]{:S(2)}, u32[]{:S(2)}) collective-permute-start(bf16[2,512,2048]{2,1,0:T(8,128)(2,1)} %collective-permute-done.54), channel_id=1, source_target_pairs={{0,1},{1,0},{2,3},{3,2},{4,5},{5,4},{6,7},{7,6}} | collective-permute-start | bytes 12582920 | tf_op jit(solution)/shard_map/cond/branch_6_fun/ppermute | solution.py:52
  510.4 97.0 %collective-permute-start.60 = (bf16[2,256,2048]{2,1,0:T(8,128)(2,1)}, bf16[2,256,2048]{2,1,0:T(8,128)(2,1)}, u32[]{:S(2)}, u32[]{:S(2)}) collective-permute-start(bf16[2,256,2048]{2,1,0:T(8,128)(2,1)} %collective-permute-done.57), channel_id=1, source_target_pairs={{0,1},{1,0},{2,3},{3,2},{4,5},{5,4},{6,7},{7,6}} | collective-permute-start | bytes 6291464 | tf_op jit(solution)/shard_map/cond/branch_6_fun/ppermute | solution.py:52
  616.3 75.7 %collective-permute-start.71 = (bf16[2,384,2048]{2,1,0:T(8,128)(2,1)}, bf16[2,384,2048]{2,1,0:T(8,128)(2,1)S(1)}, u32[]{:S(2)}, u32[]{:S(2)}) collective-permute-start(bf16[2,384,2048]{2,1,0:T(8,128)(2,1)} %get-tuple-element.888), channel_id=1, source_target_pairs={{0,4},{4,0},{1,5},{5,1},{2,6},{6,2},{3,7},{7,3}} | collective-permute-start | bytes 9437192 | tf_op jit(solution)/shard_map/ppermute | solution.py:64
  771.5 56.2 %collective-permute-start.89 = (f32[128,2048]{1,0:T(8,128)}, f32[128,2048]{1,0:T(8,128)}, u32[]{:S(2)}, u32[]{:S(2)}) collective-permute-start(f32[128,2048]{1,0:T(8,128)} %get-tuple-element.932), channel_id=1, source_target_pairs={{0,2},{2,0},{1,3},{3,1},{4,6},{6,4},{5,7},{7,5}} | collective-permute-start | bytes 3145736 | tf_op jit(solution)/shard_map/ppermute | solution.py:56
  771.5 69.3 %collective-permute-start.96 = (f32[128,2048]{1,0:T(8,128)}, f32[128,2048]{1,0:T(8,128)}, u32[]{:S(2)}, u32[]{:S(2)}) collective-permute-start(f32[128,2048]{1,0:T(8,128)} %get-tuple-element.941), channel_id=1, source_target_pairs={{0,2},{2,0},{1,3},{3,1},{4,6},{6,4},{5,7},{7,5}} | collective-permute-start | bytes 3145736 | tf_op jit(solution)/shard_map/ppermute | solution.py:56
  776.6 113.0 %collective-permute-start.91 = (f32[2,512,128]{2,1,0:T(8,128)}, f32[2,512,128]{2,1,0:T(8,128)S(1)}, u32[]{:S(2)}, u32[]{:S(2)}) collective-permute-start(f32[2,512,128]{2,1,0:T(8,128)} %get-tuple-element.934.refs_23_), channel_id=1, source_target_pairs={{0,4},{4,0},{1,5},{5,1},{2,6},{6,2},{3,7},{7,3}} | collective-permute-start | bytes 1572872 | tf_op jit(solution)/shard_map/ppermute | solution.py:64
  800.6 89.7 %collective-permute-start.95 = (f32[128,2048]{1,0:T(8,128)}, f32[128,2048]{1,0:T(8,128)}, u32[]{:S(2)}, u32[]{:S(2)}) collective-permute-start(f32[128,2048]{1,0:T(8,128)} %get-tuple-element.939), channel_id=1, source_target_pairs={{0,2},{2,0},{1,3},{3,1},{4,6},{6,4},{5,7},{7,5}} | collective-permute-start | bytes 3145736 | tf_op jit(solution)/shard_map/ppermute | solution.py:56
  800.6 84.6 %collective-permute-start.97 = (f32[128,2048]{1,0:T(8,128)}, f32[128,2048]{1,0:T(8,128)}, u32[]{:S(2)}, u32[]{:S(2)}) collective-permute-start(f32[128,2048]{1,0:T(8,128)} %get-tuple-element.947), channel_id=1, source_target_pairs={{0,2},{2,0},{1,3},{3,1},{4,6},{6,4},{5,7},{7,5}} | collective-permute-start | bytes 3145736 | tf_op jit(solution)/shard_map/ppermute | solution.py:56
  827.6 109.2 %collective-permute-start.92 = (f32[2,512,128]{2,1,0:T(8,128)}, f32[2,512,128]{2,1,0:T(8,128)S(1)}, u32[]{:S(2)}, u32[]{:S(2)}) collective-permute-start(f32[2,512,128]{2,1,0:T(8,128)} %get-tuple-element.935), channel_id=1, source_target_pairs={{0,5},{1,4},{2,7},{3,6},{4,1},{5,0},{6,3},{7,2}} | collective-permute-start | bytes 1572872 | tf_op jit(solution)/shard_map/ppermute | solution.py:68
  840.8 96.1 %collective-permute-start.93 = (f32[2,512,128]{2,1,0:T(8,128)}, f32[2,512,128]{2,1,0:T(8,128)S(1)}, u32[]{:S(2)}, u32[]{:S(2)}) collective-permute-start(f32[2,512,128]{2,1,0:T(8,128)} %get-tuple-element.935), channel_id=1, source_target_pairs={{0,1},{1,0},{2,3},{3,2},{4,5},{5,4},{6,7},{7,6}} | collective-permute-start | bytes 1572872 | tf_op jit(solution)/shard_map/ppermute | solution.py:52
  885.2 58.0 %collective-permute-start.88 = (f32[128,2048]{1,0:T(8,128)}, f32[128,2048]{1,0:T(8,128)}, u32[]{:S(2)}, u32[]{:S(2)}) collective-permute-start(f32[128,2048]{1,0:T(8,128)} %get-tuple-element.930), channel_id=1, source_target_pairs={{0,2},{2,0},{1,3},{3,1},{4,6},{6,4},{5,7},{7,5}} | collective-permute-start | bytes 3145736 | tf_op jit(solution)/shard_map/ppermute | solution.py:56
  889.5 49.1 %collective-permute-start.90 = (f32[128,2048]{1,0:T(8,128)}, f32[128,2048]{1,0:T(8,128)S(1)}, u32[]{:S(2)}, u32[]{:S(2)}) collective-permute-start(f32[128,2048]{1,0:T(8,128)} %get-tuple-element.933), channel_id=1, source_target_pairs={{0,4},{4,0},{1,5},{5,1},{2,6},{6,2},{3,7},{7,3}} | collective-permute-start | bytes 3145736 | tf_op jit(solution)/shard_map/ppermute | solution.py:64
  890.2 42.5 %collective-permute-start.94 = (f32[128,2048]{1,0:T(8,128)}, f32[128,2048]{1,0:T(8,128)}, u32[]{:S(2)}, u32[]{:S(2)}) collective-permute-start(f32[128,2048]{1,0:T(8,128)} %get-tuple-element.937), channel_id=1, source_target_pairs={{0,2},{2,0},{1,3},{3,1},{4,6},{6,4},{5,7},{7,5}} | collective-permute-start | bytes 3145736 | tf_op jit(solution)/shard_map/ppermute | solution.py:56
  938.7 42.7 %collective-permute-start.104 = (f32[128,2048]{1,0:T(8,128)}, f32[128,2048]{1,0:T(8,128)S(1)}, u32[]{:S(2)}, u32[]{:S(2)}) collective-permute-start(f32[128,2048]{1,0:T(8,128)} %get-tuple-element.959), channel_id=1, source_target_pairs={{0,4},{4,0},{1,5},{5,1},{2,6},{6,2},{3,7},{7,3}} | collective-permute-start | bytes 3145736 | tf_op jit(solution)/shard_map/ppermute | solution.py:64
  947.7 43.1 %collective-permute-start.109 = (f32[128,2048]{1,0:T(8,128)}, f32[128,2048]{1,0:T(8,128)}, u32[]{:S(2)}, u32[]{:S(2)}) collective-permute-start(f32[128,2048]{1,0:T(8,128)} %get-tuple-element.969), channel_id=1, source_target_pairs={{0,2},{2,0},{1,3},{3,1},{4,6},{6,4},{5,7},{7,5}} | collective-permute-start | bytes 3145736 | tf_op jit(solution)/shard_map/ppermute | solution.py:56
  990.8 78.9 %collective-permute-start.98 = (f32[128,2048]{1,0:T(8,128)}, f32[128,2048]{1,0:T(8,128)}, u32[]{:S(2)}, u32[]{:S(2)}) collective-permute-start(f32[128,2048]{1,0:T(8,128)} %get-tuple-element.953), channel_id=1, source_target_pairs={{0,2},{2,0},{1,3},{3,1},{4,6},{6,4},{5,7},{7,5}} | collective-permute-start | bytes 3145736 | tf_op jit(solution)/shard_map/ppermute | solution.py:56
  995.2 75.1 %collective-permute-start.99 = (f32[128,2048]{1,0:T(8,128)}, f32[128,2048]{1,0:T(8,128)S(1)}, u32[]{:S(2)}, u32[]{:S(2)}) collective-permute-start(f32[128,2048]{1,0:T(8,128)} %get-tuple-element.954), channel_id=1, source_target_pairs={{0,4},{4,0},{1,5},{5,1},{2,6},{6,2},{3,7},{7,3}} | collective-permute-start | bytes 3145736 | tf_op jit(solution)/shard_map/ppermute | solution.py:64
  1003.4 67.6 %collective-permute-start.103 = (f32[128,2048]{1,0:T(8,128)}, f32[128,2048]{1,0:T(8,128)}, u32[]{:S(2)}, u32[]{:S(2)}) collective-permute-start(f32[128,2048]{1,0:T(8,128)} %get-tuple-element.958), channel_id=1, source_target_pairs={{0,2},{2,0},{1,3},{3,1},{4,6},{6,4},{5,7},{7,5}} | collective-permute-start | bytes 3145736 | tf_op jit(solution)/shard_map/ppermute | solution.py:56
  1004.0 79.7 %collective-permute-start.111 = (f32[128,2048]{1,0:T(8,128)}, f32[128,2048]{1,0:T(8,128)S(1)}, u32[]{:S(2)}, u32[]{:S(2)}) collective-permute-start(f32[128,2048]{1,0:T(8,128)} %get-tuple-element.976), channel_id=1, source_target_pairs={{0,4},{4,0},{1,5},{5,1},{2,6},{6,2},{3,7},{7,3}} | collective-permute-start | bytes 3145736 | tf_op jit(solution)/shard_map/ppermute | solution.py:64
  1015.1 52.2 %collective-permute-start.113 = (f32[2,512,128]{2,1,0:T(8,128)}, f32[2,512,128]{2,1,0:T(8,128)S(1)}, u32[]{:S(2)}, u32[]{:S(2)}) collective-permute-start(f32[2,512,128]{2,1,0:T(8,128)} %get-tuple-element.977), channel_id=1, source_target_pairs={{0,5},{1,4},{2,7},{3,6},{4,1},{5,0},{6,3},{7,2}} | collective-permute-start | bytes 1572872 | tf_op jit(solution)/shard_map/ppermute | solution.py:68
  1094.2 39.3 %collective-permute-start.122 = (f32[128,2048]{1,0:T(8,128)}, f32[128,2048]{1,0:T(8,128)}, u32[]{:S(2)}, u32[]{:S(2)}) collective-permute-start(f32[128,2048]{1,0:T(8,128)} %get-tuple-element.992), channel_id=1, source_target_pairs={{0,2},{2,0},{1,3},{3,1},{4,6},{6,4},{5,7},{7,5}} | collective-permute-start | bytes 3145736 | tf_op jit(solution)/shard_map/ppermute | solution.py:56
  1117.7 38.4 %collective-permute-start.110 = (f32[128,2048]{1,0:T(8,128)}, f32[128,2048]{1,0:T(8,128)}, u32[]{:S(2)}, u32[]{:S(2)}) collective-permute-start(f32[128,2048]{1,0:T(8,128)} %get-tuple-element.975), channel_id=1, source_target_pairs={{0,2},{2,0},{1,3},{3,1},{4,6},{6,4},{5,7},{7,5}} | collective-permute-start | bytes 3145736 | tf_op jit(solution)/shard_map/ppermute | solution.py:56
  1120.5 56.5 %collective-permute-start.117 = (f32[128,2048]{1,0:T(8,128)}, f32[128,2048]{1,0:T(8,128)}, u32[]{:S(2)}, u32[]{:S(2)}) collective-permute-start(f32[128,2048]{1,0:T(8,128)} %get-tuple-element.987), channel_id=1, source_target_pairs={{0,2},{2,0},{1,3},{3,1},{4,6},{6,4},{5,7},{7,5}} | collective-permute-start | bytes 3145736 | tf_op jit(solution)/shard_map/ppermute | solution.py:56
  1121.3 55.7 %collective-permute-start.118 = (f32[128,2048]{1,0:T(8,128)}, f32[128,2048]{1,0:T(8,128)S(1)}, u32[]{:S(2)}, u32[]{:S(2)}) collective-permute-start(f32[128,2048]{1,0:T(8,128)} %get-tuple-element.988), channel_id=1, source_target_pairs={{0,4},{4,0},{1,5},{5,1},{2,6},{6,2},{3,7},{7,3}} | collective-permute-start | bytes 3145736 | tf_op jit(solution)/shard_map/ppermute | solution.py:64
  1121.8 59.6 %collective-permute-start.130 = (f32[128,2048]{1,0:T(8,128)}, f32[128,2048]{1,0:T(8,128)S(1)}, u32[]{:S(2)}, u32[]{:S(2)}) collective-permute-start(f32[128,2048]{1,0:T(8,128)} %get-tuple-element.1001), channel_id=1, source_target_pairs={{0,4},{4,0},{1,5},{5,1},{2,6},{6,2},{3,7},{7,3}} | collective-permute-start | bytes 3145736 | tf_op jit(solution)/shard_map/ppermute | solution.py:64
  1133.5 86.7 %collective-permute-start.126 = (f32[128,2048]{1,0:T(8,128)}, f32[128,2048]{1,0:T(8,128)S(1)}, u32[]{:S(2)}, u32[]{:S(2)}) collective-permute-start(f32[128,2048]{1,0:T(8,128)} %get-tuple-element.998), channel_id=1, source_target_pairs={{0,4},{4,0},{1,5},{5,1},{2,6},{6,2},{3,7},{7,3}} | collective-permute-start | bytes 3145736 | tf_op jit(solution)/shard_map/ppermute | solution.py:64
  1156.0 59.0 %collective-permute-start.128 = (f32[2,512,128]{2,1,0:T(8,128)}, f32[2,512,128]{2,1,0:T(8,128)}, u32[]{:S(2)}, u32[]{:S(2)}) collective-permute-start(f32[2,512,128]{2,1,0:T(8,128)} %get-tuple-element.1000), channel_id=1, source_target_pairs={{0,5},{1,4},{2,7},{3,6},{4,1},{5,0},{6,3},{7,2}} | collective-permute-start | bytes 1572872 | tf_op jit(solution)/shard_map/ppermute | solution.py:68
  1177.0 38.7 %collective-permute-start.129 = (f32[2,512,128]{2,1,0:T(8,128)}, f32[2,512,128]{2,1,0:T(8,128)}, u32[]{:S(2)}, u32[]{:S(2)}) collective-permute-start(f32[2,512,128]{2,1,0:T(8,128)} %get-tuple-element.1000), channel_id=1, source_target_pairs={{0,1},{1,0},{2,3},{3,2},{4,5},{5,4},{6,7},{7,6}} | collective-permute-start | bytes 1572872 | tf_op jit(solution)/shard_map/ppermute | solution.py:52
  1181.5 78.4 %collective-permute-start.116 = (f32[128,2048]{1,0:T(8,128)}, f32[128,2048]{1,0:T(8,128)}, u32[]{:S(2)}, u32[]{:S(2)}) collective-permute-start(f32[128,2048]{1,0:T(8,128)} %get-tuple-element.985), channel_id=1, source_target_pairs={{0,4},{4,0},{1,5},{5,1},{2,6},{6,2},{3,7},{7,3}} | collective-permute-start | bytes 3145736 | tf_op jit(solution)/shard_map/ppermute | solution.py:64
  1215.0 44.8 %collective-permute-start.124 = (f32[2,512,128]{2,1,0:T(8,128)}, f32[2,512,128]{2,1,0:T(8,128)S(1)}, u32[]{:S(2)}, u32[]{:S(2)}) collective-permute-start(f32[2,512,128]{2,1,0:T(8,128)} %get-tuple-element.997), channel_id=1, source_target_pairs={{0,5},{1,4},{2,7},{3,6},{4,1},{5,0},{6,3},{7,2}} | collective-permute-start | bytes 1572872 | tf_op jit(solution)/shard_map/ppermute | solution.py:68
  1215.0 44.8 %collective-permute-start.125 = (f32[2,512,128]{2,1,0:T(8,128)}, f32[2,512,128]{2,1,0:T(8,128)S(1)}, u32[]{:S(2)}, u32[]{:S(2)}) collective-permute-start(f32[2,512,128]{2,1,0:T(8,128)} %get-tuple-element.997), channel_id=1, source_target_pairs={{0,1},{1,0},{2,3},{3,2},{4,5},{5,4},{6,7},{7,6}} | collective-permute-start | bytes 1572872 | tf_op jit(solution)/shard_map/ppermute | solution.py:52
  1215.7 44.1 %collective-permute-start.123 = (f32[2,512,128]{2,1,0:T(8,128)}, f32[2,512,128]{2,1,0:T(8,128)S(1)}, u32[]{:S(2)}, u32[]{:S(2)}) collective-permute-start(f32[2,512,128]{2,1,0:T(8,128)} %get-tuple-element.996), channel_id=1, source_target_pairs={{0,4},{4,0},{1,5},{5,1},{2,6},{6,2},{3,7},{7,3}} | collective-permute-start | bytes 1572872 | tf_op jit(solution)/shard_map/ppermute | solution.py:64
  (61 other events, 1435.3 us)
